TPU v7x, 128 devices: a whole 4x4x4 slice. The times are simulated.
128 devices in a mesh: gx: 4 (over y), gy: 16 (over x_lo, z, core), gz: 2 (over x_hi).
Axes of the slice: x: 4 (x_hi: 2, x_lo: 2; x = x_hi * 2 + x_lo), y: 4, z: 4, core: 2. Of those that a mesh axis runs over, the one named last changes fastest.
Arguments:
- heat_source: float32 [64, 512, 2048], P('gz', 'gx', 'gy'), may hold values from -18 to 18
- conductance: float32 [64, 512, 2048], P('gz', 'gx', 'gy'), may hold values from 0.5 to 4
- projection: float32 [2, 4, 16, 3, 128, 128], P('gz', 'gx', 'gy'), may hold values from -1 to 2, as said below
- segment_map: int32 [2, 4, 16, 3, 128], P('gz', 'gx', 'gy'), may hold values from 0 to 127, each once within a row
Outputs:
- thermal_state: float32 [64, 512, 2048], P('gz', 'gx', 'gy')
- multiplier_x: float32 [2, 4, 16, 32, 128], P('gz', 'gx', 'gy')
- multiplier_y: float32 [2, 4, 16, 32, 128], P('gz', 'gx', 'gy')
- multiplier_z: float32 [2, 4, 16, 128, 128], P('gz', 'gx', 'gy')
Inputs may be any that keep to these rules, and one draw needn't show every extreme that they name: projection entries are finite.
All inputs are finite; a program needn't handle non-finite values.
Results may differ from a plain program's by a relative error of at most 0.0001.
Values sent between devices are 32-bit elements; how exact they have to be, the bound alone decides.
No kernel may reach another device: no remote copies, remote signals or barrier semaphores. Data moves between devices by JAX's collectives and lax.ppermute only.
A program may use at most 128 MiB of HBM per device.

v0:
```python
import functools

import jax
import jax.numpy as jnp
from jax import lax
from jax.experimental import pallas as pl
from jax.experimental.pallas import tpu as pltpu
from jax.sharding import PartitionSpec as P

HIGH = lax.Precision.HIGHEST
DAMPING_WEIGHT = 0.8
EPSILON = 1e-06
AXES = ("gx", "gy", "gz")
CZ = 32
C = 128
F32 = jnp.float32
UNROLL = 4

VM = pl.BlockSpec(memory_space=pltpu.MemorySpace.VMEM)


def dot(a, b):
    return jnp.dot(a, b, precision=HIGH, preferred_element_type=F32)


def dot_t(a, b):
    return lax.dot_general(a, b, (((1,), (1,)), ((), ())), precision=HIGH, preferred_element_type=F32)


def lane_of(shape):
    return lax.broadcasted_iota(jnp.int32, shape, len(shape) - 1)


def row_of(shape):
    return lax.broadcasted_iota(jnp.int32, shape, len(shape) - 2)


def zero_ends(ref):
    ref[0] = jnp.zeros((C, C), F32)
    ref[CZ + 1] = jnp.zeros((C, C), F32)


def neighbours(src, z):
    centre = src[z + 1]
    rows = row_of((C, C))
    lanes = lane_of((C, C))
    near = src[z] + src[z + 2]
    near = near + jnp.where(rows == 0, 0.0, pltpu.roll(centre, 1, 0))
    near = near + jnp.where(rows == C - 1, 0.0, pltpu.roll(centre, C - 1, 0))
    near = near + jnp.where(lanes == 0, 0.0, pltpu.roll(centre, 1, 1))
    near = near + jnp.where(lanes == C - 1, 0.0, pltpu.roll(centre, C - 1, 1))
    return centre, near


def sweep(src, dst, weight, supply):
    def plane(z, carry):
        centre, near = neighbours(src, z)
        dst[z + 1] = (1.0 - DAMPING_WEIGHT) * centre + weight[z] * (supply[z] + near)
        return carry

    lax.fori_loop(0, CZ, plane, 0, unroll=UNROLL)


def row_faces(src, low, high):
    for z in range(CZ):
        low[z : z + 1, :] = src[z + 1, 0:1, :]
        high[z : z + 1, :] = src[z + 1, C - 1 : C, :]


def column_faces(src, turn, low, high):
    half = lane_of((C, C)) // 2

    def plane(z, packed):
        return jnp.where(half == z, pltpu.roll(src[z + 1], 2 * z + 1, 1), packed)

    packed = lax.fori_loop(0, CZ, plane, jnp.zeros((C, C), F32), unroll=UNROLL)
    turn[...] = packed.T
    high[...] = turn[pl.ds(0, CZ, stride=2), :]
    low[...] = turn[pl.ds(1, CZ, stride=2), :]


def pack_columns(turn, low, high):
    turn[...] = jnp.zeros((C, C), F32)
    turn[pl.ds(0, CZ, stride=2), :] = high
    turn[pl.ds(1, CZ, stride=2), :] = low
    return turn[...].T


def column_plane(packed, z):
    lanes = lane_of((C, C))
    edge = (lanes == 0) | (lanes == C - 1)
    return jnp.where(edge, pltpu.roll(packed, C - 1 - 2 * z, 1), 0.0)


def lift_dense(dst, cols, faces, base, sign):
    def plane(z, carry):
        col = column_plane(cols[...], z)
        if base is None:
            dst[z] = sign * col
        else:
            dst[z] = base[z] + sign * col
        return carry

    lax.fori_loop(0, CZ, plane, 0, unroll=UNROLL)
    for z in range(CZ):
        dst[z, 0:1, :] = dst[z, 0:1, :] + sign * faces[0][z : z + 1, :]
        dst[z, C - 1 : C, :] = dst[z, C - 1 : C, :] + sign * faces[1][z : z + 1, :]
    dst[0] = dst[0] + sign * faces[4][...]
    dst[CZ - 1] = dst[CZ - 1] + sign * faces[5][...]


def places():
    x, y, z = (lax.axis_index(a) for a in AXES)
    more = [i < lax.axis_size(a) - 1 for a, i in zip(AXES, (x, y, z))]
    return x % 2 == 0, y % 2 == 0, z == 0, more


def pick(flag, a, b):
    return lax.select(jnp.broadcast_to(flag, a.shape), a, b)


def pack_sends(sends, own, index, extra):
    xeven, yeven, zlow, _ = places()
    xa, xb, ya, yb, zz = sends
    for even, a, b, low, high, n in (
        (xeven, xa, xb, own[0], own[1], CZ),
        (yeven, ya, yb, own[2], own[3], CZ),
    ):
        lo = low[...]
        hi = high[...]
        a[index * n : (index + 1) * n, :] = pick(even, hi, lo)
        b[index * n : (index + 1) * n, :] = pick(even, lo, hi)
    zz[index * C : (index + 1) * C, :] = pick(zlow, own[5][...], own[4][...])
    if extra is not None:
        for a in (xa, xb):
            a[CZ : CZ + C, :] = extra[0]
        for a in (ya, yb):
            a[CZ : CZ + C, :] = extra[1]
        zz[C : 2 * C, :] = extra[2]


def own_faces(src, own, turn):
    row_faces(src, own[0], own[1])
    column_faces(src, turn, own[2], own[3])
    own[4][...] = src[1]
    own[5][...] = src[CZ]


def first_kernel(heat, cond, proj, segs, weight, state, bases, x0, x1, y0, y1, z0, z1, xa, xb, ya, yb, zz, start, turn):
    own = (x0, x1, y0, y1, z0, z1)
    for d in range(3):
        onehot = jnp.where(row_of((C, C)) == segs[d : d + 1, :], 1.0, 0.0).astype(F32)
        bases[d] = dot_t(onehot, proj[d])
    zero_ends(start)
    zero_ends(state)

    def plane(z, carry):
        w = DAMPING_WEIGHT / (6.0 + cond[z])
        weight[z] = w
        start[z + 1] = w * heat[z]
        return carry

    lax.fori_loop(0, CZ, plane, 0, unroll=UNROLL)
    sweep(start, state, weight, heat)
    own_faces(state, own, turn)
    pack_sends((xa, xb, ya, yb, zz), own, 0, bases)


def free_kernel(state, weight, supply, out, mid):
    zero_ends(mid)
    zero_ends(out)
    sweep(state, mid, weight, supply)
    sweep(mid, out, weight, supply)


def jumps(own, got, bases, prev_bases, index, lifted):
    xeven, yeven, zlow, more = places()
    xa, xb, ya, yb, zz = got
    for d, (even, a, b, n) in enumerate(((xeven, xa, xb, CZ), (yeven, ya, yb, CZ), (zlow, zz, zz, C))):
        s = slice(index * n, (index + 1) * n)
        after = pick(even, a[s, :], b[s, :])
        before = pick(even, b[s, :], a[s, :])
        up = own[2 * d + 1][...] - dot(after, bases[d])
        lifted[2 * d + 1][...] = jnp.where(more[d], up, 0.0)
        down = before - dot(own[2 * d][...], prev_bases[d])
        back = -dot_t(down, prev_bases[d])
        if d == 2:
            back = jnp.where(zlow, 0.0, back)
        lifted[2 * d][...] = back


def square_sums(a, b):
    return sum(jnp.sum(a[i][...] * b[i][...]) for i in (1, 3, 5))


def row_of_sums(values):
    lanes = lane_of((1, C))
    row = jnp.zeros((1, C), F32)
    for i, v in enumerate(values):
        row = jnp.where(lanes == i, v, row)
    return row


def energy_sums(pairs, weight):
    def plane(z, carry):
        w = weight[z]
        out = []
        for (a, b), acc in zip(pairs, carry):
            t = a[z] * b[z] * w
            out.append(acc + jnp.sum(t.reshape(C // 8, 8, C), axis=0))
        return tuple(out)

    zero = jnp.zeros((8, C), F32)
    accs = lax.fori_loop(0, CZ, plane, (zero,) * len(pairs), unroll=UNROLL)
    return [jnp.sum(a) / DAMPING_WEIGHT for a in accs]


def second_kernel(first, *refs):
    it = iter(refs)
    take = lambda n: [next(it) for _ in range(n)]
    own = take(6)
    got = take(5)
    (bases,) = take(1)
    (prev,) = take(1) if not first else (None,)
    weight, free = take(2)
    lifted = take(6)
    (sums, resp) = take(2)
    own_u = take(6)
    own_v = take(6)
    sends = take(5)
    if first:
        (prev,) = take(1)
    lift, mid, turn, cols = take(4)
    xeven, yeven, zlow, _ = places()
    if first:
        xa, xb, ya, yb, zz = got
        prev[0] = pick(xeven, xb[CZ:, :], xa[CZ:, :])
        prev[1] = pick(yeven, yb[CZ:, :], ya[CZ:, :])
        prev[2] = zz[C:, :]
    jumps(own, got, bases, prev, 0, lifted)
    cols[...] = pack_columns(turn, lifted[2][...], lifted[3][...])
    lift_dense(lift, cols, lifted, None, 1.0)
    zero_ends(mid)
    zero_ends(resp)

    def plane(z, carry):
        mid[z + 1] = weight[z] * lift[z]
        return carry

    lax.fori_loop(0, CZ, plane, 0, unroll=UNROLL)
    sweep(mid, resp, weight, lift)
    own_faces(free, own_u, turn)
    own_faces(resp, own_v, turn)
    pack_sends(sends, own_u, 0, None)
    pack_sends(sends, own_v, 1, None)
    gg = square_sums(lifted, lifted)
    (gh,) = energy_sums([(lift, lift)], weight)
    sums[...] = row_of_sums([gg, gh])


def third_kernel(*refs):
    it = iter(refs)
    take = lambda n: [next(it) for _ in range(n)]
    own_u = take(6)
    own_v = take(6)
    got = take(5)
    bases, prev, weight, before = take(4)
    lift_u = take(6)
    lift_v = take(6)
    (rows,) = take(1)
    dense_u, dense_v, turn, cols = take(4)
    jumps(own_u, got, bases, prev, 0, lift_u)
    jumps(own_v, got, bases, prev, 1, lift_v)
    cols[...] = pack_columns(turn, lift_u[2][...], lift_u[3][...])
    lift_dense(dense_u, cols, lift_u, None, 1.0)
    cols[...] = pack_columns(turn, lift_v[2][...], lift_v[3][...])
    lift_dense(dense_v, cols, lift_v, None, 1.0)
    sums = [square_sums(lift_u, lift_u), square_sums(lift_u, lift_v), square_sums(lift_v, lift_v)]
    sums += energy_sums([(dense_u, dense_u), (dense_u, dense_v), (dense_v, dense_v)], weight)
    lanes = lane_of((1, C))
    row = row_of_sums([0.0, 0.0] + sums)
    row = jnp.where(lanes < 2, before[...], row)
    rows[...] = jnp.broadcast_to(row, (C, C))


def steps(totals):
    row = jnp.sum(totals[...], axis=0, keepdims=True)
    lanes = lane_of((1, C))
    gg, gh, guu, guv, gvv, huu, huv, hvv = [jnp.sum(jnp.where(lanes == i, row, 0.0), axis=1, keepdims=True) for i in range(8)]
    one = gg / (gh + EPSILON)
    two = (guu - 2.0 * one * guv + one * one * gvv) / (huu - 2.0 * one * huv + one * one * hvv + EPSILON)
    return one, two


def fourth_kernel(*refs):
    it = iter(refs)
    take = lambda n: [next(it) for _ in range(n)]
    totals, heat, weight, free, resp = take(5)
    lift_1 = take(6)
    lift_u = take(6)
    lift_v = take(6)
    supply, state = take(2)
    held = take(6)
    own = take(6)
    sends = take(5)
    mid, turn, cols = take(3)
    one, two = steps(totals)
    for i in range(6):
        held[i][...] = one * lift_1[i][...] + two * (lift_u[i][...] - one * lift_v[i][...])
    cols[...] = pack_columns(turn, held[2][...], held[3][...])
    lift_dense(supply, cols, held, heat, -1.0)
    zero_ends(mid)
    zero_ends(state)

    def plane(z, carry):
        state[z + 1] = free[z + 1] - one * resp[z + 1]
        return carry

    lax.fori_loop(0, CZ, plane, 0, unroll=UNROLL)
    sweep(state, mid, weight, supply)
    sweep(mid, state, weight, supply)
    own_faces(state, own, turn)
    pack_sends(sends, own, 0, None)


def last_kernel(*refs):
    it = iter(refs)
    take = lambda n: [next(it) for _ in range(n)]
    totals, free, resp = take(3)
    held = take(3)
    lift_3 = take(3)
    lift_u = take(3)
    lift_v = take(3)
    (state,) = take(1)
    outs = take(3)
    one, two = steps(totals)

    def plane(z, carry):
        state[z] = free[z + 1] - one * resp[z + 1]
        return carry

    lax.fori_loop(0, CZ, plane, 0, unroll=UNROLL)
    for i in range(3):
        outs[i][...] = held[i][...] + one * lift_3[i][...] + two * (lift_u[i][...] - one * lift_v[i][...])


FIELD = jax.ShapeDtypeStruct((CZ, C, C), F32)
PADDED = jax.ShapeDtypeStruct((CZ + 2, C, C), F32)
FACE = jax.ShapeDtypeStruct((CZ, C), F32)
SQUARE = jax.ShapeDtypeStruct((C, C), F32)
FACES = [FACE] * 4 + [SQUARE] * 2
BASES = jax.ShapeDtypeStruct((3, C, C), F32)
ROW = jax.ShapeDtypeStruct((1, C), F32)
S_FIELD = pltpu.VMEM((CZ, C, C), F32)
S_PADDED = pltpu.VMEM((CZ + 2, C, C), F32)
S_SQUARE = pltpu.VMEM((C, C), F32)


def sends_of(n, extra):
    small = jax.ShapeDtypeStruct((n * CZ + extra, C), F32)
    return [small] * 4 + [jax.ShapeDtypeStruct((n * C + extra, C), F32)]


def call(kernel, name, outs, scratch, args, us):
    return pl.pallas_call(
        kernel,
        out_shape=tuple(outs),
        in_specs=[VM] * len(args),
        out_specs=tuple([VM] * len(outs)),
        scratch_shapes=scratch,
        name=name,
        compiler_params=pltpu.CompilerParams(vmem_limit_bytes=40 * 1024 * 1024),
        cost_estimate=pl.CostEstimate(flops=us * 10**7, transcendentals=0, bytes_accessed=2**20),
    )(*args)


def swap_pairs(axis, start):
    n = lax.axis_size(axis)
    pairs = []
    for i in range(start, n - 1, 2):
        pairs += [(i, i + 1), (i + 1, i)]
    return pairs


def exchange(sends):
    xa, xb, ya, yb, zz = sends
    zz = lax.ppermute(zz, "gz", swap_pairs("gz", 0))
    yb = lax.ppermute(yb, "gy", swap_pairs("gy", 1))
    xb = lax.ppermute(xb, "gx", swap_pairs("gx", 1))
    xa = lax.ppermute(xa, "gx", swap_pairs("gx", 0))
    ya = lax.ppermute(ya, "gy", swap_pairs("gy", 0))
    return [xa, xb, ya, yb, zz]


def gather_rows(rows):
    rows = lax.all_to_all(rows.reshape(C, 1, C), AXES, 0, 0)
    return rows.reshape(C, C)


def body(heat, cond, projection, segment_map):
    proj = projection[0, 0, 0]
    segs = segment_map[0, 0, 0]
    out = call(first_kernel, "first", [FIELD, PADDED, BASES] + FACES + sends_of(1, C), [S_PADDED, S_SQUARE], (heat, cond, proj, segs), 4)
    weight, state, bases = out[:3]
    own, sends = list(out[3:9]), out[9:]
    supply = heat
    prev = None
    held = None
    for pair in range(2):
        got = exchange(sends)
        (free,) = call(free_kernel, "free", [PADDED], [S_PADDED], (state, weight, supply), 3)
        first = pair == 0
        args = own + got + [bases] + ([] if first else [prev]) + [weight, free]
        outs = FACES + [ROW, PADDED] + FACES + FACES + sends_of(2, 0) + ([BASES] if first else [])
        out = list(call(functools.partial(second_kernel, first), "second", outs, [S_FIELD, S_PADDED, S_SQUARE, S_SQUARE], args, 4))
        lift_1, (sums, resp), own_u, own_v, sends = out[:6], out[6:8], out[8:14], out[14:20], out[20:25]
        if first:
            prev = out[25]
        got = exchange(sends)
        args = own_u + own_v + got + [bases, prev, weight, sums]
        out = list(call(third_kernel, "third", FACES + FACES + [SQUARE], [S_FIELD, S_FIELD, S_SQUARE, S_SQUARE], args, 3))
        lift_u, lift_v, rows = out[:6], out[6:12], out[12]
        totals = gather_rows(rows)
        if first:
            args = [totals, heat, weight, free, resp] + lift_1 + lift_u + lift_v
            out = list(call(fourth_kernel, "fourth", [FIELD, PADDED] + FACES + FACES + sends_of(1, 0), [S_PADDED, S_SQUARE, S_SQUARE], args, 5))
            supply, state, held, own, sends = out[0], out[1], out[2:8], out[8:14], out[14:]
    upper = lambda faces: [faces[1], faces[3], faces[5]]
    args = [totals, free, resp] + upper(held) + upper(lift_1) + upper(lift_u) + upper(lift_v)
    state, mx, my, mz = call(last_kernel, "last", [FIELD, FACE, FACE, SQUARE], [], args, 2)
    return state, mx[None, None, None], my[None, None, None], mz[None, None, None]


def solution(mesh):
    field = P("gz", "gx", "gy")
    in_specs = (field, field, P("gz", "gx", "gy", None, None, None), P("gz", "gx", "gy", None, None))
    face = P("gz", "gx", "gy", None, None)
    return jax.shard_map(body, mesh=mesh, in_specs=in_specs, out_specs=(field, face, face, face), check_vma=False)
```

profile of v0, /device:TPU:1, one launch (start us, length us, event | category | flops | bytes accessed | tf_op | source)
XLA Modules:
  0.0 128.1 jit_solution(15949244778380774776)
XLA Ops:
  0.6 0.7 copy.12
  1.3 1.6 %copy-done = f32[32,128,128]{2,1,0:T(8,128)S(1)} copy-done((f32[32,128,128]{2,1,0:T(8,128)S(1)}, f32[32,128,128]{2,1,0:T(8,128)}, u32[]{:S(2)}) %copy-start) | copy-done | bytes 2097176
  2.9 1.6 %copy-done.1 = f32[32,128,128]{2,1,0:T(8,128)S(1)} copy-done((f32[32,128,128]{2,1,0:T(8,128)S(1)}, f32[32,128,128]{2,1,0:T(8,128)}, u32[]{:S(2)}) %copy-start.1) | copy-done | bytes 2097176
  4.5 0.9 copy-done.2
  5.4 3.8 %first.1 = (f32[32,128,128]{2,1,0:T(8,128)S(1)}, f32[34,128,128]{2,1,0:T(8,128)S(1)}, f32[3,128,128]{2,1,0:T(8,128)S(1)}, f32[32,128]{1,0:T(8,128)S(1)}, f32[32,...) custom-call(f32[32,128,128]{2,1,0:T(8,128)S(1)} %copy-done, ...), custom_call_target="tpu_custom_call" | custom-call | flops 40000000 | bytes 1048576 | tf_op jit(solution)/shard_map/first/pallas_call | solution.py:365
  9.2 3.6 %collective-permute-start.4 = (f32[256,128]{1,0:T(8,128)S(1)}, f32[256,128]{1,0:T(8,128)S(1)}, u32[]{:S(2)}, u32[]{:S(2)}) collective-permute-start(f32[256,128]{1,0:T(8,128)S(1)} %get-tuple-element.116), channel_id=1, source_target_pairs={{0,1},{1,0},{2,3},{3,2},{4,5},{5,4},{6,7},{7,6},{8,9},{9,8},{10,11... | collective-permute-start | bytes 393224 | tf_op jit(solution)/shard_map/ppermute | solution.py:387
  12.8 1.3 %collective-permute-start = (f32[160,128]{1,0:T(8,128)S(1)}, f32[160,128]{1,0:T(8,128)S(1)}, u32[]{:S(2)}, u32[]{:S(2)}) collective-permute-start(f32[160,128]{1,0:T(8,128)S(1)} %get-tuple-element.112), channel_id=1, source_target_pairs={{0,32},{32,0},{64,96},{96,64},{1,33},{33,1},{65,97},{97,65},{2,34}... | collective-permute-start | bytes 245768 | tf_op jit(solution)/shard_map/ppermute | solution.py:390
  14.1 0.7 collective-permute-start.1
  14.8 1.3 %collective-permute-start.2 = (f32[160,128]{1,0:T(8,128)S(1)}, f32[160,128]{1,0:T(8,128)S(1)}, u32[]{:S(2)}, u32[]{:S(2)}) collective-permute-start(f32[160,128]{1,0:T(8,128)S(1)} %get-tuple-element.114), channel_id=1, source_target_pairs={{0,2},{2,0},{4,6},{6,4},{8,10},{10,8},{12,14},{14,12},{16,18},{18,... | collective-permute-start | bytes 245768 | tf_op jit(solution)/shard_map/ppermute | solution.py:391
  16.1 3.4 %collective-permute-start.3 = (f32[160,128]{1,0:T(8,128)S(1)}, f32[160,128]{1,0:T(8,128)S(1)}, u32[]{:S(2)}, u32[]{:S(2)}) collective-permute-start(f32[160,128]{1,0:T(8,128)S(1)} %get-tuple-element.115), channel_id=1, source_target_pairs={{2,4},{4,2},{6,8},{8,6},{10,12},{12,10},{14,16},{16,14},{18,20},{2... | collective-permute-start | bytes 245768 | tf_op jit(solution)/shard_map/ppermute | solution.py:388
  19.5 3.4 %free.2.refs_13_.refs_3_ = f32[34,128,128]{2,1,0:T(8,128)S(1)} custom-call(f32[34,128,128]{2,1,0:T(8,128)S(1)} %get-tuple-element.119.state, f32[32,128,128]{2,1,0:T(8,128)S(1)} %get-tuple-element.118.weight.refs_12_.refs_19_.refs_2_.refs_13_, f32[32,128,128]{2,1,0:T(8,128)S(1)} %copy-done), custom_call_target="tpu_custom_call" | custom-call | flops 30000000 | bytes 1048576 | tf_op jit(solution)/shard_map/free/pallas_call | solution.py:365
  23.0 7.0 %second.2 = (f32[32,128]{1,0:T(8,128)S(1)}, f32[32,128]{1,0:T(8,128)S(1)}, f32[32,128]{1,0:T(8,128)S(1)}, f32[32,128]{1,0:T(8,128)S(1)}, f32[128,128]{1,0:T(8,12...) custom-call(f32[32,128]{1,0:T(8,128)S(1)} %get-tuple-element.106.ref, ...), custom_call_target="tpu_custom_call" | custom-call | flops 40000000 | bytes 1048576 | tf_op jit(solution)/shard_map/second/pallas_call | solution.py:365
  30.3 3.8 %collective-permute-start.5 = (f32[64,128]{1,0:T(8,128)S(1)}, f32[64,128]{1,0:T(8,128)S(1)}, u32[]{:S(2)}, u32[]{:S(2)}) collective-permute-start(f32[64,128]{1,0:T(8,128)S(1)} %get-tuple-element.132), channel_id=1, source_target_pairs={{0,32},{32,0},{64,96},{96,64},{1,33},{33,1},{65,97},{97,65},{2,34}... | collective-permute-start | bytes 98312 | tf_op jit(solution)/shard_map/ppermute | solution.py:390
  34.1 0.7 collective-permute-start.6
  34.9 3.9 %collective-permute-start.8 = (f32[64,128]{1,0:T(8,128)S(1)}, f32[64,128]{1,0:T(8,128)S(1)}, u32[]{:S(2)}, u32[]{:S(2)}) collective-permute-start(f32[64,128]{1,0:T(8,128)S(1)} %get-tuple-element.135), channel_id=1, source_target_pairs={{2,4},{4,2},{6,8},{8,6},{10,12},{12,10},{14,16},{16,14},{18,20},{2... | collective-permute-start | bytes 98312 | tf_op jit(solution)/shard_map/ppermute | solution.py:388
  38.8 1.6 %collective-permute-done.8.refs_15_ = f32[64,128]{1,0:T(8,128)S(1)} collective-permute-done((f32[64,128]{1,0:T(8,128)S(1)}, f32[64,128]{1,0:T(8,128)S(1)}, u32[]{:S(2)}, u32[]{:S(2)}) %collective-permute-start.8) | collective-permute-done | bytes 32800 | tf_op jit(solution)/shard_map/ppermute | solution.py:388
  40.4 5.0 %third.2 = (f32[32,128]{1,0:T(8,128)S(1)}, f32[32,128]{1,0:T(8,128)S(1)}, f32[32,128]{1,0:T(8,128)S(1)}, f32[32,128]{1,0:T(8,128)S(1)}, f32[128,128]{1,0:T(8,128...) custom-call(f32[32,128]{1,0:T(8,128)S(1)} %get-tuple-element.120.ref, ...), custom_call_target="tpu_custom_call" | custom-call | flops 30000000 | bytes 1048576 | tf_op jit(solution)/shard_map/third/pallas_call | solution.py:365
  45.4 22.6 %all_to_all.10 = f32[128,1,128]{2,1,0:T(1,128)S(1)} all-to-all(f32[128,1,128]{2,1,0:T(1,128)S(1)} %bitcast.19), channel_id=1, replica_groups=mesh['gx'=4,'gy'=16,'gz'=2] {'gx','gy','gz'}, dimensions={0} | all-to-all | bytes 131072 | tf_op jit(solution)/shard_map/all_to_all | solution.py:396
  68.0 6.7 %fourth.1 = (f32[32,128,128]{2,1,0:T(8,128)S(1)}, f32[34,128,128]{2,1,0:T(8,128)S(1)}, f32[32,128]{1,0:T(8,128)}, f32[32,128]{1,0:T(8,128)S(1)}, f32[32,128]{1,0...) custom-call(f32[128,128]{1,0:T(8,128)S(1)} %bitcast.15, ...), custom_call_target="tpu_custom_call" | custom-call | flops 50000000 | bytes 1048576 | tf_op jit(solution)/shard_map/fourth/pallas_call | solution.py:365
  74.7 1.1 collective-permute-start.14
  76.8 1.2 collective-permute-start.12
  78.0 2.4 %collective-permute-start.13 = (f32[32,128]{1,0:T(8,128)S(1)}, f32[32,128]{1,0:T(8,128)S(1)}, u32[]{:S(2)}, u32[]{:S(2)}) collective-permute-start(f32[32,128]{1,0:T(8,128)S(1)} %get-tuple-element.168), channel_id=1, source_target_pairs={{2,4},{4,2},{6,8},{8,6},{10,12},{12,10},{14,16},{16,14},{18,20},{2... | collective-permute-start | bytes 49160 | tf_op jit(solution)/shard_map/ppermute | solution.py:388
  80.4 3.3 %free.3.refs_14_.refs_1_ = f32[34,128,128]{2,1,0:T(8,128)S(1)} custom-call(f32[34,128,128]{2,1,0:T(8,128)S(1)} %get-tuple-element.170.state, f32[32,128,128]{2,1,0:T(8,128)S(1)} %get-tuple-element.118.weight.refs_12_.refs_19_.refs_2_.refs_13_, f32[32,128,128]{2,1,0:T(8,128)S(1)} %get-tuple-element.171.supply), custom_call_target="tpu_custom_call" | custom-call | flops 30000000 | bytes 1048576 | tf_op jit(solution)/shard_map/free/pallas_call | solution.py:365
  83.7 7.6 %second.3 = (f32[32,128]{1,0:T(8,128)}, f32[32,128]{1,0:T(8,128)S(1)}, f32[32,128]{1,0:T(8,128)}, f32[32,128]{1,0:T(8,128)S(1)}, f32[128,128]{1,0:T(8,128)}, /*i...) custom-call(f32[32,128]{1,0:T(8,128)S(1)} %get-tuple-element.159.ref, ...), custom_call_target="tpu_custom_call" | custom-call | flops 40000000 | bytes 1048576 | tf_op jit(solution)/shard_map/second/pallas_call | solution.py:365
  91.3 1.7 %collective-permute-start.19 = (f32[256,128]{1,0:T(8,128)S(1)}, f32[256,128]{1,0:T(8,128)S(1)}, u32[]{:S(2)}, u32[]{:S(2)}) collective-permute-start(f32[256,128]{1,0:T(8,128)S(1)} %get-tuple-element.188), channel_id=1, source_target_pairs={{0,1},{1,0},{2,3},{3,2},{4,5},{5,4},{6,7},{7,6},{8,9},{9,8},{10,11... | collective-permute-start | bytes 393224 | tf_op jit(solution)/shard_map/ppermute | solution.py:387
  93.0 2.9 %collective-permute-start.15 = (f32[64,128]{1,0:T(8,128)S(1)}, f32[64,128]{1,0:T(8,128)S(1)}, u32[]{:S(2)}, u32[]{:S(2)}) collective-permute-start(f32[64,128]{1,0:T(8,128)S(1)} %get-tuple-element.184), channel_id=1, source_target_pairs={{0,32},{32,0},{64,96},{96,64},{1,33},{33,1},{65,97},{97,65},{2,34}... | collective-permute-start | bytes 98312 | tf_op jit(solution)/shard_map/ppermute | solution.py:390
  95.9 0.7 collective-permute-start.16
  96.6 4.1 %collective-permute-start.18 = (f32[64,128]{1,0:T(8,128)S(1)}, f32[64,128]{1,0:T(8,128)S(1)}, u32[]{:S(2)}, u32[]{:S(2)}) collective-permute-start(f32[64,128]{1,0:T(8,128)S(1)} %get-tuple-element.187), channel_id=1, source_target_pairs={{2,4},{4,2},{6,8},{8,6},{10,12},{12,10},{14,16},{16,14},{18,20},{2... | collective-permute-start | bytes 98312 | tf_op jit(solution)/shard_map/ppermute | solution.py:388
  100.8 1.4 %collective-permute-done.18.refs_15_ = f32[64,128]{1,0:T(8,128)S(1)} collective-permute-done((f32[64,128]{1,0:T(8,128)S(1)}, f32[64,128]{1,0:T(8,128)S(1)}, u32[]{:S(2)}, u32[]{:S(2)}) %collective-permute-start.18) | collective-permute-done | bytes 32800 | tf_op jit(solution)/shard_map/ppermute | solution.py:388
  102.2 5.5 %third.3 = (f32[32,128]{1,0:T(8,128)}, f32[32,128]{1,0:T(8,128)S(1)}, f32[32,128]{1,0:T(8,128)}, f32[32,128]{1,0:T(8,128)S(1)}, f32[128,128]{1,0:T(8,128)}, /*in...) custom-call(f32[32,128]{1,0:T(8,128)S(1)} %get-tuple-element.172.ref, ...), custom_call_target="tpu_custom_call" | custom-call | flops 30000000 | bytes 1048576 | tf_op jit(solution)/shard_map/third/pallas_call | solution.py:365
  107.7 18.8 %all_to_all.11 = f32[128,1,128]{2,1,0:T(1,128)S(1)} all-to-all(f32[128,1,128]{2,1,0:T(1,128)S(1)} %bitcast.18), channel_id=1, replica_groups=mesh['gx'=4,'gy'=16,'gz'=2] {'gx','gy','gz'}, dimensions={0} | all-to-all | bytes 131072 | tf_op jit(solution)/shard_map/all_to_all | solution.py:396
  126.4 1.7 %last.1 = (f32[32,128,128]{2,1,0:T(8,128)}, f32[32,128]{1,0:T(8,128)}, f32[32,128]{1,0:T(8,128)}, f32[128,128]{1,0:T(8,128)}) custom-call(f32[128,128]{1,0:T(8,128)S(1)} %bitcast.16, f32[34,128,128]{2,1,0:T(8,128)S(1)} %free.3.refs_14_.refs_1_, f32[34,128,128]{2,1,0:T(8,128)S(1)} %get-tuple-element.191.refs_2_, f32[32,128]{1,0:T(8,128)S(1)} %get-tuple-element.192.refs_3_, ...), custom_call_target="tpu_custom_call" | custom-call | flops 20000000 | bytes 1048576 | tf_op jit(solution)/shard_map/last/pallas_call | solution.py:365
  (26 shorter events, 1.5 us)
Async XLA Ops:
  1.3 1.6 %copy-start = (f32[32,128,128]{2,1,0:T(8,128)S(1)}, f32[32,128,128]{2,1,0:T(8,128)}, u32[]{:S(2)}) copy-start(f32[32,128,128]{2,1,0:T(8,128)} %refs_1_.1) | copy-start | bytes 6291460
  2.9 1.6 %copy-start.1 = (f32[32,128,128]{2,1,0:T(8,128)S(1)}, f32[32,128,128]{2,1,0:T(8,128)}, u32[]{:S(2)}) copy-start(f32[32,128,128]{2,1,0:T(8,128)} %cond.1) | copy-start | bytes 6291460
  4.5 0.9 copy-start.2
  9.2 13.8 %collective-permute-start.4 = (f32[256,128]{1,0:T(8,128)S(1)}, f32[256,128]{1,0:T(8,128)S(1)}, u32[]{:S(2)}, u32[]{:S(2)}) collective-permute-start(f32[256,128]{1,0:T(8,128)S(1)} %get-tuple-element.116), channel_id=1, source_target_pairs={{0,1},{1,0},{2,3},{3,2},{4,5},{5,4},{6,7},{7,6},{8,9},{9,8},{10,11... | collective-permute-start | bytes 393224 | tf_op jit(solution)/shard_map/ppermute | solution.py:387
  12.8 10.1 %collective-permute-start = (f32[160,128]{1,0:T(8,128)S(1)}, f32[160,128]{1,0:T(8,128)S(1)}, u32[]{:S(2)}, u32[]{:S(2)}) collective-permute-start(f32[160,128]{1,0:T(8,128)S(1)} %get-tuple-element.112), channel_id=1, source_target_pairs={{0,32},{32,0},{64,96},{96,64},{1,33},{33,1},{65,97},{97,65},{2,34}... | collective-permute-start | bytes 245768 | tf_op jit(solution)/shard_map/ppermute | solution.py:390
  14.1 8.8 %collective-permute-start.1 = (f32[160,128]{1,0:T(8,128)S(1)}, f32[160,128]{1,0:T(8,128)S(1)}, u32[]{:S(2)}, u32[]{:S(2)}) collective-permute-start(f32[160,128]{1,0:T(8,128)S(1)} %get-tuple-element.113), channel_id=1, source_target_pairs={{32,64},{64,32},{33,65},{65,33},{34,66},{66,34},{35,67},{67,35},{3... | collective-permute-start | bytes 245768 | tf_op jit(solution)/shard_map/ppermute | solution.py:389
  14.8 8.2 %collective-permute-start.2 = (f32[160,128]{1,0:T(8,128)S(1)}, f32[160,128]{1,0:T(8,128)S(1)}, u32[]{:S(2)}, u32[]{:S(2)}) collective-permute-start(f32[160,128]{1,0:T(8,128)S(1)} %get-tuple-element.114), channel_id=1, source_target_pairs={{0,2},{2,0},{4,6},{6,4},{8,10},{10,8},{12,14},{14,12},{16,18},{18,... | collective-permute-start | bytes 245768 | tf_op jit(solution)/shard_map/ppermute | solution.py:391
  16.1 6.9 %collective-permute-start.3 = (f32[160,128]{1,0:T(8,128)S(1)}, f32[160,128]{1,0:T(8,128)S(1)}, u32[]{:S(2)}, u32[]{:S(2)}) collective-permute-start(f32[160,128]{1,0:T(8,128)S(1)} %get-tuple-element.115), channel_id=1, source_target_pairs={{2,4},{4,2},{6,8},{8,6},{10,12},{12,10},{14,16},{16,14},{18,20},{2... | collective-permute-start | bytes 245768 | tf_op jit(solution)/shard_map/ppermute | solution.py:388
  30.0 10.4 %collective-permute-start.9 = (f32[256,128]{1,0:T(8,128)S(1)}, f32[256,128]{1,0:T(8,128)S(1)}, u32[]{:S(2)}, u32[]{:S(2)}) collective-permute-start(f32[256,128]{1,0:T(8,128)S(1)} %get-tuple-element.136), channel_id=1, source_target_pairs={{0,1},{1,0},{2,3},{3,2},{4,5},{5,4},{6,7},{7,6},{8,9},{9,8},{10,11... | collective-permute-start | bytes 393224 | tf_op jit(solution)/shard_map/ppermute | solution.py:387
  30.3 8.5 %collective-permute-start.5 = (f32[64,128]{1,0:T(8,128)S(1)}, f32[64,128]{1,0:T(8,128)S(1)}, u32[]{:S(2)}, u32[]{:S(2)}) collective-permute-start(f32[64,128]{1,0:T(8,128)S(1)} %get-tuple-element.132), channel_id=1, source_target_pairs={{0,32},{32,0},{64,96},{96,64},{1,33},{33,1},{65,97},{97,65},{2,34}... | collective-permute-start | bytes 98312 | tf_op jit(solution)/shard_map/ppermute | solution.py:390
  34.1 4.7 %collective-permute-start.6 = (f32[64,128]{1,0:T(8,128)S(1)}, f32[64,128]{1,0:T(8,128)S(1)}, u32[]{:S(2)}, u32[]{:S(2)}) collective-permute-start(f32[64,128]{1,0:T(8,128)S(1)} %get-tuple-element.133), channel_id=1, source_target_pairs={{32,64},{64,32},{33,65},{65,33},{34,66},{66,34},{35,67},{67,35},{3... | collective-permute-start | bytes 98312 | tf_op jit(solution)/shard_map/ppermute | solution.py:389
  34.8 4.0 %collective-permute-start.7 = (f32[64,128]{1,0:T(8,128)S(1)}, f32[64,128]{1,0:T(8,128)S(1)}, u32[]{:S(2)}, u32[]{:S(2)}) collective-permute-start(f32[64,128]{1,0:T(8,128)S(1)} %get-tuple-element.134), channel_id=1, source_target_pairs={{0,2},{2,0},{4,6},{6,4},{8,10},{10,8},{12,14},{14,12},{16,18},{18,... | collective-permute-start | bytes 98312 | tf_op jit(solution)/shard_map/ppermute | solution.py:391
  34.9 5.5 %collective-permute-start.8 = (f32[64,128]{1,0:T(8,128)S(1)}, f32[64,128]{1,0:T(8,128)S(1)}, u32[]{:S(2)}, u32[]{:S(2)}) collective-permute-start(f32[64,128]{1,0:T(8,128)S(1)} %get-tuple-element.135), channel_id=1, source_target_pairs={{2,4},{4,2},{6,8},{8,6},{10,12},{12,10},{14,16},{16,14},{18,20},{2... | collective-permute-start | bytes 98312 | tf_op jit(solution)/shard_map/ppermute | solution.py:388
  74.7 9.0 %collective-permute-start.14 = (f32[128,128]{1,0:T(8,128)S(1)}, f32[128,128]{1,0:T(8,128)S(1)}, u32[]{:S(2)}, u32[]{:S(2)}) collective-permute-start(f32[128,128]{1,0:T(8,128)S(1)} %get-tuple-element.169), channel_id=1, source_target_pairs={{0,1},{1,0},{2,3},{3,2},{4,5},{5,4},{6,7},{7,6},{8,9},{9,8},{10,11... | collective-permute-start | bytes 196616 | tf_op jit(solution)/shard_map/ppermute | solution.py:387
  75.8 7.9 %collective-permute-start.10 = (f32[32,128]{1,0:T(8,128)S(1)}, f32[32,128]{1,0:T(8,128)S(1)}, u32[]{:S(2)}, u32[]{:S(2)}) collective-permute-start(f32[32,128]{1,0:T(8,128)S(1)} %get-tuple-element.165), channel_id=1, source_target_pairs={{0,32},{32,0},{64,96},{96,64},{1,33},{33,1},{65,97},{97,65},{2,34}... | collective-permute-start | bytes 49160 | tf_op jit(solution)/shard_map/ppermute | solution.py:390
  76.2 7.5 %collective-permute-start.11 = (f32[32,128]{1,0:T(8,128)S(1)}, f32[32,128]{1,0:T(8,128)S(1)}, u32[]{:S(2)}, u32[]{:S(2)}) collective-permute-start(f32[32,128]{1,0:T(8,128)S(1)} %get-tuple-element.166), channel_id=1, source_target_pairs={{32,64},{64,32},{33,65},{65,33},{34,66},{66,34},{35,67},{67,35},{3... | collective-permute-start | bytes 49160 | tf_op jit(solution)/shard_map/ppermute | solution.py:389
  76.8 6.9 %collective-permute-start.12 = (f32[32,128]{1,0:T(8,128)S(1)}, f32[32,128]{1,0:T(8,128)S(1)}, u32[]{:S(2)}, u32[]{:S(2)}) collective-permute-start(f32[32,128]{1,0:T(8,128)S(1)} %get-tuple-element.167), channel_id=1, source_target_pairs={{0,2},{2,0},{4,6},{6,4},{8,10},{10,8},{12,14},{14,12},{16,18},{18,... | collective-permute-start | bytes 49160 | tf_op jit(solution)/shard_map/ppermute | solution.py:391
  78.0 5.7 %collective-permute-start.13 = (f32[32,128]{1,0:T(8,128)S(1)}, f32[32,128]{1,0:T(8,128)S(1)}, u32[]{:S(2)}, u32[]{:S(2)}) collective-permute-start(f32[32,128]{1,0:T(8,128)S(1)} %get-tuple-element.168), channel_id=1, source_target_pairs={{2,4},{4,2},{6,8},{8,6},{10,12},{12,10},{14,16},{16,14},{18,20},{2... | collective-permute-start | bytes 49160 | tf_op jit(solution)/shard_map/ppermute | solution.py:388
  91.3 10.9 %collective-permute-start.19 = (f32[256,128]{1,0:T(8,128)S(1)}, f32[256,128]{1,0:T(8,128)S(1)}, u32[]{:S(2)}, u32[]{:S(2)}) collective-permute-start(f32[256,128]{1,0:T(8,128)S(1)} %get-tuple-element.188), channel_id=1, source_target_pairs={{0,1},{1,0},{2,3},{3,2},{4,5},{5,4},{6,7},{7,6},{8,9},{9,8},{10,11... | collective-permute-start | bytes 393224 | tf_op jit(solution)/shard_map/ppermute | solution.py:387
  93.0 7.8 %collective-permute-start.15 = (f32[64,128]{1,0:T(8,128)S(1)}, f32[64,128]{1,0:T(8,128)S(1)}, u32[]{:S(2)}, u32[]{:S(2)}) collective-permute-start(f32[64,128]{1,0:T(8,128)S(1)} %get-tuple-element.184), channel_id=1, source_target_pairs={{0,32},{32,0},{64,96},{96,64},{1,33},{33,1},{65,97},{97,65},{2,34}... | collective-permute-start | bytes 98312 | tf_op jit(solution)/shard_map/ppermute | solution.py:390
  95.9 4.9 %collective-permute-start.16 = (f32[64,128]{1,0:T(8,128)S(1)}, f32[64,128]{1,0:T(8,128)S(1)}, u32[]{:S(2)}, u32[]{:S(2)}) collective-permute-start(f32[64,128]{1,0:T(8,128)S(1)} %get-tuple-element.185), channel_id=1, source_target_pairs={{32,64},{64,32},{33,65},{65,33},{34,66},{66,34},{35,67},{67,35},{3... | collective-permute-start | bytes 98312 | tf_op jit(solution)/shard_map/ppermute | solution.py:389
  96.5 4.3 %collective-permute-start.17 = (f32[64,128]{1,0:T(8,128)S(1)}, f32[64,128]{1,0:T(8,128)S(1)}, u32[]{:S(2)}, u32[]{:S(2)}) collective-permute-start(f32[64,128]{1,0:T(8,128)S(1)} %get-tuple-element.186), channel_id=1, source_target_pairs={{0,2},{2,0},{4,6},{6,4},{8,10},{10,8},{12,14},{14,12},{16,18},{18,... | collective-permute-start | bytes 98312 | tf_op jit(solution)/shard_map/ppermute | solution.py:391
  96.6 5.5 %collective-permute-start.18 = (f32[64,128]{1,0:T(8,128)S(1)}, f32[64,128]{1,0:T(8,128)S(1)}, u32[]{:S(2)}, u32[]{:S(2)}) collective-permute-start(f32[64,128]{1,0:T(8,128)S(1)} %get-tuple-element.187), channel_id=1, source_target_pairs={{2,4},{4,2},{6,8},{8,6},{10,12},{12,10},{14,16},{16,14},{18,20},{2... | collective-permute-start | bytes 98312 | tf_op jit(solution)/shard_map/ppermute | solution.py:388
where the time goes:
time: 129 us; the launch traced here: 128 us
  Pallas kernels  44 us (34%)
  blocking collectives  41.4 us (32%)
  starting transfers between devices  34.2 us (27%)
  local copies, waits for them, and re-layouts  4.79 us (4%)
  waiting for transfers between devices  2.97 us (2%)
    pallas_call x9, Pallas kernels, call(): pl.pallas_call(kernel, out_shape=tuple(outs), in_specs=[VM] * len(args),...  44 us
    all_to_all x2, blocking collectives, gather_rows(): rows = lax.all_to_all(rows.reshape(C, 1, C), AXES, 0, 0)  41.4 us
    ppermute x4, starting transfers between devices, exchange(): yb = lax.ppermute(yb, 'gy', swap_pairs('gy', 1))  13.8 us
    ppermute x4, starting transfers between devices, exchange(): xa = lax.ppermute(xa, 'gx', swap_pairs('gx', 0))  8.33 us
    ppermute x4, starting transfers between devices, exchange(): zz = lax.ppermute(zz, 'gz', swap_pairs('gz', 0))  6.71 us
    unnamed x7, local copies, waits for them, and re-layouts  4.79 us
    ppermute x4, waiting for transfers between devices, exchange(): yb = lax.ppermute(yb, 'gy', swap_pairs('gy', 1))  2.93 us
    ppermute x4, starting transfers between devices, exchange(): ya = lax.ppermute(ya, 'gy', swap_pairs('gy', 0))  2.66 us
  transfers between devices with their start and end apart: 20, of which 2 were waited for; matrix products, arithmetic and copies ran while one was open for 0% of the time, Pallas kernels for 5%

commit v1 on v0

v1 whole, which is shorter than its diff:
```python
import functools

import jax
import jax.numpy as jnp
from jax import lax
from jax.experimental import pallas as pl
from jax.experimental.pallas import tpu as pltpu
from jax.sharding import PartitionSpec as P

HIGH = lax.Precision.HIGHEST
DAMPING_WEIGHT = 0.8
EPSILON = 1e-06
AXES = ("gx", "gy", "gz")
CZ = 32
C = 128
F32 = jnp.float32
UNROLL = 4
WIDE = 16
PARTS = 4
KEPT = 1.0 - DAMPING_WEIGHT

VM = pl.BlockSpec(memory_space=pltpu.MemorySpace.VMEM)


def dot(a, b):
    return jnp.dot(a, b, precision=HIGH, preferred_element_type=F32)


def dot_t(a, b):
    return lax.dot_general(a, b, (((1,), (1,)), ((), ())), precision=HIGH, preferred_element_type=F32)


def lane_of(shape):
    return lax.broadcasted_iota(jnp.int32, shape, len(shape) - 1)


def row_of(shape):
    return lax.broadcasted_iota(jnp.int32, shape, len(shape) - 2)


def zero_ends(ref):
    ref[0] = jnp.zeros((C, C), F32)
    ref[CZ + 1] = jnp.zeros((C, C), F32)


def neighbours(src, z):
    centre = src[z + 1]
    return centre, src[z] + src[z + 2] + in_plane(centre)


def in_plane(centre):
    shape = centre.shape
    rows = row_of(shape)
    lanes = lane_of(shape)
    near = jnp.where(rows == 0, 0.0, pltpu.roll(centre, 1, 0))
    near = near + jnp.where(rows == shape[0] - 1, 0.0, pltpu.roll(centre, shape[0] - 1, 0))
    near = near + jnp.where(lanes == 0, 0.0, pltpu.roll(centre, 1, 1))
    return near + jnp.where(lanes == C - 1, 0.0, pltpu.roll(centre, C - 1, 1))


def sweep(src, dst, weight, supply):
    def plane(z, carry):
        centre, near = neighbours(src, z)
        dst[z + 1] = KEPT * centre + weight[z] * (supply[z] + near)
        return carry

    lax.fori_loop(0, CZ, plane, 0, unroll=UNROLL)


def row_layer(src, base, at, out):
    for z in range(CZ):
        out[z : z + 1, :] = src[z + base, at : at + 1, :]


def column_layers(src, base, turn):
    group = lane_of((C, C)) // 4

    def plane(z, packed):
        return jnp.where(group == z, pltpu.roll(src[z + base], 4 * z + 2, 1), packed)

    packed = lax.fori_loop(0, CZ, plane, jnp.zeros((C, C), F32), unroll=WIDE)
    turn[...] = packed.T


def layer_rows(i):
    return pl.ds(i, CZ, stride=4)


def pack_columns(turn, low, high):
    turn[...] = jnp.zeros((C, C), F32)
    turn[layer_rows(1), :] = high
    turn[layer_rows(2), :] = low
    return turn[...].T


def column_plane(packed, z):
    lanes = lane_of((C, C))
    edge = (lanes == 0) | (lanes == C - 1)
    return jnp.where(edge, pltpu.roll(packed, C - 2 - 4 * z, 1), 0.0)


def lift_dense(dst, cols, faces, base, sign):
    def plane(z, carry):
        col = column_plane(cols[...], z)
        if base is None:
            dst[z] = sign * col
        else:
            dst[z] = base[z] + sign * col
        return carry

    lax.fori_loop(0, CZ, plane, 0, unroll=WIDE)
    for z in range(CZ):
        dst[z, 0:1, :] = dst[z, 0:1, :] + sign * faces[0][z : z + 1, :]
        dst[z, C - 1 : C, :] = dst[z, C - 1 : C, :] + sign * faces[1][z : z + 1, :]
    dst[0] = dst[0] + sign * faces[4][...]
    dst[CZ - 1] = dst[CZ - 1] + sign * faces[5][...]


EDGES = (0, 1, C - 2, C - 1)


def rim(low, high, at):
    lanes = lane_of(low.shape)
    a = low if at == 0 else pltpu.roll(low, C - at, 1)
    b = high if at == C - 1 else pltpu.roll(high, C - 1 - at, 1)
    return jnp.where(lanes == 0, a, jnp.where(lanes == C - 1, b, 0.0))


def ends(low, high):
    rows = row_of((CZ, C))
    return jnp.where(rows == 0, low, jnp.where(rows == CZ - 1, high, 0.0))


def lift_layers(faces, turn, inner):
    bx, hx, by, hy, bz, hz = [f[...] for f in faces]
    lanes = lane_of((C, C))
    columns = jnp.where(lanes < 4, pltpu.roll(bz, 2, 1), pltpu.roll(hz, 6, 1)).T
    at = lambda i: columns[i : i + 1, :]
    column = {C - 2: (at(0), at(4)), C - 1: (at(1), at(5)), 0: (at(2), at(6)), 1: (at(3), at(7))}
    edges = EDGES if inner else (0, C - 1)
    on_x = {}
    on_y = {}
    for e in edges:
        on_x[e] = rim(by, hy, e) + ends(bz[e : e + 1, :], hz[e : e + 1, :])
        on_y[e] = rim(bx, hx, e) + ends(*column[e])
    on_x[0] = on_x[0] + bx
    on_x[C - 1] = on_x[C - 1] + hx
    on_y[0] = on_y[0] + by
    on_y[C - 1] = on_y[C - 1] + hy
    packed = pack_columns(turn, by, hy)
    rows = row_of((C, C))
    on_z = {}
    for z in (0, 1, CZ - 2, CZ - 1) if inner else (0, CZ - 1):
        p = column_plane(packed, z)
        p = p + jnp.where(rows == 0, bx[z : z + 1, :], jnp.where(rows == C - 1, hx[z : z + 1, :], 0.0))
        on_z[z] = p + bz if z == 0 else p + hz if z == CZ - 1 else p
    return on_x, on_y, on_z


def layer_weights(weight, wx, wy):
    return (
        {e: wx[i] for i, e in enumerate(EDGES)},
        {e: wy[i] for i, e in enumerate(EDGES)},
        {z: weight[z] for z in (0, 1, CZ - 2, CZ - 1)},
    )


def face_response(layers, weights):
    out = []
    for layer, w, last in zip(layers, weights, (C - 1, C - 1, CZ - 1)):
        for face, inside in ((0, 1), (last, last - 1)):
            once = w[face] * layer[face]
            near = in_plane(once) + w[inside] * layer[inside]
            out.append(KEPT * once + w[face] * (layer[face] + near))
    return out


def fold(t):
    return jnp.sum(t.reshape(t.shape[0] // 8, 8, C), axis=0)


def layer_energy(a, b, weights):
    rows = row_of((CZ, C))
    lanes = lane_of((CZ, C))
    inner = (rows > 0) & (rows < CZ - 1)
    both = inner & (lanes > 0) & (lanes < C - 1)
    acc = jnp.zeros((8, C), F32)
    for layers_a, layers_b, w, last, mask in zip(a, b, weights, (C - 1, C - 1, CZ - 1), (inner, both, None)):
        for e in (0, last):
            t = layers_a[e] * layers_b[e] * w[e]
            acc = acc + fold(t if mask is None else jnp.where(mask, t, 0.0))
    return jnp.sum(acc) / DAMPING_WEIGHT


def places():
    x, y, z = (lax.axis_index(a) for a in AXES)
    more = [i < lax.axis_size(a) - 1 for a, i in zip(AXES, (x, y, z))]
    return x % 2 == 0, y % 2 == 0, z == 0, more


def pick(flag, a, b):
    return lax.select(jnp.broadcast_to(flag, a.shape), a, b)


def pack_sends(sends, faces, index):
    xeven, yeven, zlow, _ = places()
    xa, xb, ya, yb, zz = sends
    for even, a, b, lo, hi in ((xeven, xa, xb, faces[0], faces[1]), (yeven, ya, yb, faces[2], faces[3])):
        s = slice(index * CZ, (index + 1) * CZ)
        a[s, :] = pick(even, hi, lo)
        b[s, :] = pick(even, lo, hi)
    zz[index * C : (index + 1) * C, :] = pick(zlow, faces[5], faces[4])


def own_faces(src, own, turn):
    row_layer(src, 1, 0, own[0])
    row_layer(src, 1, C - 1, own[1])
    column_layers(src, 1, turn)
    own[2][...] = turn[layer_rows(2), :]
    own[3][...] = turn[layer_rows(1), :]
    own[4][...] = src[1]
    own[5][...] = src[CZ]


def first_kernel(heat_in, cond_in, proj, segs, weight, state, bases, heat, *refs):
    own = refs[:6]
    sends = refs[6:11]
    cond, start, turn, sems = refs[11:]
    part = CZ // PARTS
    copies = []
    for i in range(PARTS):
        s = pl.ds(i * part, part)
        pair = (
            pltpu.make_async_copy(cond_in.at[s], cond.at[s], sems.at[0, i]),
            pltpu.make_async_copy(heat_in.at[s], heat.at[s], sems.at[1, i]),
        )
        for c in pair:
            c.start()
        copies.append(pair)
    for d in range(3):
        onehot = jnp.where(row_of((C, C)) == segs[d : d + 1, :], 1.0, 0.0).astype(F32)
        bases[d] = dot_t(onehot, proj[d])
    zero_ends(start)
    zero_ends(state)

    def plane(z, carry):
        w = DAMPING_WEIGHT / (6.0 + cond[z])
        weight[z] = w
        start[z + 1] = w * heat[z]
        return carry

    for i, pair in enumerate(copies):
        for c in pair:
            c.wait()
        lax.fori_loop(i * part, (i + 1) * part, plane, 0, unroll=UNROLL)
    sweep(start, state, weight, heat)
    own_faces(state, own, turn)
    pack_sends(sends, [f[...] for f in own], 0)
    for a in sends[:2]:
        a[CZ : CZ + C, :] = bases[0]
    for a in sends[2:4]:
        a[CZ : CZ + C, :] = bases[1]
    sends[4][C : 2 * C, :] = bases[2]


def free_kernel(first, state, weight, supply, *refs):
    out = refs[0]
    own = refs[1:7]
    mid, turn = refs[-2:]
    zero_ends(mid)
    zero_ends(out)
    sweep(state, mid, weight, supply)
    sweep(mid, out, weight, supply)
    own_faces(out, own, turn)
    if first:
        wx, wy = refs[7:9]
        for i, e in enumerate(EDGES):
            row_layer(weight, 0, e, wx.at[i])
        column_layers(weight, 0, turn)
        for i, e in enumerate((2, 3, 0, 1)):
            wy[i] = turn[layer_rows(e), :]


def jumps(own, got, bases, prev_bases, n, lifted):
    xeven, yeven, zlow, more = places()
    xa, xb, ya, yb, zz = got
    for d, (even, a, b, rows) in enumerate(((xeven, xa, xb, n * CZ), (yeven, ya, yb, n * CZ), (zlow, zz, zz, n * C))):
        a = a[0:rows, :]
        b = b[0:rows, :]
        up = own[2 * d + 1][...] - dot(pick(even, a, b), bases[d])
        up = jnp.where(more[d], up, 0.0)
        down = pick(even, b, a) - dot(own[2 * d][...], prev_bases[d])
        back = -dot_t(down, prev_bases[d])
        if d == 2:
            back = jnp.where(zlow, 0.0, back)
        size = rows // n
        for i in range(n):
            lifted[i][2 * d][...] = back[i * size : (i + 1) * size, :]
            lifted[i][2 * d + 1][...] = up[i * size : (i + 1) * size, :]


def square_sum(a, b):
    return jnp.sum(sum(fold(a[i][...] * b[i][...]) for i in (1, 3, 5)))


def row_of_sums(values):
    lanes = lane_of((1, C))
    row = jnp.zeros((1, C), F32)
    for i, v in enumerate(values):
        row = jnp.where(lanes == i, v, row)
    return row


def second_kernel(first, *refs):
    it = iter(refs)
    take = lambda n: [next(it) for _ in range(n)]
    own = take(6)
    got = take(5)
    (bases,) = take(1)
    (prev,) = take(1) if not first else (None,)
    weight, wx, wy = take(3)
    own_u = take(6)
    lifted = take(6)
    own_uv = take(6)
    sends = take(5)
    if first:
        (prev,) = take(1)
    (turn,) = take(1)
    xeven, yeven, zlow, _ = places()
    if first:
        xa, xb, ya, yb, zz = got
        prev[0] = pick(xeven, xb[CZ:, :], xa[CZ:, :])
        prev[1] = pick(yeven, yb[CZ:, :], ya[CZ:, :])
        prev[2] = zz[C:, :]
    jumps(own, got, bases, prev, 1, [lifted])
    response = face_response(lift_layers(lifted, turn, True), layer_weights(weight, wx, wy))
    free = [f[...] for f in own_u]
    for o, u, v in zip(own_uv, free, response):
        n = u.shape[0]
        o[0:n, :] = u
        o[n:, :] = v
    pack_sends(sends, free, 0)
    pack_sends(sends, response, 1)


def response_kernel(*refs):
    lifted = refs[:6]
    weight, resp, sums, lift, mid, turn, cols = refs[6:]
    cols[...] = pack_columns(turn, lifted[2][...], lifted[3][...])
    lift_dense(lift, cols, lifted, None, 1.0)
    zero_ends(mid)
    zero_ends(resp)

    def plane(z, acc):
        once = weight[z] * lift[z]
        mid[z + 1] = once
        return acc + fold(once * lift[z])

    acc = lax.fori_loop(0, CZ, plane, jnp.zeros((8, C), F32), unroll=UNROLL)
    sweep(mid, resp, weight, lift)
    sums[...] = row_of_sums([square_sum(lifted, lifted), jnp.sum(acc) / DAMPING_WEIGHT])


def third_kernel(*refs):
    it = iter(refs)
    take = lambda n: [next(it) for _ in range(n)]
    own_uv = take(6)
    got = take(5)
    bases, prev, weight, wx, wy, before = take(6)
    lift_u = take(6)
    lift_v = take(6)
    (rows,) = take(1)
    (turn,) = take(1)
    jumps(own_uv, got, bases, prev, 2, [lift_u, lift_v])
    weights = layer_weights(weight, wx, wy)
    u = lift_layers(lift_u, turn.at[0], False)
    v = lift_layers(lift_v, turn.at[1], False)
    sums = [square_sum(lift_u, lift_u), square_sum(lift_u, lift_v), square_sum(lift_v, lift_v)]
    sums += [layer_energy(u, u, weights), layer_energy(u, v, weights), layer_energy(v, v, weights)]
    lanes = lane_of((1, C))
    row = row_of_sums([0.0, 0.0] + sums)
    row = jnp.where(lanes < 2, before[...], row)
    rows[...] = jnp.broadcast_to(row, (C, C))


def steps(totals):
    row = jnp.sum(totals[...], axis=0, keepdims=True)
    lanes = lane_of((1, C))
    gg, gh, guu, guv, gvv, huu, huv, hvv = [jnp.sum(jnp.where(lanes == i, row, 0.0), axis=1, keepdims=True) for i in range(8)]
    one = gg / (gh + EPSILON)
    two = (guu - 2.0 * one * guv + one * one * gvv) / (huu - 2.0 * one * huv + one * one * hvv + EPSILON)
    return one, two


def fourth_kernel(*refs):
    it = iter(refs)
    take = lambda n: [next(it) for _ in range(n)]
    totals, heat, weight, free, resp = take(5)
    lift_1 = take(6)
    lift_u = take(6)
    lift_v = take(6)
    supply, state = take(2)
    held = take(6)
    own = take(6)
    sends = take(5)
    mid, turn, cols = take(3)
    one, two = steps(totals)
    for i in range(6):
        held[i][...] = one * lift_1[i][...] + two * (lift_u[i][...] - one * lift_v[i][...])
    cols[...] = pack_columns(turn, held[2][...], held[3][...])
    lift_dense(supply, cols, held, heat, -1.0)
    zero_ends(mid)
    zero_ends(state)

    def plane(z, carry):
        state[z + 1] = free[z + 1] - one * resp[z + 1]
        return carry

    lax.fori_loop(0, CZ, plane, 0, unroll=UNROLL)
    sweep(state, mid, weight, supply)
    sweep(mid, state, weight, supply)
    own_faces(state, own, turn)
    pack_sends(sends, [f[...] for f in own], 0)


def last_kernel(*refs):
    it = iter(refs)
    take = lambda n: [next(it) for _ in range(n)]
    totals, free, resp = take(3)
    held = take(3)
    lift_3 = take(3)
    lift_u = take(3)
    lift_v = take(3)
    (state,) = take(1)
    outs = take(3)
    one, two = steps(totals)

    def plane(z, carry):
        state[z] = free[z + 1] - one * resp[z + 1]
        return carry

    lax.fori_loop(0, CZ, plane, 0, unroll=UNROLL)
    for i in range(3):
        outs[i][...] = held[i][...] + one * lift_3[i][...] + two * (lift_u[i][...] - one * lift_v[i][...])


FIELD = jax.ShapeDtypeStruct((CZ, C, C), F32)
PADDED = jax.ShapeDtypeStruct((CZ + 2, C, C), F32)
FACE = jax.ShapeDtypeStruct((CZ, C), F32)
SQUARE = jax.ShapeDtypeStruct((C, C), F32)
FACES = [FACE] * 4 + [SQUARE] * 2
BASES = jax.ShapeDtypeStruct((3, C, C), F32)
LAYERS = jax.ShapeDtypeStruct((4, CZ, C), F32)
ROW = jax.ShapeDtypeStruct((1, C), F32)
S_FIELD = pltpu.VMEM((CZ, C, C), F32)
S_PADDED = pltpu.VMEM((CZ + 2, C, C), F32)
S_SQUARE = pltpu.VMEM((C, C), F32)


def sends_of(n, extra):
    small = jax.ShapeDtypeStruct((n * CZ + extra, C), F32)
    return [small] * 4 + [jax.ShapeDtypeStruct((n * C + extra, C), F32)]


def call(kernel, name, outs, scratch, args, us, in_specs=None):
    return list(
        pl.pallas_call(
            kernel,
            out_shape=tuple(outs),
            in_specs=in_specs or [VM] * len(args),
            out_specs=tuple([VM] * len(outs)),
            scratch_shapes=scratch,
            name=name,
            compiler_params=pltpu.CompilerParams(vmem_limit_bytes=40 * 1024 * 1024),
            cost_estimate=pl.CostEstimate(flops=us * 10**7, transcendentals=0, bytes_accessed=2**20),
        )(*args)
    )


def swap_pairs(axis, start):
    n = lax.axis_size(axis)
    pairs = []
    for i in range(start, n - 1, 2):
        pairs += [(i, i + 1), (i + 1, i)]
    return pairs


def exchange(sends):
    xa, xb, ya, yb, zz = sends
    zz = lax.ppermute(zz, "gz", swap_pairs("gz", 0))
    yb = lax.ppermute(yb, "gy", swap_pairs("gy", 1))
    xb = lax.ppermute(xb, "gx", swap_pairs("gx", 1))
    xa = lax.ppermute(xa, "gx", swap_pairs("gx", 0))
    ya = lax.ppermute(ya, "gy", swap_pairs("gy", 0))
    return [xa, xb, ya, yb, zz]


def gather_rows(rows):
    rows = lax.all_to_all(rows.reshape(C, 1, C), AXES, 0, 0)
    return rows.reshape(C, C)


def body(heat, cond, projection, segment_map):
    proj = projection[0, 0, 0]
    segs = segment_map[0, 0, 0]
    scratch = [S_FIELD, S_PADDED, S_SQUARE, pltpu.SemaphoreType.DMA((2, PARTS))]
    outs = [FIELD, PADDED, BASES, FIELD] + FACES + sends_of(1, C)
    away = pl.BlockSpec(memory_space=pl.ANY)
    out = call(first_kernel, "first", outs, scratch, (heat, cond, proj, segs), 4, [away, away, VM, VM])
    weight, state, bases, heat = out[:4]
    own, sends = out[4:10], out[10:]
    supply = heat
    prev = []
    held = None
    for pair in range(2):
        first = pair == 0
        got = exchange(sends)
        outs = [PADDED] + FACES + ([LAYERS, LAYERS] if first else [])
        out = call(functools.partial(free_kernel, first), "free", outs, [S_PADDED, S_SQUARE], (state, weight, supply), 3)
        free, own_u = out[0], out[1:7]
        if first:
            wx, wy = out[7:]
        args = own + got + [bases] + prev + [weight, wx, wy] + own_u
        stacked = [jax.ShapeDtypeStruct((2 * f.shape[0], C), F32) for f in FACES]
        outs = FACES + stacked + sends_of(2, 0) + ([BASES] if first else [])
        out = call(functools.partial(second_kernel, first), "second", outs, [S_SQUARE], args, 2)
        lift_1, own_uv, sends = out[:6], out[6:12], out[12:17]
        if first:
            prev = [out[17]]
        got = exchange(sends)
        resp, sums = call(response_kernel, "response", [PADDED, ROW], [S_FIELD, S_PADDED, S_SQUARE, S_SQUARE], lift_1 + [weight], 3)
        args = own_uv + got + [bases] + prev + [weight, wx, wy, sums]
        out = call(third_kernel, "third", FACES + FACES + [SQUARE], [pltpu.VMEM((2, C, C), F32)], args, 2)
        lift_u, lift_v, rows = out[:6], out[6:12], out[12]
        totals = gather_rows(rows)
        if first:
            args = [totals, heat, weight, free, resp] + lift_1 + lift_u + lift_v
            out = call(fourth_kernel, "fourth", [FIELD, PADDED] + FACES + FACES + sends_of(1, 0), [S_PADDED, S_SQUARE, S_SQUARE], args, 5)
            supply, state, held, own, sends = out[0], out[1], out[2:8], out[8:14], out[14:]
    upper = lambda faces: [faces[1], faces[3], faces[5]]
    args = [totals, free, resp] + upper(held) + upper(lift_1) + upper(lift_u) + upper(lift_v)
    state, mx, my, mz = call(last_kernel, "last", [FIELD, FACE, FACE, SQUARE], [], args, 2)
    return state, mx[None, None, None], my[None, None, None], mz[None, None, None]


def solution(mesh):
    field = P("gz", "gx", "gy")
    in_specs = (field, field, P("gz", "gx", "gy", None, None, None), P("gz", "gx", "gy", None, None))
    face = P("gz", "gx", "gy", None, None)
    return jax.shard_map(body, mesh=mesh, in_specs=in_specs, out_specs=(field, face, face, face), check_vma=False)
```

time: 129 us -> 112 us (0.87)
  Pallas kernels: 44 us -> 33.2 us
  waiting for transfers between devices: 2.97 us -> 0.05 us
  blocking collectives: 41.4 us -> 38.6 us
    pallas_call x9 -> x11, Pallas kernels: 44 us -> 33.2 us  [call(): pl.pallas_call(kernel, out_shape=tuple(outs), in_specs=in_specs or [VM] *...]
    ppermute x4, waiting for transfers between devices: 2.93 us -> 0.01 us  [exchange(): yb = lax.ppermute(yb, 'gy', swap_pairs('gy', 1))]
    all_to_all x2, blocking collectives: 41.4 us -> 38.6 us  [gather_rows(): rows = lax.all_to_all(rows.reshape(C, 1, C), AXES, 0, 0)]
  transfers between devices with their start and end apart: 20 -> 20, of which waited for: 2 -> 0; matrix products, arithmetic and copies ran while one was open for 0% -> 0% of each run, Pallas kernels for 5% -> 14%
where the time goes in v1:
time: 112 us
  blocking collectives  38.6 us (34%)
  starting transfers between devices  34.1 us (30%)
  Pallas kernels  33.2 us (30%)
  local copies, waits for them, and re-layouts  4.79 us (4%)
    all_to_all x2, blocking collectives, gather_rows(): rows = lax.all_to_all(rows.reshape(C, 1, C), AXES, 0, 0)  38.6 us
    pallas_call x11, Pallas kernels, call(): pl.pallas_call(kernel, out_shape=tuple(outs), in_specs=in_specs or [VM] *...  33.2 us
    ppermute x4, starting transfers between devices, exchange(): yb = lax.ppermute(yb, 'gy', swap_pairs('gy', 1))  13.7 us
    ppermute x4, starting transfers between devices, exchange(): xa = lax.ppermute(xa, 'gx', swap_pairs('gx', 0))  8.32 us
    ppermute x4, starting transfers between devices, exchange(): zz = lax.ppermute(zz, 'gz', swap_pairs('gz', 0))  6.8 us
    unnamed x7, local copies, waits for them, and re-layouts  4.79 us
    ppermute x4, starting transfers between devices, exchange(): ya = lax.ppermute(ya, 'gy', swap_pairs('gy', 0))  2.66 us
    ppermute x4, starting transfers between devices, exchange(): xb = lax.ppermute(xb, 'gx', swap_pairs('gx', 1))  2.61 us
  transfers between devices with their start and end apart: 20, of which 0 were waited for; matrix products, arithmetic and copies ran while one was open for 0% of the time, Pallas kernels for 14%

profile of v1, /device:TPU:1, one launch (start us, length us, event | category | flops | bytes accessed | tf_op | source)
XLA Modules:
  0.0 111.6 jit_solution(14369261702645750638)
XLA Ops:
  0.6 0.7 copy.12
  1.3 1.6 %copy-done = f32[32,128,128]{2,1,0:T(8,128)S(1)} copy-done((f32[32,128,128]{2,1,0:T(8,128)S(1)}, f32[32,128,128]{2,1,0:T(8,128)}, u32[]{:S(2)}) %copy-start) | copy-done | bytes 2097176
  2.9 1.6 %copy-done.1 = f32[32,128,128]{2,1,0:T(8,128)S(1)} copy-done((f32[32,128,128]{2,1,0:T(8,128)S(1)}, f32[32,128,128]{2,1,0:T(8,128)}, u32[]{:S(2)}) %copy-start.1) | copy-done | bytes 2097176
  4.5 0.9 copy-done.2
  5.4 3.8 %first.1 = (f32[32,128,128]{2,1,0:T(8,128)S(1)}, f32[34,128,128]{2,1,0:T(8,128)S(1)}, f32[3,128,128]{2,1,0:T(8,128)S(1)}, f32[32,128,128]{2,1,0:T(8,128)S(1)}, f...) custom-call(f32[32,128,128]{2,1,0:T(8,128)S(1)} %copy-done, ...), custom_call_target="tpu_custom_call" | custom-call | flops 40000000 | bytes 1048576 | tf_op jit(solution)/shard_map/first/pallas_call | solution.py:467
  9.2 3.6 %collective-permute-start.4 = (f32[256,128]{1,0:T(8,128)S(1)}, f32[256,128]{1,0:T(8,128)S(1)}, u32[]{:S(2)}, u32[]{:S(2)}) collective-permute-start(f32[256,128]{1,0:T(8,128)S(1)} %get-tuple-element.124), channel_id=1, source_target_pairs={{0,1},{1,0},{2,3},{3,2},{4,5},{5,4},{6,7},{7,6},{8,9},{9,8},{10,11... | collective-permute-start | bytes 393224 | tf_op jit(solution)/shard_map/ppermute | solution.py:490
  12.8 1.3 %collective-permute-start = (f32[160,128]{1,0:T(8,128)S(1)}, f32[160,128]{1,0:T(8,128)S(1)}, u32[]{:S(2)}, u32[]{:S(2)}) collective-permute-start(f32[160,128]{1,0:T(8,128)S(1)} %get-tuple-element.120), channel_id=1, source_target_pairs={{0,32},{32,0},{64,96},{96,64},{1,33},{33,1},{65,97},{97,65},{2,34}... | collective-permute-start | bytes 245768 | tf_op jit(solution)/shard_map/ppermute | solution.py:493
  14.1 0.7 collective-permute-start.1
  14.8 1.3 %collective-permute-start.2 = (f32[160,128]{1,0:T(8,128)S(1)}, f32[160,128]{1,0:T(8,128)S(1)}, u32[]{:S(2)}, u32[]{:S(2)}) collective-permute-start(f32[160,128]{1,0:T(8,128)S(1)} %get-tuple-element.122), channel_id=1, source_target_pairs={{0,2},{2,0},{4,6},{6,4},{8,10},{10,8},{12,14},{14,12},{16,18},{18,... | collective-permute-start | bytes 245768 | tf_op jit(solution)/shard_map/ppermute | solution.py:494
  16.1 3.4 %collective-permute-start.3 = (f32[160,128]{1,0:T(8,128)S(1)}, f32[160,128]{1,0:T(8,128)S(1)}, u32[]{:S(2)}, u32[]{:S(2)}) collective-permute-start(f32[160,128]{1,0:T(8,128)S(1)} %get-tuple-element.123), channel_id=1, source_target_pairs={{2,4},{4,2},{6,8},{8,6},{10,12},{12,10},{14,16},{16,14},{18,20},{2... | collective-permute-start | bytes 245768 | tf_op jit(solution)/shard_map/ppermute | solution.py:491
  19.6 5.1 %free.2 = (f32[34,128,128]{2,1,0:T(8,128)S(1)}, f32[32,128]{1,0:T(8,128)S(1)}, f32[32,128]{1,0:T(8,128)S(1)}, f32[32,128]{1,0:T(8,128)S(1)}, f32[32,128]{1,0:T(8...) custom-call(f32[34,128,128]{2,1,0:T(8,128)S(1)} %get-tuple-element.1, ...), custom_call_target="tpu_custom_call" | custom-call | flops 30000000 | bytes 1048576 | tf_op jit(solution)/shard_map/free/pallas_call | solution.py:467
  24.7 1.4 %second.2 = (f32[32,128]{1,0:T(8,128)S(1)}, f32[32,128]{1,0:T(8,128)S(1)}, f32[32,128]{1,0:T(8,128)S(1)}, f32[32,128]{1,0:T(8,128)S(1)}, f32[128,128]{1,0:T(8,12...) custom-call(f32[32,128]{1,0:T(8,128)S(1)} %get-tuple-element.114.ref, ...), custom_call_target="tpu_custom_call" | custom-call | flops 20000000 | bytes 1048576 | tf_op jit(solution)/shard_map/second/pallas_call | solution.py:467
  26.4 3.8 %collective-permute-start.5 = (f32[64,128]{1,0:T(8,128)S(1)}, f32[64,128]{1,0:T(8,128)S(1)}, u32[]{:S(2)}, u32[]{:S(2)}) collective-permute-start(f32[64,128]{1,0:T(8,128)S(1)} %get-tuple-element.143), channel_id=1, source_target_pairs={{0,32},{32,0},{64,96},{96,64},{1,33},{33,1},{65,97},{97,65},{2,34}... | collective-permute-start | bytes 98312 | tf_op jit(solution)/shard_map/ppermute | solution.py:493
  30.3 0.7 collective-permute-start.6
  31.0 3.9 %collective-permute-start.8 = (f32[64,128]{1,0:T(8,128)S(1)}, f32[64,128]{1,0:T(8,128)S(1)}, u32[]{:S(2)}, u32[]{:S(2)}) collective-permute-start(f32[64,128]{1,0:T(8,128)S(1)} %get-tuple-element.146), channel_id=1, source_target_pairs={{2,4},{4,2},{6,8},{8,6},{10,12},{12,10},{14,16},{16,14},{18,20},{2... | collective-permute-start | bytes 98312 | tf_op jit(solution)/shard_map/ppermute | solution.py:491
  34.9 3.0 %response.2 = (f32[34,128,128]{2,1,0:T(8,128)S(1)}, f32[1,128]{1,0:T(1,128)S(1)}) custom-call(f32[32,128]{1,0:T(8,128)S(1)} %get-tuple-element.149.refs_0_.refs_5_, f32[32,128]{1,0:T(8,128)S(1)} %get-tuple-element.150.refs_1_.refs_6_, f32[32,128]{1,0:T(8,128)S(1)} %get-tuple-element.151.refs_2_.refs_7_, f32[32,128]{1,0:T(8,128)S(1)} %get-tuple-element.152.refs_3_.refs_8_, ...), custom_call_target="tpu_custom_call" | custom-call | flops 30000000 | bytes 1048576 | tf_op jit(solution)/shard_map/response/pallas_call | solution.py:467
  38.0 1.5 %third.2 = (f32[32,128]{1,0:T(8,128)S(1)}, f32[32,128]{1,0:T(8,128)S(1)}, f32[32,128]{1,0:T(8,128)S(1)}, f32[32,128]{1,0:T(8,128)S(1)}, f32[128,128]{1,0:T(8,128...) custom-call(f32[64,128]{1,0:T(8,128)S(1)} %get-tuple-element.137.ref, ...), custom_call_target="tpu_custom_call" | custom-call | flops 20000000 | bytes 1048576 | tf_op jit(solution)/shard_map/third/pallas_call | solution.py:467
  39.5 21.3 %all_to_all.10 = f32[128,1,128]{2,1,0:T(1,128)S(1)} all-to-all(f32[128,1,128]{2,1,0:T(1,128)S(1)} %bitcast.19), channel_id=1, replica_groups=mesh['gx'=4,'gy'=16,'gz'=2] {'gx','gy','gz'}, dimensions={0} | all-to-all | bytes 131072 | tf_op jit(solution)/shard_map/all_to_all | solution.py:499
  60.8 6.0 %fourth.1 = (f32[32,128,128]{2,1,0:T(8,128)S(1)}, f32[34,128,128]{2,1,0:T(8,128)S(1)}, f32[32,128]{1,0:T(8,128)}, f32[32,128]{1,0:T(8,128)S(1)}, f32[32,128]{1,0...) custom-call(f32[128,128]{1,0:T(8,128)S(1)} %bitcast.15, ...), custom_call_target="tpu_custom_call" | custom-call | flops 50000000 | bytes 1048576 | tf_op jit(solution)/shard_map/fourth/pallas_call | solution.py:467
  66.8 1.1 collective-permute-start.14
  68.9 1.2 %collective-permute-start.12 = (f32[32,128]{1,0:T(8,128)S(1)}, f32[32,128]{1,0:T(8,128)S(1)}, u32[]{:S(2)}, u32[]{:S(2)}) collective-permute-start(f32[32,128]{1,0:T(8,128)S(1)} %get-tuple-element.179), channel_id=1, source_target_pairs={{0,2},{2,0},{4,6},{6,4},{8,10},{10,8},{12,14},{14,12},{16,18},{18,... | collective-permute-start | bytes 49160 | tf_op jit(solution)/shard_map/ppermute | solution.py:494
  70.1 2.4 %collective-permute-start.13 = (f32[32,128]{1,0:T(8,128)S(1)}, f32[32,128]{1,0:T(8,128)S(1)}, u32[]{:S(2)}, u32[]{:S(2)}) collective-permute-start(f32[32,128]{1,0:T(8,128)S(1)} %get-tuple-element.180), channel_id=1, source_target_pairs={{2,4},{4,2},{6,8},{8,6},{10,12},{12,10},{14,16},{16,14},{18,20},{2... | collective-permute-start | bytes 49160 | tf_op jit(solution)/shard_map/ppermute | solution.py:491
  72.4 4.2 %free.3 = (f32[34,128,128]{2,1,0:T(8,128)S(1)}, f32[32,128]{1,0:T(8,128)S(1)}, f32[32,128]{1,0:T(8,128)S(1)}, f32[32,128]{1,0:T(8,128)S(1)}, f32[32,128]{1,0:T(8...) custom-call(f32[34,128,128]{2,1,0:T(8,128)S(1)} %get-tuple-element.182.state, ...), custom_call_target="tpu_custom_call" | custom-call | flops 30000000 | bytes 1048576 | tf_op jit(solution)/shard_map/free/pallas_call | solution.py:467
  76.7 1.4 %second.3 = (f32[32,128]{1,0:T(8,128)S(1)}, f32[32,128]{1,0:T(8,128)S(1)}, f32[32,128]{1,0:T(8,128)S(1)}, f32[32,128]{1,0:T(8,128)S(1)}, f32[128,128]{1,0:T(8,12...) custom-call(f32[32,128]{1,0:T(8,128)S(1)} %get-tuple-element.171.ref, ...), custom_call_target="tpu_custom_call" | custom-call | flops 20000000 | bytes 1048576 | tf_op jit(solution)/shard_map/second/pallas_call | solution.py:467
  78.1 1.8 %collective-permute-start.19 = (f32[256,128]{1,0:T(8,128)S(1)}, f32[256,128]{1,0:T(8,128)S(1)}, u32[]{:S(2)}, u32[]{:S(2)}) collective-permute-start(f32[256,128]{1,0:T(8,128)S(1)} %get-tuple-element.200), channel_id=1, source_target_pairs={{0,1},{1,0},{2,3},{3,2},{4,5},{5,4},{6,7},{7,6},{8,9},{9,8},{10,11... | collective-permute-start | bytes 393224 | tf_op jit(solution)/shard_map/ppermute | solution.py:490
  79.9 2.9 %collective-permute-start.15 = (f32[64,128]{1,0:T(8,128)S(1)}, f32[64,128]{1,0:T(8,128)S(1)}, u32[]{:S(2)}, u32[]{:S(2)}) collective-permute-start(f32[64,128]{1,0:T(8,128)S(1)} %get-tuple-element.196), channel_id=1, source_target_pairs={{0,32},{32,0},{64,96},{96,64},{1,33},{33,1},{65,97},{97,65},{2,34}... | collective-permute-start | bytes 98312 | tf_op jit(solution)/shard_map/ppermute | solution.py:493
  82.8 0.7 collective-permute-start.16
  83.5 3.9 %collective-permute-start.18 = (f32[64,128]{1,0:T(8,128)S(1)}, f32[64,128]{1,0:T(8,128)S(1)}, u32[]{:S(2)}, u32[]{:S(2)}) collective-permute-start(f32[64,128]{1,0:T(8,128)S(1)} %get-tuple-element.199), channel_id=1, source_target_pairs={{2,4},{4,2},{6,8},{8,6},{10,12},{12,10},{14,16},{16,14},{18,20},{2... | collective-permute-start | bytes 98312 | tf_op jit(solution)/shard_map/ppermute | solution.py:491
  87.5 3.0 %response.3 = (f32[34,128,128]{2,1,0:T(8,128)S(1)}, f32[1,128]{1,0:T(1,128)S(1)}) custom-call(f32[32,128]{1,0:T(8,128)S(1)} %get-tuple-element.201.refs_0_, f32[32,128]{1,0:T(8,128)S(1)} %get-tuple-element.202.refs_1_.refs_6_, f32[32,128]{1,0:T(8,128)S(1)} %get-tuple-element.203.refs_2_, f32[32,128]{1,0:T(8,128)S(1)} %get-tuple-element.204.refs_3_.refs_7_, ...), custom_call_target="tpu_custom_call" | custom-call | flops 30000000 | bytes 1048576 | tf_op jit(solution)/shard_map/response/pallas_call | solution.py:467
  90.5 2.0 %third.3 = (f32[32,128]{1,0:T(8,128)}, f32[32,128]{1,0:T(8,128)S(1)}, f32[32,128]{1,0:T(8,128)}, f32[32,128]{1,0:T(8,128)S(1)}, f32[128,128]{1,0:T(8,128)}, /*in...) custom-call(f32[64,128]{1,0:T(8,128)S(1)} %get-tuple-element.190.ref, ...), custom_call_target="tpu_custom_call" | custom-call | flops 20000000 | bytes 1048576 | tf_op jit(solution)/shard_map/third/pallas_call | solution.py:467
  92.6 17.3 %all_to_all.11 = f32[128,1,128]{2,1,0:T(1,128)S(1)} all-to-all(f32[128,1,128]{2,1,0:T(1,128)S(1)} %bitcast.18), channel_id=1, replica_groups=mesh['gx'=4,'gy'=16,'gz'=2] {'gx','gy','gz'}, dimensions={0} | all-to-all | bytes 131072 | tf_op jit(solution)/shard_map/all_to_all | solution.py:499
  109.9 1.7 %last.1 = (f32[32,128,128]{2,1,0:T(8,128)}, f32[32,128]{1,0:T(8,128)}, f32[32,128]{1,0:T(8,128)}, f32[128,128]{1,0:T(8,128)}) custom-call(f32[128,128]{1,0:T(8,128)S(1)} %bitcast.16, f32[34,128,128]{2,1,0:T(8,128)S(1)} %get-tuple-element.209.refs_1_, f32[34,128,128]{2,1,0:T(8,128)S(1)} %get-tuple-element.210.refs_2_, ...), custom_call_target="tpu_custom_call" | custom-call | flops 20000000 | bytes 1048576 | tf_op jit(solution)/shard_map/last/pallas_call | solution.py:467
  (28 shorter events, 1.5 us)
Async XLA Ops:
  1.3 1.6 %copy-start = (f32[32,128,128]{2,1,0:T(8,128)S(1)}, f32[32,128,128]{2,1,0:T(8,128)}, u32[]{:S(2)}) copy-start(f32[32,128,128]{2,1,0:T(8,128)} %heat_in.1) | copy-start | bytes 6291460
  2.9 1.6 %copy-start.1 = (f32[32,128,128]{2,1,0:T(8,128)S(1)}, f32[32,128,128]{2,1,0:T(8,128)}, u32[]{:S(2)}) copy-start(f32[32,128,128]{2,1,0:T(8,128)} %cond_in.1) | copy-start | bytes 6291460
  4.5 0.9 copy-start.2
  9.2 15.5 %collective-permute-start.4 = (f32[256,128]{1,0:T(8,128)S(1)}, f32[256,128]{1,0:T(8,128)S(1)}, u32[]{:S(2)}, u32[]{:S(2)}) collective-permute-start(f32[256,128]{1,0:T(8,128)S(1)} %get-tuple-element.124), channel_id=1, source_target_pairs={{0,1},{1,0},{2,3},{3,2},{4,5},{5,4},{6,7},{7,6},{8,9},{9,8},{10,11... | collective-permute-start | bytes 393224 | tf_op jit(solution)/shard_map/ppermute | solution.py:490
  12.8 11.8 %collective-permute-start = (f32[160,128]{1,0:T(8,128)S(1)}, f32[160,128]{1,0:T(8,128)S(1)}, u32[]{:S(2)}, u32[]{:S(2)}) collective-permute-start(f32[160,128]{1,0:T(8,128)S(1)} %get-tuple-element.120), channel_id=1, source_target_pairs={{0,32},{32,0},{64,96},{96,64},{1,33},{33,1},{65,97},{97,65},{2,34}... | collective-permute-start | bytes 245768 | tf_op jit(solution)/shard_map/ppermute | solution.py:493
  14.1 10.5 %collective-permute-start.1 = (f32[160,128]{1,0:T(8,128)S(1)}, f32[160,128]{1,0:T(8,128)S(1)}, u32[]{:S(2)}, u32[]{:S(2)}) collective-permute-start(f32[160,128]{1,0:T(8,128)S(1)} %get-tuple-element.121), channel_id=1, source_target_pairs={{32,64},{64,32},{33,65},{65,33},{34,66},{66,34},{35,67},{67,35},{3... | collective-permute-start | bytes 245768 | tf_op jit(solution)/shard_map/ppermute | solution.py:492
  14.8 9.9 %collective-permute-start.2 = (f32[160,128]{1,0:T(8,128)S(1)}, f32[160,128]{1,0:T(8,128)S(1)}, u32[]{:S(2)}, u32[]{:S(2)}) collective-permute-start(f32[160,128]{1,0:T(8,128)S(1)} %get-tuple-element.122), channel_id=1, source_target_pairs={{0,2},{2,0},{4,6},{6,4},{8,10},{10,8},{12,14},{14,12},{16,18},{18,... | collective-permute-start | bytes 245768 | tf_op jit(solution)/shard_map/ppermute | solution.py:494
  16.1 8.5 %collective-permute-start.3 = (f32[160,128]{1,0:T(8,128)S(1)}, f32[160,128]{1,0:T(8,128)S(1)}, u32[]{:S(2)}, u32[]{:S(2)}) collective-permute-start(f32[160,128]{1,0:T(8,128)S(1)} %get-tuple-element.123), channel_id=1, source_target_pairs={{2,4},{4,2},{6,8},{8,6},{10,12},{12,10},{14,16},{16,14},{18,20},{2... | collective-permute-start | bytes 245768 | tf_op jit(solution)/shard_map/ppermute | solution.py:491
  26.1 11.9 %collective-permute-start.9 = (f32[256,128]{1,0:T(8,128)S(1)}, f32[256,128]{1,0:T(8,128)S(1)}, u32[]{:S(2)}, u32[]{:S(2)}) collective-permute-start(f32[256,128]{1,0:T(8,128)S(1)} %get-tuple-element.147), channel_id=1, source_target_pairs={{0,1},{1,0},{2,3},{3,2},{4,5},{5,4},{6,7},{7,6},{8,9},{9,8},{10,11... | collective-permute-start | bytes 393224 | tf_op jit(solution)/shard_map/ppermute | solution.py:490
  26.4 11.5 %collective-permute-start.5 = (f32[64,128]{1,0:T(8,128)S(1)}, f32[64,128]{1,0:T(8,128)S(1)}, u32[]{:S(2)}, u32[]{:S(2)}) collective-permute-start(f32[64,128]{1,0:T(8,128)S(1)} %get-tuple-element.143), channel_id=1, source_target_pairs={{0,32},{32,0},{64,96},{96,64},{1,33},{33,1},{65,97},{97,65},{2,34}... | collective-permute-start | bytes 98312 | tf_op jit(solution)/shard_map/ppermute | solution.py:493
  30.3 7.7 %collective-permute-start.6 = (f32[64,128]{1,0:T(8,128)S(1)}, f32[64,128]{1,0:T(8,128)S(1)}, u32[]{:S(2)}, u32[]{:S(2)}) collective-permute-start(f32[64,128]{1,0:T(8,128)S(1)} %get-tuple-element.144), channel_id=1, source_target_pairs={{32,64},{64,32},{33,65},{65,33},{34,66},{66,34},{35,67},{67,35},{3... | collective-permute-start | bytes 98312 | tf_op jit(solution)/shard_map/ppermute | solution.py:492
  30.9 7.0 %collective-permute-start.7 = (f32[64,128]{1,0:T(8,128)S(1)}, f32[64,128]{1,0:T(8,128)S(1)}, u32[]{:S(2)}, u32[]{:S(2)}) collective-permute-start(f32[64,128]{1,0:T(8,128)S(1)} %get-tuple-element.145), channel_id=1, source_target_pairs={{0,2},{2,0},{4,6},{6,4},{8,10},{10,8},{12,14},{14,12},{16,18},{18,... | collective-permute-start | bytes 98312 | tf_op jit(solution)/shard_map/ppermute | solution.py:494
  31.0 7.0 %collective-permute-start.8 = (f32[64,128]{1,0:T(8,128)S(1)}, f32[64,128]{1,0:T(8,128)S(1)}, u32[]{:S(2)}, u32[]{:S(2)}) collective-permute-start(f32[64,128]{1,0:T(8,128)S(1)} %get-tuple-element.146), channel_id=1, source_target_pairs={{2,4},{4,2},{6,8},{8,6},{10,12},{12,10},{14,16},{16,14},{18,20},{2... | collective-permute-start | bytes 98312 | tf_op jit(solution)/shard_map/ppermute | solution.py:491
  66.8 9.9 %collective-permute-start.14 = (f32[128,128]{1,0:T(8,128)S(1)}, f32[128,128]{1,0:T(8,128)S(1)}, u32[]{:S(2)}, u32[]{:S(2)}) collective-permute-start(f32[128,128]{1,0:T(8,128)S(1)} %get-tuple-element.181), channel_id=1, source_target_pairs={{0,1},{1,0},{2,3},{3,2},{4,5},{5,4},{6,7},{7,6},{8,9},{9,8},{10,11... | collective-permute-start | bytes 196616 | tf_op jit(solution)/shard_map/ppermute | solution.py:490
  67.9 8.8 %collective-permute-start.10 = (f32[32,128]{1,0:T(8,128)S(1)}, f32[32,128]{1,0:T(8,128)S(1)}, u32[]{:S(2)}, u32[]{:S(2)}) collective-permute-start(f32[32,128]{1,0:T(8,128)S(1)} %get-tuple-element.177), channel_id=1, source_target_pairs={{0,32},{32,0},{64,96},{96,64},{1,33},{33,1},{65,97},{97,65},{2,34}... | collective-permute-start | bytes 49160 | tf_op jit(solution)/shard_map/ppermute | solution.py:493
  68.2 8.4 %collective-permute-start.11 = (f32[32,128]{1,0:T(8,128)S(1)}, f32[32,128]{1,0:T(8,128)S(1)}, u32[]{:S(2)}, u32[]{:S(2)}) collective-permute-start(f32[32,128]{1,0:T(8,128)S(1)} %get-tuple-element.178), channel_id=1, source_target_pairs={{32,64},{64,32},{33,65},{65,33},{34,66},{66,34},{35,67},{67,35},{3... | collective-permute-start | bytes 49160 | tf_op jit(solution)/shard_map/ppermute | solution.py:492
  68.9 7.8 %collective-permute-start.12 = (f32[32,128]{1,0:T(8,128)S(1)}, f32[32,128]{1,0:T(8,128)S(1)}, u32[]{:S(2)}, u32[]{:S(2)}) collective-permute-start(f32[32,128]{1,0:T(8,128)S(1)} %get-tuple-element.179), channel_id=1, source_target_pairs={{0,2},{2,0},{4,6},{6,4},{8,10},{10,8},{12,14},{14,12},{16,18},{18,... | collective-permute-start | bytes 49160 | tf_op jit(solution)/shard_map/ppermute | solution.py:494
  70.1 6.6 %collective-permute-start.13 = (f32[32,128]{1,0:T(8,128)S(1)}, f32[32,128]{1,0:T(8,128)S(1)}, u32[]{:S(2)}, u32[]{:S(2)}) collective-permute-start(f32[32,128]{1,0:T(8,128)S(1)} %get-tuple-element.180), channel_id=1, source_target_pairs={{2,4},{4,2},{6,8},{8,6},{10,12},{12,10},{14,16},{16,14},{18,20},{2... | collective-permute-start | bytes 49160 | tf_op jit(solution)/shard_map/ppermute | solution.py:491
  78.1 12.4 %collective-permute-start.19 = (f32[256,128]{1,0:T(8,128)S(1)}, f32[256,128]{1,0:T(8,128)S(1)}, u32[]{:S(2)}, u32[]{:S(2)}) collective-permute-start(f32[256,128]{1,0:T(8,128)S(1)} %get-tuple-element.200), channel_id=1, source_target_pairs={{0,1},{1,0},{2,3},{3,2},{4,5},{5,4},{6,7},{7,6},{8,9},{9,8},{10,11... | collective-permute-start | bytes 393224 | tf_op jit(solution)/shard_map/ppermute | solution.py:490
  79.9 10.6 %collective-permute-start.15 = (f32[64,128]{1,0:T(8,128)S(1)}, f32[64,128]{1,0:T(8,128)S(1)}, u32[]{:S(2)}, u32[]{:S(2)}) collective-permute-start(f32[64,128]{1,0:T(8,128)S(1)} %get-tuple-element.196), channel_id=1, source_target_pairs={{0,32},{32,0},{64,96},{96,64},{1,33},{33,1},{65,97},{97,65},{2,34}... | collective-permute-start | bytes 98312 | tf_op jit(solution)/shard_map/ppermute | solution.py:493
  82.8 7.7 %collective-permute-start.16 = (f32[64,128]{1,0:T(8,128)S(1)}, f32[64,128]{1,0:T(8,128)S(1)}, u32[]{:S(2)}, u32[]{:S(2)}) collective-permute-start(f32[64,128]{1,0:T(8,128)S(1)} %get-tuple-element.197), channel_id=1, source_target_pairs={{32,64},{64,32},{33,65},{65,33},{34,66},{66,34},{35,67},{67,35},{3... | collective-permute-start | bytes 98312 | tf_op jit(solution)/shard_map/ppermute | solution.py:492
  83.4 7.1 %collective-permute-start.17 = (f32[64,128]{1,0:T(8,128)S(1)}, f32[64,128]{1,0:T(8,128)S(1)}, u32[]{:S(2)}, u32[]{:S(2)}) collective-permute-start(f32[64,128]{1,0:T(8,128)S(1)} %get-tuple-element.198), channel_id=1, source_target_pairs={{0,2},{2,0},{4,6},{6,4},{8,10},{10,8},{12,14},{14,12},{16,18},{18,... | collective-permute-start | bytes 98312 | tf_op jit(solution)/shard_map/ppermute | solution.py:494
  83.5 7.0 %collective-permute-start.18 = (f32[64,128]{1,0:T(8,128)S(1)}, f32[64,128]{1,0:T(8,128)S(1)}, u32[]{:S(2)}, u32[]{:S(2)}) collective-permute-start(f32[64,128]{1,0:T(8,128)S(1)} %get-tuple-element.199), channel_id=1, source_target_pairs={{2,4},{4,2},{6,8},{8,6},{10,12},{12,10},{14,16},{16,14},{18,20},{2... | collective-permute-start | bytes 98312 | tf_op jit(solution)/shard_map/ppermute | solution.py:491

commit v2 on v1

--- a/solution.py
+++ b/solution.py
@@ -17,19 +17,43 @@
 UNROLL = 4
 WIDE = 16
 PARTS = 4
+BLOCK = 16
+DEPTH = 8
 KEPT = 1.0 - DAMPING_WEIGHT
 
 VM = pl.BlockSpec(memory_space=pltpu.MemorySpace.VMEM)
-
-
-def dot(a, b):
-    return jnp.dot(a, b, precision=HIGH, preferred_element_type=F32)
+AWAY = pl.BlockSpec(memory_space=pltpu.MemorySpace.HBM)
+BF16 = jnp.bfloat16
+PAD = 8
 
 
 def dot_t(a, b):
     return lax.dot_general(a, b, (((1,), (1,)), ((), ())), precision=HIGH, preferred_element_type=F32)
 
 
+def parts_of(a):
+    first = a.astype(BF16)
+    rest = a - first.astype(F32)
+    second = rest.astype(BF16)
+    third = (rest - second.astype(F32)).astype(BF16)
+    return first, second, third
+
+
+def dot(a, parts, d):
+    n = a.shape[0]
+    mul = functools.partial(jnp.dot, preferred_element_type=F32)
+    a1, a2, a3 = parts_of(a)
+    r = mul(jnp.concatenate([a1, a2, a3], axis=0), parts[3 * d])
+    s = mul(jnp.concatenate([a1, a2], axis=0), parts[3 * d + 1])
+    t = mul(a1, parts[3 * d + 2])
+    return r[:n] + (r[n : 2 * n] + s[:n] + (r[2 * n :] + s[n:] + t))
+
+
+def store_parts(ref, d, a):
+    for i, p in enumerate(parts_of(a)):
+        ref[3 * d + i] = p
+
+
 def lane_of(shape):
     return lax.broadcasted_iota(jnp.int32, shape, len(shape) - 1)
 
@@ -38,14 +62,15 @@
     return lax.broadcasted_iota(jnp.int32, shape, len(shape) - 2)
 
 
+INNER = slice(PAD, PAD + C)
+
+
 def zero_ends(ref):
-    ref[0] = jnp.zeros((C, C), F32)
-    ref[CZ + 1] = jnp.zeros((C, C), F32)
-
-
-def neighbours(src, z):
-    centre = src[z + 1]
-    return centre, src[z] + src[z + 2] + in_plane(centre)
+    ref[0] = jnp.zeros((C + 2 * PAD, C), F32)
+    ref[CZ + 1] = jnp.zeros((C + 2 * PAD, C), F32)
+    for z in range(1, CZ + 1):
+        ref[z, 0:PAD, :] = jnp.zeros((PAD, C), F32)
+        ref[z, PAD + C :, :] = jnp.zeros((PAD, C), F32)
 
 
 def in_plane(centre):
@@ -59,24 +84,36 @@
 
 
 def sweep(src, dst, weight, supply):
-    def plane(z, carry):
-        centre, near = neighbours(src, z)
-        dst[z + 1] = KEPT * centre + weight[z] * (supply[z] + near)
+    lanes = lane_of((BLOCK, C))
+    low = lanes == 0
+    high = lanes == C - 1
+
+    def planes(i, carry):
+        z = i * DEPTH
+        for x in range(0, C, BLOCK):
+            r = PAD + x
+            column = [src[z + j, r : r + BLOCK, :] for j in range(DEPTH + 2)]
+            for j in range(DEPTH):
+                centre = column[j + 1]
+                near = column[j] + column[j + 2]
+                near = near + src[z + j + 1, r - 1 : r - 1 + BLOCK, :] + src[z + j + 1, r + 1 : r + 1 + BLOCK, :]
+                near = near + jnp.where(low, 0.0, pltpu.roll(centre, 1, 1)) + jnp.where(high, 0.0, pltpu.roll(centre, C - 1, 1))
+                dst[z + j + 1, r : r + BLOCK, :] = KEPT * centre + weight[z + j, x : x + BLOCK, :] * (supply[z + j, x : x + BLOCK, :] + near)
         return carry
 
-    lax.fori_loop(0, CZ, plane, 0, unroll=UNROLL)
+    lax.fori_loop(0, CZ // DEPTH, planes, 0)
 
 
 def row_layer(src, base, at, out):
     for z in range(CZ):
-        out[z : z + 1, :] = src[z + base, at : at + 1, :]
+        out[z : z + 1, :] = src[z + base, PAD * base + at : PAD * base + at + 1, :]
 
 
 def column_layers(src, base, turn):
     group = lane_of((C, C)) // 4
 
     def plane(z, packed):
-        return jnp.where(group == z, pltpu.roll(src[z + base], 4 * z + 2, 1), packed)
+        return jnp.where(group == z, pltpu.roll(src[z + base, PAD * base : PAD * base + C, :], 4 * z + 2, 1), packed)
 
     packed = lax.fori_loop(0, CZ, plane, jnp.zeros((C, C), F32), unroll=WIDE)
     turn[...] = packed.T
@@ -99,16 +136,7 @@
     return jnp.where(edge, pltpu.roll(packed, C - 2 - 4 * z, 1), 0.0)
 
 
-def lift_dense(dst, cols, faces, base, sign):
-    def plane(z, carry):
-        col = column_plane(cols[...], z)
-        if base is None:
-            dst[z] = sign * col
-        else:
-            dst[z] = base[z] + sign * col
-        return carry
-
-    lax.fori_loop(0, CZ, plane, 0, unroll=WIDE)
+def add_rows(dst, faces, sign):
     for z in range(CZ):
         dst[z, 0:1, :] = dst[z, 0:1, :] + sign * faces[0][z : z + 1, :]
         dst[z, C - 1 : C, :] = dst[z, C - 1 : C, :] + sign * faces[1][z : z + 1, :]
@@ -218,14 +246,17 @@
     column_layers(src, 1, turn)
     own[2][...] = turn[layer_rows(2), :]
     own[3][...] = turn[layer_rows(1), :]
-    own[4][...] = src[1]
-    own[5][...] = src[CZ]
-
-
-def first_kernel(heat_in, cond_in, proj, segs, weight, state, bases, heat, *refs):
+    own[4][...] = src[1, INNER, :]
+    own[5][...] = src[CZ, INNER, :]
+
+
+def first_kernel(heat_in, cond_in, proj_in, segs_in, weight, state, parts, heat, *refs):
     own = refs[:6]
     sends = refs[6:11]
-    cond, start, turn, sems = refs[11:]
+    cond, proj, segs, start, turn, sems, small = refs[11:]
+    tables = (pltpu.make_async_copy(proj_in, proj, small.at[0]), pltpu.make_async_copy(segs_in, segs, small.at[1]))
+    for c in tables:
+        c.start()
     part = CZ // PARTS
     copies = []
     for i in range(PARTS):
@@ -237,16 +268,23 @@
         for c in pair:
             c.start()
         copies.append(pair)
-    for d in range(3):
-        onehot = jnp.where(row_of((C, C)) == segs[d : d + 1, :], 1.0, 0.0).astype(F32)
-        bases[d] = dot_t(onehot, proj[d])
     zero_ends(start)
     zero_ends(state)
+    for c in tables:
+        c.wait()
+    for d in range(3):
+        onehot = jnp.where(row_of((C, C)) == segs[d : d + 1, :], 1.0, 0.0).astype(BF16)
+        base = sum(lax.dot_general(onehot, p, (((1,), (1,)), ((), ())), preferred_element_type=F32) for p in reversed(parts_of(proj[d])))
+        store_parts(parts, d, base)
+        for a in (sends[:2], sends[2:4])[d] if d < 2 else ():
+            a[CZ : CZ + C, :] = base
+        if d == 2:
+            sends[4][C : 2 * C, :] = base
 
     def plane(z, carry):
         w = DAMPING_WEIGHT / (6.0 + cond[z])
         weight[z] = w
-        start[z + 1] = w * heat[z]
+        start[z + 1, INNER, :] = w * heat[z]
         return carry
 
     for i, pair in enumerate(copies):
@@ -256,11 +294,6 @@
     sweep(start, state, weight, heat)
     own_faces(state, own, turn)
     pack_sends(sends, [f[...] for f in own], 0)
-    for a in sends[:2]:
-        a[CZ : CZ + C, :] = bases[0]
-    for a in sends[2:4]:
-        a[CZ : CZ + C, :] = bases[1]
-    sends[4][C : 2 * C, :] = bases[2]
 
 
 def free_kernel(first, state, weight, supply, *refs):
@@ -281,16 +314,16 @@
             wy[i] = turn[layer_rows(e), :]
 
 
-def jumps(own, got, bases, prev_bases, n, lifted):
+def jumps(own, got, bases, prev_bases, back_bases, n, lifted):
     xeven, yeven, zlow, more = places()
     xa, xb, ya, yb, zz = got
     for d, (even, a, b, rows) in enumerate(((xeven, xa, xb, n * CZ), (yeven, ya, yb, n * CZ), (zlow, zz, zz, n * C))):
         a = a[0:rows, :]
         b = b[0:rows, :]
-        up = own[2 * d + 1][...] - dot(pick(even, a, b), bases[d])
+        up = own[2 * d + 1][...] - dot(pick(even, a, b), bases, d)
         up = jnp.where(more[d], up, 0.0)
-        down = pick(even, b, a) - dot(own[2 * d][...], prev_bases[d])
-        back = -dot_t(down, prev_bases[d])
+        down = pick(even, b, a) - dot(own[2 * d][...], prev_bases, d)
+        back = -dot(down, back_bases, d)
         if d == 2:
             back = jnp.where(zlow, 0.0, back)
         size = rows // n
@@ -317,22 +350,22 @@
     own = take(6)
     got = take(5)
     (bases,) = take(1)
-    (prev,) = take(1) if not first else (None,)
+    prev, back = take(2) if not first else (None, None)
     weight, wx, wy = take(3)
     own_u = take(6)
     lifted = take(6)
     own_uv = take(6)
     sends = take(5)
     if first:
-        (prev,) = take(1)
+        prev, back = take(2)
     (turn,) = take(1)
     xeven, yeven, zlow, _ = places()
     if first:
         xa, xb, ya, yb, zz = got
-        prev[0] = pick(xeven, xb[CZ:, :], xa[CZ:, :])
-        prev[1] = pick(yeven, yb[CZ:, :], ya[CZ:, :])
-        prev[2] = zz[C:, :]
-    jumps(own, got, bases, prev, 1, [lifted])
+        for d, base in enumerate((pick(xeven, xb[CZ:, :], xa[CZ:, :]), pick(yeven, yb[CZ:, :], ya[CZ:, :]), zz[C:, :])):
+            store_parts(prev, d, base)
+            store_parts(back, d, base.T)
+    jumps(own, got, bases, prev, back, 1, [lifted])
     response = face_response(lift_layers(lifted, turn, True), layer_weights(weight, wx, wy))
     free = [f[...] for f in own_u]
     for o, u, v in zip(own_uv, free, response):
@@ -347,16 +380,22 @@
     lifted = refs[:6]
     weight, resp, sums, lift, mid, turn, cols = refs[6:]
     cols[...] = pack_columns(turn, lifted[2][...], lifted[3][...])
-    lift_dense(lift, cols, lifted, None, 1.0)
+
+    def plane(z, carry):
+        lift[z] = column_plane(cols[...], z)
+        return carry
+
+    lax.fori_loop(0, CZ, plane, 0, unroll=WIDE)
+    add_rows(lift, lifted, 1.0)
     zero_ends(mid)
     zero_ends(resp)
 
-    def plane(z, acc):
+    def scale(z, acc):
         once = weight[z] * lift[z]
-        mid[z + 1] = once
+        mid[z + 1, INNER, :] = once
         return acc + fold(once * lift[z])
 
-    acc = lax.fori_loop(0, CZ, plane, jnp.zeros((8, C), F32), unroll=UNROLL)
+    acc = lax.fori_loop(0, CZ, scale, jnp.zeros((8, C), F32), unroll=UNROLL)
     sweep(mid, resp, weight, lift)
     sums[...] = row_of_sums([square_sum(lifted, lifted), jnp.sum(acc) / DAMPING_WEIGHT])
 
@@ -366,12 +405,12 @@
     take = lambda n: [next(it) for _ in range(n)]
     own_uv = take(6)
     got = take(5)
-    bases, prev, weight, wx, wy, before = take(6)
+    bases, prev, back, weight, wx, wy, before = take(7)
     lift_u = take(6)
     lift_v = take(6)
     (rows,) = take(1)
     (turn,) = take(1)
-    jumps(own_uv, got, bases, prev, 2, [lift_u, lift_v])
+    jumps(own_uv, got, bases, prev, back, 2, [lift_u, lift_v])
     weights = layer_weights(weight, wx, wy)
     u = lift_layers(lift_u, turn.at[0], False)
     v = lift_layers(lift_v, turn.at[1], False)
@@ -408,15 +447,16 @@
     for i in range(6):
         held[i][...] = one * lift_1[i][...] + two * (lift_u[i][...] - one * lift_v[i][...])
     cols[...] = pack_columns(turn, held[2][...], held[3][...])
-    lift_dense(supply, cols, held, heat, -1.0)
     zero_ends(mid)
     zero_ends(state)
 
     def plane(z, carry):
-        state[z + 1] = free[z + 1] - one * resp[z + 1]
+        supply[z] = heat[z] - column_plane(cols[...], z)
+        state[z + 1, INNER, :] = free[z + 1, INNER, :] - one * resp[z + 1, INNER, :]
         return carry
 
-    lax.fori_loop(0, CZ, plane, 0, unroll=UNROLL)
+    lax.fori_loop(0, CZ, plane, 0, unroll=2 * UNROLL)
+    add_rows(supply, held, -1.0)
     sweep(state, mid, weight, supply)
     sweep(mid, state, weight, supply)
     own_faces(state, own, turn)
@@ -431,29 +471,38 @@
     lift_3 = take(3)
     lift_u = take(3)
     lift_v = take(3)
-    (state,) = take(1)
+    (out,) = take(1)
     outs = take(3)
+    state, sems = take(2)
     one, two = steps(totals)
 
     def plane(z, carry):
-        state[z] = free[z + 1] - one * resp[z + 1]
+        state[z] = free[z + 1, INNER, :] - one * resp[z + 1, INNER, :]
         return carry
 
-    lax.fori_loop(0, CZ, plane, 0, unroll=UNROLL)
+    part = CZ // PARTS
+    copies = []
+    for i in range(PARTS):
+        lax.fori_loop(i * part, (i + 1) * part, plane, 0, unroll=UNROLL)
+        s = pl.ds(i * part, part)
+        copies.append(pltpu.make_async_copy(state.at[s], out.at[s], sems.at[i]))
+        copies[-1].start()
     for i in range(3):
         outs[i][...] = held[i][...] + one * lift_3[i][...] + two * (lift_u[i][...] - one * lift_v[i][...])
+    for c in copies:
+        c.wait()
 
 
 FIELD = jax.ShapeDtypeStruct((CZ, C, C), F32)
-PADDED = jax.ShapeDtypeStruct((CZ + 2, C, C), F32)
+PADDED = jax.ShapeDtypeStruct((CZ + 2, C + 2 * PAD, C), F32)
 FACE = jax.ShapeDtypeStruct((CZ, C), F32)
 SQUARE = jax.ShapeDtypeStruct((C, C), F32)
 FACES = [FACE] * 4 + [SQUARE] * 2
-BASES = jax.ShapeDtypeStruct((3, C, C), F32)
 LAYERS = jax.ShapeDtypeStruct((4, CZ, C), F32)
 ROW = jax.ShapeDtypeStruct((1, C), F32)
 S_FIELD = pltpu.VMEM((CZ, C, C), F32)
-S_PADDED = pltpu.VMEM((CZ + 2, C, C), F32)
+S_PADDED = pltpu.VMEM((CZ + 2, C + 2 * PAD, C), F32)
+PIECES = jax.ShapeDtypeStruct((9, C, C), BF16)
 S_SQUARE = pltpu.VMEM((C, C), F32)
 
 
@@ -462,13 +511,13 @@
     return [small] * 4 + [jax.ShapeDtypeStruct((n * C + extra, C), F32)]
 
 
-def call(kernel, name, outs, scratch, args, us, in_specs=None):
+def call(kernel, name, outs, scratch, args, us, in_specs=None, out_specs=None):
     return list(
         pl.pallas_call(
             kernel,
             out_shape=tuple(outs),
             in_specs=in_specs or [VM] * len(args),
-            out_specs=tuple([VM] * len(outs)),
+            out_specs=tuple(out_specs or [VM] * len(outs)),
             scratch_shapes=scratch,
             name=name,
             compiler_params=pltpu.CompilerParams(vmem_limit_bytes=40 * 1024 * 1024),
@@ -503,10 +552,10 @@
 def body(heat, cond, projection, segment_map):
     proj = projection[0, 0, 0]
     segs = segment_map[0, 0, 0]
-    scratch = [S_FIELD, S_PADDED, S_SQUARE, pltpu.SemaphoreType.DMA((2, PARTS))]
-    outs = [FIELD, PADDED, BASES, FIELD] + FACES + sends_of(1, C)
-    away = pl.BlockSpec(memory_space=pl.ANY)
-    out = call(first_kernel, "first", outs, scratch, (heat, cond, proj, segs), 4, [away, away, VM, VM])
+    dma = pltpu.SemaphoreType.DMA
+    scratch = [S_FIELD, pltpu.VMEM(proj.shape, F32), pltpu.VMEM(segs.shape, jnp.int32), S_PADDED, S_SQUARE, dma((2, PARTS)), dma((2,))]
+    outs = [FIELD, PADDED, PIECES, FIELD] + FACES + sends_of(1, C)
+    out = call(first_kernel, "first", outs, scratch, (heat, cond, proj, segs), 4, [AWAY] * 4)
     weight, state, bases, heat = out[:4]
     own, sends = out[4:10], out[10:]
     supply = heat
@@ -522,11 +571,11 @@
             wx, wy = out[7:]
         args = own + got + [bases] + prev + [weight, wx, wy] + own_u
         stacked = [jax.ShapeDtypeStruct((2 * f.shape[0], C), F32) for f in FACES]
-        outs = FACES + stacked + sends_of(2, 0) + ([BASES] if first else [])
+        outs = FACES + stacked + sends_of(2, 0) + ([PIECES, PIECES] if first else [])
         out = call(functools.partial(second_kernel, first), "second", outs, [S_SQUARE], args, 2)
         lift_1, own_uv, sends = out[:6], out[6:12], out[12:17]
         if first:
-            prev = [out[17]]
+            prev = out[17:]
         got = exchange(sends)
         resp, sums = call(response_kernel, "response", [PADDED, ROW], [S_FIELD, S_PADDED, S_SQUARE, S_SQUARE], lift_1 + [weight], 3)
         args = own_uv + got + [bases] + prev + [weight, wx, wy, sums]
@@ -539,7 +588,7 @@
             supply, state, held, own, sends = out[0], out[1], out[2:8], out[8:14], out[14:]
     upper = lambda faces: [faces[1], faces[3], faces[5]]
     args = [totals, free, resp] + upper(held) + upper(lift_1) + upper(lift_u) + upper(lift_v)
-    state, mx, my, mz = call(last_kernel, "last", [FIELD, FACE, FACE, SQUARE], [], args, 2)
+    state, mx, my, mz = call(last_kernel, "last", [FIELD, FACE, FACE, SQUARE], [S_FIELD, dma((PARTS,))], args, 2, None, [AWAY, VM, VM, VM])
     return state, mx[None, None, None], my[None, None, None], mz[None, None, None]
 
 

time: 112 us -> 113 us (level)
  local copies, waits for them, and re-layouts: 4.79 us -> 6.26 us
    unnamed x7 -> x9, local copies, waits for them, and re-layouts: 4.79 us -> 6.26 us
  transfers between devices with their start and end apart: 20 -> 20, of which waited for: 0 -> 0; matrix products, arithmetic and copies ran while one was open for 0% -> 0% of each run, Pallas kernels for 14% -> 12%
where the time goes in v2:
time: 113 us
  blocking collectives  39 us (35%)
  starting transfers between devices  34.2 us (30%)
  Pallas kernels  32.2 us (28%)
  local copies, waits for them, and re-layouts  6.26 us (6%)
    all_to_all x2, blocking collectives, gather_rows(): rows = lax.all_to_all(rows.reshape(C, 1, C), AXES, 0, 0)  39 us
    pallas_call x11, Pallas kernels, call(): pl.pallas_call(kernel, out_shape=tuple(outs), in_specs=in_specs or [VM] *...  32.2 us
    ppermute x4, starting transfers between devices, exchange(): yb = lax.ppermute(yb, 'gy', swap_pairs('gy', 1))  13.7 us
    ppermute x4, starting transfers between devices, exchange(): xa = lax.ppermute(xa, 'gx', swap_pairs('gx', 0))  8.33 us
    ppermute x4, starting transfers between devices, exchange(): zz = lax.ppermute(zz, 'gz', swap_pairs('gz', 0))  6.98 us
    unnamed x9, local copies, waits for them, and re-layouts  6.26 us
    ppermute x4, starting transfers between devices, exchange(): ya = lax.ppermute(ya, 'gy', swap_pairs('gy', 0))  2.66 us
    ppermute x4, starting transfers between devices, exchange(): xb = lax.ppermute(xb, 'gx', swap_pairs('gx', 1))  2.61 us
  transfers between devices with their start and end apart: 20, of which 0 were waited for; matrix products, arithmetic and copies ran while one was open for 0% of the time, Pallas kernels for 12%

profile of v2, /device:TPU:1, one launch (start us, length us, event | category | flops | bytes accessed | tf_op | source)
XLA Modules:
  0.0 112.8 jit_solution(9317934773027476644)
XLA Ops:
  0.6 0.7 copy.12
  1.3 1.6 %copy-done.1 = f32[32,128,128]{2,1,0:T(8,128)S(1)} copy-done((f32[32,128,128]{2,1,0:T(8,128)S(1)}, f32[32,128,128]{2,1,0:T(8,128)}, u32[]{:S(2)}) %copy-start.1) | copy-done | bytes 2097176
  2.9 1.6 %copy-done.2 = f32[32,128,128]{2,1,0:T(8,128)S(1)} copy-done((f32[32,128,128]{2,1,0:T(8,128)S(1)}, f32[32,128,128]{2,1,0:T(8,128)}, u32[]{:S(2)}) %copy-start.2) | copy-done | bytes 2097176
  4.5 0.9 copy-done.3
  5.4 3.7 %first.1 = (f32[32,128,128]{2,1,0:T(8,128)S(1)}, f32[34,144,128]{2,1,0:T(8,128)S(1)}, bf16[9,128,128]{2,1,0:T(8,128)(2,1)S(1)}, f32[32,128,128]{2,1,0:T(8,128)S(...) custom-call(f32[32,128,128]{2,1,0:T(8,128)S(1)} %copy-done.1, ...), custom_call_target="tpu_custom_call" | custom-call | flops 40000000 | bytes 1048576 | tf_op jit(solution)/shard_map/first/pallas_call | solution.py:516
  9.1 3.6 %collective-permute-start.4 = (f32[256,128]{1,0:T(8,128)S(1)}, f32[256,128]{1,0:T(8,128)S(1)}, u32[]{:S(2)}, u32[]{:S(2)}) collective-permute-start(f32[256,128]{1,0:T(8,128)S(1)} %get-tuple-element.125), channel_id=1, source_target_pairs={{0,1},{1,0},{2,3},{3,2},{4,5},{5,4},{6,7},{7,6},{8,9},{9,8},{10,11... | collective-permute-start | bytes 393224 | tf_op jit(solution)/shard_map/ppermute | solution.py:539
  12.7 1.3 %collective-permute-start = (f32[160,128]{1,0:T(8,128)S(1)}, f32[160,128]{1,0:T(8,128)S(1)}, u32[]{:S(2)}, u32[]{:S(2)}) collective-permute-start(f32[160,128]{1,0:T(8,128)S(1)} %get-tuple-element.121), channel_id=1, source_target_pairs={{0,32},{32,0},{64,96},{96,64},{1,33},{33,1},{65,97},{97,65},{2,34}... | collective-permute-start | bytes 245768 | tf_op jit(solution)/shard_map/ppermute | solution.py:542
  14.0 0.7 collective-permute-start.1
  14.7 1.3 %collective-permute-start.2 = (f32[160,128]{1,0:T(8,128)S(1)}, f32[160,128]{1,0:T(8,128)S(1)}, u32[]{:S(2)}, u32[]{:S(2)}) collective-permute-start(f32[160,128]{1,0:T(8,128)S(1)} %get-tuple-element.123), channel_id=1, source_target_pairs={{0,2},{2,0},{4,6},{6,4},{8,10},{10,8},{12,14},{14,12},{16,18},{18,... | collective-permute-start | bytes 245768 | tf_op jit(solution)/shard_map/ppermute | solution.py:543
  16.0 3.4 %collective-permute-start.3 = (f32[160,128]{1,0:T(8,128)S(1)}, f32[160,128]{1,0:T(8,128)S(1)}, u32[]{:S(2)}, u32[]{:S(2)}) collective-permute-start(f32[160,128]{1,0:T(8,128)S(1)} %get-tuple-element.124), channel_id=1, source_target_pairs={{2,4},{4,2},{6,8},{8,6},{10,12},{12,10},{14,16},{16,14},{18,20},{2... | collective-permute-start | bytes 245768 | tf_op jit(solution)/shard_map/ppermute | solution.py:540
  19.5 4.4 %free.2 = (f32[34,144,128]{2,1,0:T(8,128)S(1)}, f32[32,128]{1,0:T(8,128)S(1)}, f32[32,128]{1,0:T(8,128)S(1)}, f32[32,128]{1,0:T(8,128)S(1)}, f32[32,128]{1,0:T(8...) custom-call(f32[34,144,128]{2,1,0:T(8,128)S(1)} %get-tuple-element.1, ...), custom_call_target="tpu_custom_call" | custom-call | flops 30000000 | bytes 1048576 | tf_op jit(solution)/shard_map/free/pallas_call | solution.py:516
  24.0 1.3 %second.2 = (f32[32,128]{1,0:T(8,128)S(1)}, f32[32,128]{1,0:T(8,128)S(1)}, f32[32,128]{1,0:T(8,128)S(1)}, f32[32,128]{1,0:T(8,128)S(1)}, f32[128,128]{1,0:T(8,12...) custom-call(f32[32,128]{1,0:T(8,128)S(1)} %get-tuple-element.115.ref, ...), custom_call_target="tpu_custom_call" | custom-call | flops 20000000 | bytes 1048576 | tf_op jit(solution)/shard_map/second/pallas_call | solution.py:516
  25.5 3.8 %collective-permute-start.5 = (f32[64,128]{1,0:T(8,128)S(1)}, f32[64,128]{1,0:T(8,128)S(1)}, u32[]{:S(2)}, u32[]{:S(2)}) collective-permute-start(f32[64,128]{1,0:T(8,128)S(1)} %get-tuple-element.144), channel_id=1, source_target_pairs={{0,32},{32,0},{64,96},{96,64},{1,33},{33,1},{65,97},{97,65},{2,34}... | collective-permute-start | bytes 98312 | tf_op jit(solution)/shard_map/ppermute | solution.py:542
  30.1 3.9 %collective-permute-start.8 = (f32[64,128]{1,0:T(8,128)S(1)}, f32[64,128]{1,0:T(8,128)S(1)}, u32[]{:S(2)}, u32[]{:S(2)}) collective-permute-start(f32[64,128]{1,0:T(8,128)S(1)} %get-tuple-element.147), channel_id=1, source_target_pairs={{2,4},{4,2},{6,8},{8,6},{10,12},{12,10},{14,16},{16,14},{18,20},{2... | collective-permute-start | bytes 98312 | tf_op jit(solution)/shard_map/ppermute | solution.py:540
  34.0 2.7 %response.2 = (f32[34,144,128]{2,1,0:T(8,128)S(1)}, f32[1,128]{1,0:T(1,128)S(1)}) custom-call(f32[32,128]{1,0:T(8,128)S(1)} %get-tuple-element.151.refs_0_.refs_5_, f32[32,128]{1,0:T(8,128)S(1)} %get-tuple-element.152.refs_1_.refs_6_, f32[32,128]{1,0:T(8,128)S(1)} %get-tuple-element.153.refs_2_.refs_7_, f32[32,128]{1,0:T(8,128)S(1)} %get-tuple-element.154.refs_3_.refs_8_, ...), custom_call_target="tpu_custom_call" | custom-call | flops 30000000 | bytes 1048576 | tf_op jit(solution)/shard_map/response/pallas_call | solution.py:516
  36.7 1.5 %copy-done = f32[34,144,128]{2,1,0:T(8,128)} copy-done((f32[34,144,128]{2,1,0:T(8,128)}, f32[34,144,128]{2,1,0:T(8,128)S(1)}, u32[]{:S(2)}) %copy-start) | copy-done | bytes 2506776
  38.2 1.5 %third.2 = (f32[32,128]{1,0:T(8,128)S(1)}, f32[32,128]{1,0:T(8,128)S(1)}, f32[32,128]{1,0:T(8,128)S(1)}, f32[32,128]{1,0:T(8,128)S(1)}, f32[128,128]{1,0:T(8,128...) custom-call(f32[64,128]{1,0:T(8,128)S(1)} %get-tuple-element.138.ref, ...), custom_call_target="tpu_custom_call" | custom-call | flops 20000000 | bytes 1048576 | tf_op jit(solution)/shard_map/third/pallas_call | solution.py:516
  39.7 21.3 %all_to_all.10 = f32[128,1,128]{2,1,0:T(1,128)S(1)} all-to-all(f32[128,1,128]{2,1,0:T(1,128)S(1)} %bitcast.19), channel_id=1, replica_groups=mesh['gx'=4,'gy'=16,'gz'=2] {'gx','gy','gz'}, dimensions={0} | all-to-all | bytes 131072 | tf_op jit(solution)/shard_map/all_to_all | solution.py:548
  61.0 7.1 %fourth.1 = (f32[32,128,128]{2,1,0:T(8,128)S(1)}, f32[34,144,128]{2,1,0:T(8,128)S(1)}, f32[32,128]{1,0:T(8,128)}, f32[32,128]{1,0:T(8,128)S(1)}, f32[32,128]{1,0...) custom-call(f32[128,128]{1,0:T(8,128)S(1)} %bitcast.15, ...), custom_call_target="tpu_custom_call" | custom-call | flops 50000000 | bytes 1048576 | tf_op jit(solution)/shard_map/fourth/pallas_call | solution.py:516
  68.1 1.1 collective-permute-start.14
  70.2 1.2 %collective-permute-start.12 = (f32[32,128]{1,0:T(8,128)S(1)}, f32[32,128]{1,0:T(8,128)S(1)}, u32[]{:S(2)}, u32[]{:S(2)}) collective-permute-start(f32[32,128]{1,0:T(8,128)S(1)} %get-tuple-element.181), channel_id=1, source_target_pairs={{0,2},{2,0},{4,6},{6,4},{8,10},{10,8},{12,14},{14,12},{16,18},{18,... | collective-permute-start | bytes 49160 | tf_op jit(solution)/shard_map/ppermute | solution.py:543
  71.3 2.4 %collective-permute-start.13 = (f32[32,128]{1,0:T(8,128)S(1)}, f32[32,128]{1,0:T(8,128)S(1)}, u32[]{:S(2)}, u32[]{:S(2)}) collective-permute-start(f32[32,128]{1,0:T(8,128)S(1)} %get-tuple-element.182), channel_id=1, source_target_pairs={{2,4},{4,2},{6,8},{8,6},{10,12},{12,10},{14,16},{16,14},{18,20},{2... | collective-permute-start | bytes 49160 | tf_op jit(solution)/shard_map/ppermute | solution.py:540
  73.7 3.6 %free.3 = (f32[34,144,128]{2,1,0:T(8,128)S(1)}, f32[32,128]{1,0:T(8,128)S(1)}, f32[32,128]{1,0:T(8,128)S(1)}, f32[32,128]{1,0:T(8,128)S(1)}, f32[32,128]{1,0:T(8...) custom-call(f32[34,144,128]{2,1,0:T(8,128)S(1)} %get-tuple-element.184.state, ...), custom_call_target="tpu_custom_call" | custom-call | flops 30000000 | bytes 1048576 | tf_op jit(solution)/shard_map/free/pallas_call | solution.py:516
  77.3 1.2 %second.3 = (f32[32,128]{1,0:T(8,128)S(1)}, f32[32,128]{1,0:T(8,128)S(1)}, f32[32,128]{1,0:T(8,128)S(1)}, f32[32,128]{1,0:T(8,128)S(1)}, f32[128,128]{1,0:T(8,12...) custom-call(f32[32,128]{1,0:T(8,128)S(1)} %get-tuple-element.173.ref, ...), custom_call_target="tpu_custom_call" | custom-call | flops 20000000 | bytes 1048576 | tf_op jit(solution)/shard_map/second/pallas_call | solution.py:516
  78.5 2.0 %collective-permute-start.19 = (f32[256,128]{1,0:T(8,128)S(1)}, f32[256,128]{1,0:T(8,128)S(1)}, u32[]{:S(2)}, u32[]{:S(2)}) collective-permute-start(f32[256,128]{1,0:T(8,128)S(1)} %get-tuple-element.202), channel_id=1, source_target_pairs={{0,1},{1,0},{2,3},{3,2},{4,5},{5,4},{6,7},{7,6},{8,9},{9,8},{10,11... | collective-permute-start | bytes 393224 | tf_op jit(solution)/shard_map/ppermute | solution.py:539
  80.5 2.9 %collective-permute-start.15 = (f32[64,128]{1,0:T(8,128)S(1)}, f32[64,128]{1,0:T(8,128)S(1)}, u32[]{:S(2)}, u32[]{:S(2)}) collective-permute-start(f32[64,128]{1,0:T(8,128)S(1)} %get-tuple-element.198), channel_id=1, source_target_pairs={{0,32},{32,0},{64,96},{96,64},{1,33},{33,1},{65,97},{97,65},{2,34}... | collective-permute-start | bytes 98312 | tf_op jit(solution)/shard_map/ppermute | solution.py:542
  83.4 0.7 collective-permute-start.16
  84.1 3.9 %collective-permute-start.18 = (f32[64,128]{1,0:T(8,128)S(1)}, f32[64,128]{1,0:T(8,128)S(1)}, u32[]{:S(2)}, u32[]{:S(2)}) collective-permute-start(f32[64,128]{1,0:T(8,128)S(1)} %get-tuple-element.201), channel_id=1, source_target_pairs={{2,4},{4,2},{6,8},{8,6},{10,12},{12,10},{14,16},{16,14},{18,20},{2... | collective-permute-start | bytes 98312 | tf_op jit(solution)/shard_map/ppermute | solution.py:540
  88.1 2.7 %response.3 = (f32[34,144,128]{2,1,0:T(8,128)S(1)}, f32[1,128]{1,0:T(1,128)S(1)}) custom-call(f32[32,128]{1,0:T(8,128)S(1)} %get-tuple-element.203.refs_0_, f32[32,128]{1,0:T(8,128)S(1)} %get-tuple-element.204.refs_1_.refs_6_, f32[32,128]{1,0:T(8,128)S(1)} %get-tuple-element.205.refs_2_, f32[32,128]{1,0:T(8,128)S(1)} %get-tuple-element.206.refs_3_.refs_7_, ...), custom_call_target="tpu_custom_call" | custom-call | flops 30000000 | bytes 1048576 | tf_op jit(solution)/shard_map/response/pallas_call | solution.py:516
  90.8 2.0 %third.3 = (f32[32,128]{1,0:T(8,128)}, f32[32,128]{1,0:T(8,128)S(1)}, f32[32,128]{1,0:T(8,128)}, f32[32,128]{1,0:T(8,128)S(1)}, f32[128,128]{1,0:T(8,128)}, /*in...) custom-call(f32[64,128]{1,0:T(8,128)S(1)} %get-tuple-element.192.ref, ...), custom_call_target="tpu_custom_call" | custom-call | flops 20000000 | bytes 1048576 | tf_op jit(solution)/shard_map/third/pallas_call | solution.py:516
  92.8 17.7 %all_to_all.11 = f32[128,1,128]{2,1,0:T(1,128)S(1)} all-to-all(f32[128,1,128]{2,1,0:T(1,128)S(1)} %bitcast.18), channel_id=1, replica_groups=mesh['gx'=4,'gy'=16,'gz'=2] {'gx','gy','gz'}, dimensions={0} | all-to-all | bytes 131072 | tf_op jit(solution)/shard_map/all_to_all | solution.py:548
  110.5 2.2 %last.1 = (f32[32,128,128]{2,1,0:T(8,128)}, f32[32,128]{1,0:T(8,128)}, f32[32,128]{1,0:T(8,128)}, f32[128,128]{1,0:T(8,128)}) custom-call(f32[128,128]{1,0:T(8,128)S(1)} %bitcast.16, f32[34,144,128]{2,1,0:T(8,128)S(1)} %get-tuple-element.211.refs_1_, f32[34,144,128]{2,1,0:T(8,128)S(1)} %get-tuple-element.212.refs_2_, ...), custom_call_target="tpu_custom_call" | custom-call | flops 20000000 | bytes 1048576 | tf_op jit(solution)/shard_map/last/pallas_call | solution.py:516
  (30 shorter events, 2.2 us)
Async XLA Ops:
  1.3 1.6 %copy-start.1 = (f32[32,128,128]{2,1,0:T(8,128)S(1)}, f32[32,128,128]{2,1,0:T(8,128)}, u32[]{:S(2)}) copy-start(f32[32,128,128]{2,1,0:T(8,128)} %heat_in.1) | copy-start | bytes 6291460
  2.9 1.6 %copy-start.2 = (f32[32,128,128]{2,1,0:T(8,128)S(1)}, f32[32,128,128]{2,1,0:T(8,128)}, u32[]{:S(2)}) copy-start(f32[32,128,128]{2,1,0:T(8,128)} %cond_in.1) | copy-start | bytes 6291460
  4.5 0.9 copy-start.3
  9.1 14.9 %collective-permute-start.4 = (f32[256,128]{1,0:T(8,128)S(1)}, f32[256,128]{1,0:T(8,128)S(1)}, u32[]{:S(2)}, u32[]{:S(2)}) collective-permute-start(f32[256,128]{1,0:T(8,128)S(1)} %get-tuple-element.125), channel_id=1, source_target_pairs={{0,1},{1,0},{2,3},{3,2},{4,5},{5,4},{6,7},{7,6},{8,9},{9,8},{10,11... | collective-permute-start | bytes 393224 | tf_op jit(solution)/shard_map/ppermute | solution.py:539
  12.7 11.2 %collective-permute-start = (f32[160,128]{1,0:T(8,128)S(1)}, f32[160,128]{1,0:T(8,128)S(1)}, u32[]{:S(2)}, u32[]{:S(2)}) collective-permute-start(f32[160,128]{1,0:T(8,128)S(1)} %get-tuple-element.121), channel_id=1, source_target_pairs={{0,32},{32,0},{64,96},{96,64},{1,33},{33,1},{65,97},{97,65},{2,34}... | collective-permute-start | bytes 245768 | tf_op jit(solution)/shard_map/ppermute | solution.py:542
  14.0 9.9 %collective-permute-start.1 = (f32[160,128]{1,0:T(8,128)S(1)}, f32[160,128]{1,0:T(8,128)S(1)}, u32[]{:S(2)}, u32[]{:S(2)}) collective-permute-start(f32[160,128]{1,0:T(8,128)S(1)} %get-tuple-element.122), channel_id=1, source_target_pairs={{32,64},{64,32},{33,65},{65,33},{34,66},{66,34},{35,67},{67,35},{3... | collective-permute-start | bytes 245768 | tf_op jit(solution)/shard_map/ppermute | solution.py:541
  14.7 9.2 %collective-permute-start.2 = (f32[160,128]{1,0:T(8,128)S(1)}, f32[160,128]{1,0:T(8,128)S(1)}, u32[]{:S(2)}, u32[]{:S(2)}) collective-permute-start(f32[160,128]{1,0:T(8,128)S(1)} %get-tuple-element.123), channel_id=1, source_target_pairs={{0,2},{2,0},{4,6},{6,4},{8,10},{10,8},{12,14},{14,12},{16,18},{18,... | collective-permute-start | bytes 245768 | tf_op jit(solution)/shard_map/ppermute | solution.py:543
  16.0 7.9 %collective-permute-start.3 = (f32[160,128]{1,0:T(8,128)S(1)}, f32[160,128]{1,0:T(8,128)S(1)}, u32[]{:S(2)}, u32[]{:S(2)}) collective-permute-start(f32[160,128]{1,0:T(8,128)S(1)} %get-tuple-element.124), channel_id=1, source_target_pairs={{2,4},{4,2},{6,8},{8,6},{10,12},{12,10},{14,16},{16,14},{18,20},{2... | collective-permute-start | bytes 245768 | tf_op jit(solution)/shard_map/ppermute | solution.py:540
  25.2 13.0 %collective-permute-start.9 = (f32[256,128]{1,0:T(8,128)S(1)}, f32[256,128]{1,0:T(8,128)S(1)}, u32[]{:S(2)}, u32[]{:S(2)}) collective-permute-start(f32[256,128]{1,0:T(8,128)S(1)} %get-tuple-element.148), channel_id=1, source_target_pairs={{0,1},{1,0},{2,3},{3,2},{4,5},{5,4},{6,7},{7,6},{8,9},{9,8},{10,11... | collective-permute-start | bytes 393224 | tf_op jit(solution)/shard_map/ppermute | solution.py:539
  25.5 12.6 %collective-permute-start.5 = (f32[64,128]{1,0:T(8,128)S(1)}, f32[64,128]{1,0:T(8,128)S(1)}, u32[]{:S(2)}, u32[]{:S(2)}) collective-permute-start(f32[64,128]{1,0:T(8,128)S(1)} %get-tuple-element.144), channel_id=1, source_target_pairs={{0,32},{32,0},{64,96},{96,64},{1,33},{33,1},{65,97},{97,65},{2,34}... | collective-permute-start | bytes 98312 | tf_op jit(solution)/shard_map/ppermute | solution.py:542
  29.4 8.8 %collective-permute-start.6 = (f32[64,128]{1,0:T(8,128)S(1)}, f32[64,128]{1,0:T(8,128)S(1)}, u32[]{:S(2)}, u32[]{:S(2)}) collective-permute-start(f32[64,128]{1,0:T(8,128)S(1)} %get-tuple-element.145), channel_id=1, source_target_pairs={{32,64},{64,32},{33,65},{65,33},{34,66},{66,34},{35,67},{67,35},{3... | collective-permute-start | bytes 98312 | tf_op jit(solution)/shard_map/ppermute | solution.py:541
  30.0 8.2 %collective-permute-start.7 = (f32[64,128]{1,0:T(8,128)S(1)}, f32[64,128]{1,0:T(8,128)S(1)}, u32[]{:S(2)}, u32[]{:S(2)}) collective-permute-start(f32[64,128]{1,0:T(8,128)S(1)} %get-tuple-element.146), channel_id=1, source_target_pairs={{0,2},{2,0},{4,6},{6,4},{8,10},{10,8},{12,14},{14,12},{16,18},{18,... | collective-permute-start | bytes 98312 | tf_op jit(solution)/shard_map/ppermute | solution.py:543
  30.1 8.1 %collective-permute-start.8 = (f32[64,128]{1,0:T(8,128)S(1)}, f32[64,128]{1,0:T(8,128)S(1)}, u32[]{:S(2)}, u32[]{:S(2)}) collective-permute-start(f32[64,128]{1,0:T(8,128)S(1)} %get-tuple-element.147), channel_id=1, source_target_pairs={{2,4},{4,2},{6,8},{8,6},{10,12},{12,10},{14,16},{16,14},{18,20},{2... | collective-permute-start | bytes 98312 | tf_op jit(solution)/shard_map/ppermute | solution.py:540
  36.7 1.5 %copy-start = (f32[34,144,128]{2,1,0:T(8,128)}, f32[34,144,128]{2,1,0:T(8,128)S(1)}, u32[]{:S(2)}) copy-start(f32[34,144,128]{2,1,0:T(8,128)S(1)} %get-tuple-element.160.refs_4_) | copy-start | bytes 7520260
  68.1 9.2 %collective-permute-start.14 = (f32[128,128]{1,0:T(8,128)S(1)}, f32[128,128]{1,0:T(8,128)S(1)}, u32[]{:S(2)}, u32[]{:S(2)}) collective-permute-start(f32[128,128]{1,0:T(8,128)S(1)} %get-tuple-element.183), channel_id=1, source_target_pairs={{0,1},{1,0},{2,3},{3,2},{4,5},{5,4},{6,7},{7,6},{8,9},{9,8},{10,11... | collective-permute-start | bytes 196616 | tf_op jit(solution)/shard_map/ppermute | solution.py:539
  69.2 8.1 %collective-permute-start.10 = (f32[32,128]{1,0:T(8,128)S(1)}, f32[32,128]{1,0:T(8,128)S(1)}, u32[]{:S(2)}, u32[]{:S(2)}) collective-permute-start(f32[32,128]{1,0:T(8,128)S(1)} %get-tuple-element.179), channel_id=1, source_target_pairs={{0,32},{32,0},{64,96},{96,64},{1,33},{33,1},{65,97},{97,65},{2,34}... | collective-permute-start | bytes 49160 | tf_op jit(solution)/shard_map/ppermute | solution.py:542
  69.5 7.8 %collective-permute-start.11 = (f32[32,128]{1,0:T(8,128)S(1)}, f32[32,128]{1,0:T(8,128)S(1)}, u32[]{:S(2)}, u32[]{:S(2)}) collective-permute-start(f32[32,128]{1,0:T(8,128)S(1)} %get-tuple-element.180), channel_id=1, source_target_pairs={{32,64},{64,32},{33,65},{65,33},{34,66},{66,34},{35,67},{67,35},{3... | collective-permute-start | bytes 49160 | tf_op jit(solution)/shard_map/ppermute | solution.py:541
  70.2 7.1 %collective-permute-start.12 = (f32[32,128]{1,0:T(8,128)S(1)}, f32[32,128]{1,0:T(8,128)S(1)}, u32[]{:S(2)}, u32[]{:S(2)}) collective-permute-start(f32[32,128]{1,0:T(8,128)S(1)} %get-tuple-element.181), channel_id=1, source_target_pairs={{0,2},{2,0},{4,6},{6,4},{8,10},{10,8},{12,14},{14,12},{16,18},{18,... | collective-permute-start | bytes 49160 | tf_op jit(solution)/shard_map/ppermute | solution.py:543
  71.3 6.0 %collective-permute-start.13 = (f32[32,128]{1,0:T(8,128)S(1)}, f32[32,128]{1,0:T(8,128)S(1)}, u32[]{:S(2)}, u32[]{:S(2)}) collective-permute-start(f32[32,128]{1,0:T(8,128)S(1)} %get-tuple-element.182), channel_id=1, source_target_pairs={{2,4},{4,2},{6,8},{8,6},{10,12},{12,10},{14,16},{16,14},{18,20},{2... | collective-permute-start | bytes 49160 | tf_op jit(solution)/shard_map/ppermute | solution.py:540
  78.5 12.2 %collective-permute-start.19 = (f32[256,128]{1,0:T(8,128)S(1)}, f32[256,128]{1,0:T(8,128)S(1)}, u32[]{:S(2)}, u32[]{:S(2)}) collective-permute-start(f32[256,128]{1,0:T(8,128)S(1)} %get-tuple-element.202), channel_id=1, source_target_pairs={{0,1},{1,0},{2,3},{3,2},{4,5},{5,4},{6,7},{7,6},{8,9},{9,8},{10,11... | collective-permute-start | bytes 393224 | tf_op jit(solution)/shard_map/ppermute | solution.py:539
  80.5 10.2 %collective-permute-start.15 = (f32[64,128]{1,0:T(8,128)S(1)}, f32[64,128]{1,0:T(8,128)S(1)}, u32[]{:S(2)}, u32[]{:S(2)}) collective-permute-start(f32[64,128]{1,0:T(8,128)S(1)} %get-tuple-element.198), channel_id=1, source_target_pairs={{0,32},{32,0},{64,96},{96,64},{1,33},{33,1},{65,97},{97,65},{2,34}... | collective-permute-start | bytes 98312 | tf_op jit(solution)/shard_map/ppermute | solution.py:542
  83.4 7.4 %collective-permute-start.16 = (f32[64,128]{1,0:T(8,128)S(1)}, f32[64,128]{1,0:T(8,128)S(1)}, u32[]{:S(2)}, u32[]{:S(2)}) collective-permute-start(f32[64,128]{1,0:T(8,128)S(1)} %get-tuple-element.199), channel_id=1, source_target_pairs={{32,64},{64,32},{33,65},{65,33},{34,66},{66,34},{35,67},{67,35},{3... | collective-permute-start | bytes 98312 | tf_op jit(solution)/shard_map/ppermute | solution.py:541
  84.0 6.7 %collective-permute-start.17 = (f32[64,128]{1,0:T(8,128)S(1)}, f32[64,128]{1,0:T(8,128)S(1)}, u32[]{:S(2)}, u32[]{:S(2)}) collective-permute-start(f32[64,128]{1,0:T(8,128)S(1)} %get-tuple-element.200), channel_id=1, source_target_pairs={{0,2},{2,0},{4,6},{6,4},{8,10},{10,8},{12,14},{14,12},{16,18},{18,... | collective-permute-start | bytes 98312 | tf_op jit(solution)/shard_map/ppermute | solution.py:543
  84.1 6.7 %collective-permute-start.18 = (f32[64,128]{1,0:T(8,128)S(1)}, f32[64,128]{1,0:T(8,128)S(1)}, u32[]{:S(2)}, u32[]{:S(2)}) collective-permute-start(f32[64,128]{1,0:T(8,128)S(1)} %get-tuple-element.201), channel_id=1, source_target_pairs={{2,4},{4,2},{6,8},{8,6},{10,12},{12,10},{14,16},{16,14},{18,20},{2... | collective-permute-start | bytes 98312 | tf_op jit(solution)/shard_map/ppermute | solution.py:540

commit v3 on v2

--- a/solution.py
+++ b/solution.py
@@ -273,7 +273,7 @@
     for c in tables:
         c.wait()
     for d in range(3):
-        onehot = jnp.where(row_of((C, C)) == segs[d : d + 1, :], 1.0, 0.0).astype(BF16)
+        onehot = jnp.where(row_of((C, C)) == segs[d], 1.0, 0.0).astype(BF16)
         base = sum(lax.dot_general(onehot, p, (((1,), (1,)), ((), ())), preferred_element_type=F32) for p in reversed(parts_of(proj[d])))
         store_parts(parts, d, base)
         for a in (sends[:2], sends[2:4])[d] if d < 2 else ():
@@ -400,16 +400,22 @@
     sums[...] = row_of_sums([square_sum(lifted, lifted), jnp.sum(acc) / DAMPING_WEIGHT])
 
 
-def third_kernel(*refs):
+def merge_sides(low, high):
+    return [f for pair in zip(low, high) for f in pair]
+
+
+def third_kernel(first, *refs):
     it = iter(refs)
     take = lambda n: [next(it) for _ in range(n)]
     own_uv = take(6)
     got = take(5)
     bases, prev, back, weight, wx, wy, before = take(7)
-    lift_u = take(6)
-    lift_v = take(6)
+    high_u, high_v = take(3), take(3)
     (rows,) = take(1)
+    low_u, low_v = take(3), take(3)
     (turn,) = take(1)
+    lift_u = merge_sides(low_u, high_u)
+    lift_v = merge_sides(low_v, high_v)
     jumps(own_uv, got, bases, prev, back, 2, [lift_u, lift_v])
     weights = layer_weights(weight, wx, wy)
     u = lift_layers(lift_u, turn.at[0], False)
@@ -439,10 +445,12 @@
     lift_u = take(6)
     lift_v = take(6)
     supply, state = take(2)
-    held = take(6)
+    high = take(3)
     own = take(6)
     sends = take(5)
+    low = take(3)
     mid, turn, cols = take(3)
+    held = merge_sides(low, high)
     one, two = steps(totals)
     for i in range(6):
         held[i][...] = one * lift_1[i][...] + two * (lift_u[i][...] - one * lift_v[i][...])
@@ -500,6 +508,8 @@
 FACES = [FACE] * 4 + [SQUARE] * 2
 LAYERS = jax.ShapeDtypeStruct((4, CZ, C), F32)
 ROW = jax.ShapeDtypeStruct((1, C), F32)
+SIDE = [FACE, FACE, SQUARE]
+S_SIDE = [pltpu.VMEM(f.shape, F32) for f in SIDE]
 S_FIELD = pltpu.VMEM((CZ, C, C), F32)
 S_PADDED = pltpu.VMEM((CZ + 2, C + 2 * PAD, C), F32)
 PIECES = jax.ShapeDtypeStruct((9, C, C), BF16)
@@ -520,7 +530,7 @@
             out_specs=tuple(out_specs or [VM] * len(outs)),
             scratch_shapes=scratch,
             name=name,
-            compiler_params=pltpu.CompilerParams(vmem_limit_bytes=40 * 1024 * 1024),
+            compiler_params=pltpu.CompilerParams(vmem_limit_bytes=20 * 1024 * 1024),
             cost_estimate=pl.CostEstimate(flops=us * 10**7, transcendentals=0, bytes_accessed=2**20),
         )(*args)
     )
@@ -551,11 +561,11 @@
 
 def body(heat, cond, projection, segment_map):
     proj = projection[0, 0, 0]
-    segs = segment_map[0, 0, 0]
+    segs = segment_map.reshape(3, 1, C)
     dma = pltpu.SemaphoreType.DMA
     scratch = [S_FIELD, pltpu.VMEM(proj.shape, F32), pltpu.VMEM(segs.shape, jnp.int32), S_PADDED, S_SQUARE, dma((2, PARTS)), dma((2,))]
     outs = [FIELD, PADDED, PIECES, FIELD] + FACES + sends_of(1, C)
-    out = call(first_kernel, "first", outs, scratch, (heat, cond, proj, segs), 4, [AWAY] * 4)
+    out = call(first_kernel, "first", outs, scratch, [pltpu.with_memory_space_constraint(a, pltpu.MemorySpace.HBM) for a in (heat, cond, proj, segs)], 4, [AWAY] * 4)
     weight, state, bases, heat = out[:4]
     own, sends = out[4:10], out[10:]
     supply = heat
@@ -579,15 +589,17 @@
         got = exchange(sends)
         resp, sums = call(response_kernel, "response", [PADDED, ROW], [S_FIELD, S_PADDED, S_SQUARE, S_SQUARE], lift_1 + [weight], 3)
         args = own_uv + got + [bases] + prev + [weight, wx, wy, sums]
-        out = call(third_kernel, "third", FACES + FACES + [SQUARE], [pltpu.VMEM((2, C, C), F32)], args, 2)
-        lift_u, lift_v, rows = out[:6], out[6:12], out[12]
+        outs = SIDE + SIDE + [SQUARE] + (SIDE + SIDE if first else [])
+        scratch = ([] if first else S_SIDE + S_SIDE) + [pltpu.VMEM((2, C, C), F32)]
+        out = call(functools.partial(third_kernel, first), "third", outs, scratch, args, 2)
+        high_u, high_v, rows = out[:3], out[3:6], out[6]
         totals = gather_rows(rows)
         if first:
-            args = [totals, heat, weight, free, resp] + lift_1 + lift_u + lift_v
-            out = call(fourth_kernel, "fourth", [FIELD, PADDED] + FACES + FACES + sends_of(1, 0), [S_PADDED, S_SQUARE, S_SQUARE], args, 5)
-            supply, state, held, own, sends = out[0], out[1], out[2:8], out[8:14], out[14:]
-    upper = lambda faces: [faces[1], faces[3], faces[5]]
-    args = [totals, free, resp] + upper(held) + upper(lift_1) + upper(lift_u) + upper(lift_v)
+            args = [totals, heat, weight, free, resp] + lift_1 + merge_sides(out[7:10], high_u) + merge_sides(out[10:13], high_v)
+            outs = [FIELD, PADDED] + SIDE + FACES + sends_of(1, 0)
+            out = call(fourth_kernel, "fourth", outs, S_SIDE + [S_PADDED, S_SQUARE, S_SQUARE], args, 5)
+            supply, state, held, own, sends = out[0], out[1], out[2:5], out[5:11], out[11:]
+    args = [totals, free, resp] + held + [lift_1[i] for i in (1, 3, 5)] + high_u + high_v
     state, mx, my, mz = call(last_kernel, "last", [FIELD, FACE, FACE, SQUARE], [S_FIELD, dma((PARTS,))], args, 2, None, [AWAY, VM, VM, VM])
     return state, mx[None, None, None], my[None, None, None], mz[None, None, None]
 

time: 113 us -> 105 us (0.929)
  local copies, waits for them, and re-layouts: 6.26 us -> 0 us
  Pallas kernels: 32.2 us -> 30.6 us
    unnamed x9 -> x0, local copies, waits for them, and re-layouts: 6.26 us -> none
    pallas_call x11, Pallas kernels: 32.2 us -> 30.6 us  [call(): pl.pallas_call(kernel, out_shape=tuple(outs), in_specs=in_specs or [VM] *...]
  transfers between devices with their start and end apart: 20 -> 20, of which waited for: 0 -> 0; matrix products, arithmetic and copies ran while one was open for 0% -> 0% of each run, Pallas kernels for 12% -> 13%
where the time goes in v3:
time: 105 us
  blocking collectives  39 us (37%)
  starting transfers between devices  34.1 us (32%)
  Pallas kernels  30.6 us (29%)
  between operations  1.1 us (1%)
    all_to_all x2, blocking collectives, gather_rows(): rows = lax.all_to_all(rows.reshape(C, 1, C), AXES, 0, 0)  39 us
    pallas_call x11, Pallas kernels, call(): pl.pallas_call(kernel, out_shape=tuple(outs), in_specs=in_specs or [VM] *...  30.6 us
    ppermute x4, starting transfers between devices, exchange(): yb = lax.ppermute(yb, 'gy', swap_pairs('gy', 1))  13.7 us
    ppermute x4, starting transfers between devices, exchange(): xa = lax.ppermute(xa, 'gx', swap_pairs('gx', 0))  8.33 us
    ppermute x4, starting transfers between devices, exchange(): zz = lax.ppermute(zz, 'gz', swap_pairs('gz', 0))  6.88 us
    ppermute x4, starting transfers between devices, exchange(): ya = lax.ppermute(ya, 'gy', swap_pairs('gy', 0))  2.66 us
    ppermute x4, starting transfers between devices, exchange(): xb = lax.ppermute(xb, 'gx', swap_pairs('gx', 1))  2.61 us
  transfers between devices with their start and end apart: 20, of which 0 were waited for; matrix products, arithmetic and copies ran while one was open for 0% of the time, Pallas kernels for 13%

profile of v3, /device:TPU:1, one launch (start us, length us, event | category | flops | bytes accessed | tf_op | source)
XLA Modules:
  0.0 104.8 jit_solution(8459349557990745075)
XLA Ops:
  0.6 4.9 %first.1 = (f32[32,128,128]{2,1,0:T(8,128)S(1)}, f32[34,144,128]{2,1,0:T(8,128)S(1)}, bf16[9,128,128]{2,1,0:T(8,128)(2,1)S(1)}, f32[32,128,128]{2,1,0:T(8,128)S(...) custom-call(f32[32,128,128]{2,1,0:T(8,128)} %heat_in.1, ...), custom_call_target="tpu_custom_call" | custom-call | flops 40000000 | bytes 1048576 | tf_op jit(solution)/shard_map/first/pallas_call | solution.py:526
  5.6 3.6 %collective-permute-start.4 = (f32[256,128]{1,0:T(8,128)S(1)}, f32[256,128]{1,0:T(8,128)S(1)}, u32[]{:S(2)}, u32[]{:S(2)}) collective-permute-start(f32[256,128]{1,0:T(8,128)S(1)} %get-tuple-element.125), channel_id=1, source_target_pairs={{0,1},{1,0},{2,3},{3,2},{4,5},{5,4},{6,7},{7,6},{8,9},{9,8},{10,11... | collective-permute-start | bytes 393224 | tf_op jit(solution)/shard_map/ppermute | solution.py:549
  9.2 1.3 %collective-permute-start = (f32[160,128]{1,0:T(8,128)S(1)}, f32[160,128]{1,0:T(8,128)S(1)}, u32[]{:S(2)}, u32[]{:S(2)}) collective-permute-start(f32[160,128]{1,0:T(8,128)S(1)} %get-tuple-element.121), channel_id=1, source_target_pairs={{0,32},{32,0},{64,96},{96,64},{1,33},{33,1},{65,97},{97,65},{2,34}... | collective-permute-start | bytes 245768 | tf_op jit(solution)/shard_map/ppermute | solution.py:552
  10.5 0.7 collective-permute-start.1
  11.2 1.3 %collective-permute-start.2 = (f32[160,128]{1,0:T(8,128)S(1)}, f32[160,128]{1,0:T(8,128)S(1)}, u32[]{:S(2)}, u32[]{:S(2)}) collective-permute-start(f32[160,128]{1,0:T(8,128)S(1)} %get-tuple-element.123), channel_id=1, source_target_pairs={{0,2},{2,0},{4,6},{6,4},{8,10},{10,8},{12,14},{14,12},{16,18},{18,... | collective-permute-start | bytes 245768 | tf_op jit(solution)/shard_map/ppermute | solution.py:553
  12.5 3.4 %collective-permute-start.3 = (f32[160,128]{1,0:T(8,128)S(1)}, f32[160,128]{1,0:T(8,128)S(1)}, u32[]{:S(2)}, u32[]{:S(2)}) collective-permute-start(f32[160,128]{1,0:T(8,128)S(1)} %get-tuple-element.124), channel_id=1, source_target_pairs={{2,4},{4,2},{6,8},{8,6},{10,12},{12,10},{14,16},{16,14},{18,20},{2... | collective-permute-start | bytes 245768 | tf_op jit(solution)/shard_map/ppermute | solution.py:550
  15.9 4.3 %free.2 = (f32[34,144,128]{2,1,0:T(8,128)S(1)}, f32[32,128]{1,0:T(8,128)S(1)}, f32[32,128]{1,0:T(8,128)S(1)}, f32[32,128]{1,0:T(8,128)S(1)}, f32[32,128]{1,0:T(8...) custom-call(f32[34,144,128]{2,1,0:T(8,128)S(1)} %get-tuple-element.1, ...), custom_call_target="tpu_custom_call" | custom-call | flops 30000000 | bytes 1048576 | tf_op jit(solution)/shard_map/free/pallas_call | solution.py:526
  20.3 1.3 %second.2 = (f32[32,128]{1,0:T(8,128)S(1)}, f32[32,128]{1,0:T(8,128)S(1)}, f32[32,128]{1,0:T(8,128)S(1)}, f32[32,128]{1,0:T(8,128)S(1)}, f32[128,128]{1,0:T(8,12...) custom-call(f32[32,128]{1,0:T(8,128)S(1)} %get-tuple-element.115.ref, ...), custom_call_target="tpu_custom_call" | custom-call | flops 20000000 | bytes 1048576 | tf_op jit(solution)/shard_map/second/pallas_call | solution.py:526
  21.6 0.3 collective-permute-start.9
  21.9 3.8 %collective-permute-start.5 = (f32[64,128]{1,0:T(8,128)S(1)}, f32[64,128]{1,0:T(8,128)S(1)}, u32[]{:S(2)}, u32[]{:S(2)}) collective-permute-start(f32[64,128]{1,0:T(8,128)S(1)} %get-tuple-element.144), channel_id=1, source_target_pairs={{0,32},{32,0},{64,96},{96,64},{1,33},{33,1},{65,97},{97,65},{2,34}... | collective-permute-start | bytes 98312 | tf_op jit(solution)/shard_map/ppermute | solution.py:552
  25.7 0.7 collective-permute-start.6
  26.4 0.1 collective-permute-start.7
  26.5 3.9 %collective-permute-start.8 = (f32[64,128]{1,0:T(8,128)S(1)}, f32[64,128]{1,0:T(8,128)S(1)}, u32[]{:S(2)}, u32[]{:S(2)}) collective-permute-start(f32[64,128]{1,0:T(8,128)S(1)} %get-tuple-element.147), channel_id=1, source_target_pairs={{2,4},{4,2},{6,8},{8,6},{10,12},{12,10},{14,16},{16,14},{18,20},{2... | collective-permute-start | bytes 98312 | tf_op jit(solution)/shard_map/ppermute | solution.py:550
  30.4 2.7 %response.2 = (f32[34,144,128]{2,1,0:T(8,128)S(1)}, f32[1,128]{1,0:T(1,128)S(1)}) custom-call(f32[32,128]{1,0:T(8,128)S(1)} %get-tuple-element.151.refs_0_.refs_5_, f32[32,128]{1,0:T(8,128)S(1)} %get-tuple-element.152.refs_1_.refs_6_, f32[32,128]{1,0:T(8,128)S(1)} %get-tuple-element.153.refs_2_.refs_7_, f32[32,128]{1,0:T(8,128)S(1)} %get-tuple-element.154.refs_3_.refs_8_, ...), custom_call_target="tpu_custom_call" | custom-call | flops 30000000 | bytes 1048576 | tf_op jit(solution)/shard_map/response/pallas_call | solution.py:526
  33.1 1.5 %third.2 = (f32[32,128]{1,0:T(8,128)S(1)}, f32[32,128]{1,0:T(8,128)S(1)}, f32[128,128]{1,0:T(8,128)S(1)}, f32[32,128]{1,0:T(8,128)S(1)}, f32[32,128]{1,0:T(8,128...) custom-call(f32[64,128]{1,0:T(8,128)S(1)} %get-tuple-element.138.ref, ...), custom_call_target="tpu_custom_call" | custom-call | flops 20000000 | bytes 1048576 | tf_op jit(solution)/shard_map/third/pallas_call | solution.py:526
  34.6 21.3 %all_to_all.10 = f32[128,1,128]{2,1,0:T(1,128)S(1)} all-to-all(f32[128,1,128]{2,1,0:T(1,128)S(1)} %bitcast.15), channel_id=1, replica_groups=mesh['gx'=4,'gy'=16,'gz'=2] {'gx','gy','gz'}, dimensions={0} | all-to-all | bytes 131072 | tf_op jit(solution)/shard_map/all_to_all | solution.py:558
  55.9 4.8 %fourth.1 = (f32[32,128,128]{2,1,0:T(8,128)S(1)}, f32[34,144,128]{2,1,0:T(8,128)S(1)}, f32[32,128]{1,0:T(8,128)S(1)}, f32[32,128]{1,0:T(8,128)S(1)}, f32[128,128...) custom-call(f32[128,128]{1,0:T(8,128)S(1)} %bitcast.13, ...), custom_call_target="tpu_custom_call" | custom-call | flops 50000000 | bytes 1048576 | tf_op jit(solution)/shard_map/fourth/pallas_call | solution.py:526
  60.7 1.1 %collective-permute-start.14 = (f32[128,128]{1,0:T(8,128)S(1)}, f32[128,128]{1,0:T(8,128)S(1)}, u32[]{:S(2)}, u32[]{:S(2)}) collective-permute-start(f32[128,128]{1,0:T(8,128)S(1)} %get-tuple-element.183), channel_id=1, source_target_pairs={{0,1},{1,0},{2,3},{3,2},{4,5},{5,4},{6,7},{7,6},{8,9},{9,8},{10,11... | collective-permute-start | bytes 196616 | tf_op jit(solution)/shard_map/ppermute | solution.py:549
  61.9 0.4 collective-permute-start.10
  62.2 0.7 collective-permute-start.11
  62.9 1.2 %collective-permute-start.12 = (f32[32,128]{1,0:T(8,128)S(1)}, f32[32,128]{1,0:T(8,128)S(1)}, u32[]{:S(2)}, u32[]{:S(2)}) collective-permute-start(f32[32,128]{1,0:T(8,128)S(1)} %get-tuple-element.181), channel_id=1, source_target_pairs={{0,2},{2,0},{4,6},{6,4},{8,10},{10,8},{12,14},{14,12},{16,18},{18,... | collective-permute-start | bytes 49160 | tf_op jit(solution)/shard_map/ppermute | solution.py:553
  64.0 2.4 %collective-permute-start.13 = (f32[32,128]{1,0:T(8,128)S(1)}, f32[32,128]{1,0:T(8,128)S(1)}, u32[]{:S(2)}, u32[]{:S(2)}) collective-permute-start(f32[32,128]{1,0:T(8,128)S(1)} %get-tuple-element.182), channel_id=1, source_target_pairs={{2,4},{4,2},{6,8},{8,6},{10,12},{12,10},{14,16},{16,14},{18,20},{2... | collective-permute-start | bytes 49160 | tf_op jit(solution)/shard_map/ppermute | solution.py:550
  66.4 3.6 %free.3 = (f32[34,144,128]{2,1,0:T(8,128)S(1)}, f32[32,128]{1,0:T(8,128)S(1)}, f32[32,128]{1,0:T(8,128)S(1)}, f32[32,128]{1,0:T(8,128)S(1)}, f32[32,128]{1,0:T(8...) custom-call(f32[34,144,128]{2,1,0:T(8,128)S(1)} %get-tuple-element.184.state, ...), custom_call_target="tpu_custom_call" | custom-call | flops 30000000 | bytes 1048576 | tf_op jit(solution)/shard_map/free/pallas_call | solution.py:526
  70.0 1.2 %second.3 = (f32[32,128]{1,0:T(8,128)S(1)}, f32[32,128]{1,0:T(8,128)S(1)}, f32[32,128]{1,0:T(8,128)S(1)}, f32[32,128]{1,0:T(8,128)S(1)}, f32[128,128]{1,0:T(8,12...) custom-call(f32[32,128]{1,0:T(8,128)S(1)} %get-tuple-element.173.ref, ...), custom_call_target="tpu_custom_call" | custom-call | flops 20000000 | bytes 1048576 | tf_op jit(solution)/shard_map/second/pallas_call | solution.py:526
  71.2 1.8 %collective-permute-start.19 = (f32[256,128]{1,0:T(8,128)S(1)}, f32[256,128]{1,0:T(8,128)S(1)}, u32[]{:S(2)}, u32[]{:S(2)}) collective-permute-start(f32[256,128]{1,0:T(8,128)S(1)} %get-tuple-element.202), channel_id=1, source_target_pairs={{0,1},{1,0},{2,3},{3,2},{4,5},{5,4},{6,7},{7,6},{8,9},{9,8},{10,11... | collective-permute-start | bytes 393224 | tf_op jit(solution)/shard_map/ppermute | solution.py:549
  73.0 2.9 %collective-permute-start.15 = (f32[64,128]{1,0:T(8,128)S(1)}, f32[64,128]{1,0:T(8,128)S(1)}, u32[]{:S(2)}, u32[]{:S(2)}) collective-permute-start(f32[64,128]{1,0:T(8,128)S(1)} %get-tuple-element.198), channel_id=1, source_target_pairs={{0,32},{32,0},{64,96},{96,64},{1,33},{33,1},{65,97},{97,65},{2,34}... | collective-permute-start | bytes 98312 | tf_op jit(solution)/shard_map/ppermute | solution.py:552
  75.9 0.7 collective-permute-start.16
  76.6 4.0 %collective-permute-start.18 = (f32[64,128]{1,0:T(8,128)S(1)}, f32[64,128]{1,0:T(8,128)S(1)}, u32[]{:S(2)}, u32[]{:S(2)}) collective-permute-start(f32[64,128]{1,0:T(8,128)S(1)} %get-tuple-element.201), channel_id=1, source_target_pairs={{2,4},{4,2},{6,8},{8,6},{10,12},{12,10},{14,16},{16,14},{18,20},{2... | collective-permute-start | bytes 98312 | tf_op jit(solution)/shard_map/ppermute | solution.py:550
  80.6 2.7 %response.3 = (f32[34,144,128]{2,1,0:T(8,128)S(1)}, f32[1,128]{1,0:T(1,128)S(1)}) custom-call(f32[32,128]{1,0:T(8,128)S(1)} %get-tuple-element.203.refs_0_, f32[32,128]{1,0:T(8,128)S(1)} %get-tuple-element.204.refs_1_.refs_6_, f32[32,128]{1,0:T(8,128)S(1)} %get-tuple-element.205.refs_2_, f32[32,128]{1,0:T(8,128)S(1)} %get-tuple-element.206.refs_3_.refs_7_, ...), custom_call_target="tpu_custom_call" | custom-call | flops 30000000 | bytes 1048576 | tf_op jit(solution)/shard_map/response/pallas_call | solution.py:526
  83.3 1.5 %third.3 = (f32[32,128]{1,0:T(8,128)S(1)}, f32[32,128]{1,0:T(8,128)S(1)}, f32[128,128]{1,0:T(8,128)S(1)}, f32[32,128]{1,0:T(8,128)S(1)}, f32[32,128]{1,0:T(8,128...) custom-call(f32[64,128]{1,0:T(8,128)S(1)} %get-tuple-element.192.refs_0_, ...), custom_call_target="tpu_custom_call" | custom-call | flops 20000000 | bytes 1048576 | tf_op jit(solution)/shard_map/third/pallas_call | solution.py:526
  84.8 17.7 %all_to_all.11 = f32[128,1,128]{2,1,0:T(1,128)S(1)} all-to-all(f32[128,1,128]{2,1,0:T(1,128)S(1)} %bitcast.16), channel_id=1, replica_groups=mesh['gx'=4,'gy'=16,'gz'=2] {'gx','gy','gz'}, dimensions={0} | all-to-all | bytes 131072 | tf_op jit(solution)/shard_map/all_to_all | solution.py:558
  102.5 2.2 %last.1 = (f32[32,128,128]{2,1,0:T(8,128)}, f32[32,128]{1,0:T(8,128)}, f32[32,128]{1,0:T(8,128)}, f32[128,128]{1,0:T(8,128)}) custom-call(f32[128,128]{1,0:T(8,128)S(1)} %bitcast.14, f32[34,144,128]{2,1,0:T(8,128)S(1)} %get-tuple-element.211.refs_1_, f32[34,144,128]{2,1,0:T(8,128)S(1)} %get-tuple-element.212.refs_2_, ...), custom_call_target="tpu_custom_call" | custom-call | flops 20000000 | bytes 1048576 | tf_op jit(solution)/shard_map/last/pallas_call | solution.py:526
  (21 shorter events, 0.1 us)
Async XLA Ops:
  5.6 14.7 %collective-permute-start.4 = (f32[256,128]{1,0:T(8,128)S(1)}, f32[256,128]{1,0:T(8,128)S(1)}, u32[]{:S(2)}, u32[]{:S(2)}) collective-permute-start(f32[256,128]{1,0:T(8,128)S(1)} %get-tuple-element.125), channel_id=1, source_target_pairs={{0,1},{1,0},{2,3},{3,2},{4,5},{5,4},{6,7},{7,6},{8,9},{9,8},{10,11... | collective-permute-start | bytes 393224 | tf_op jit(solution)/shard_map/ppermute | solution.py:549
  9.2 11.1 %collective-permute-start = (f32[160,128]{1,0:T(8,128)S(1)}, f32[160,128]{1,0:T(8,128)S(1)}, u32[]{:S(2)}, u32[]{:S(2)}) collective-permute-start(f32[160,128]{1,0:T(8,128)S(1)} %get-tuple-element.121), channel_id=1, source_target_pairs={{0,32},{32,0},{64,96},{96,64},{1,33},{33,1},{65,97},{97,65},{2,34}... | collective-permute-start | bytes 245768 | tf_op jit(solution)/shard_map/ppermute | solution.py:552
  10.5 9.8 %collective-permute-start.1 = (f32[160,128]{1,0:T(8,128)S(1)}, f32[160,128]{1,0:T(8,128)S(1)}, u32[]{:S(2)}, u32[]{:S(2)}) collective-permute-start(f32[160,128]{1,0:T(8,128)S(1)} %get-tuple-element.122), channel_id=1, source_target_pairs={{32,64},{64,32},{33,65},{65,33},{34,66},{66,34},{35,67},{67,35},{3... | collective-permute-start | bytes 245768 | tf_op jit(solution)/shard_map/ppermute | solution.py:551
  11.2 9.1 %collective-permute-start.2 = (f32[160,128]{1,0:T(8,128)S(1)}, f32[160,128]{1,0:T(8,128)S(1)}, u32[]{:S(2)}, u32[]{:S(2)}) collective-permute-start(f32[160,128]{1,0:T(8,128)S(1)} %get-tuple-element.123), channel_id=1, source_target_pairs={{0,2},{2,0},{4,6},{6,4},{8,10},{10,8},{12,14},{14,12},{16,18},{18,... | collective-permute-start | bytes 245768 | tf_op jit(solution)/shard_map/ppermute | solution.py:553
  12.5 7.8 %collective-permute-start.3 = (f32[160,128]{1,0:T(8,128)S(1)}, f32[160,128]{1,0:T(8,128)S(1)}, u32[]{:S(2)}, u32[]{:S(2)}) collective-permute-start(f32[160,128]{1,0:T(8,128)S(1)} %get-tuple-element.124), channel_id=1, source_target_pairs={{2,4},{4,2},{6,8},{8,6},{10,12},{12,10},{14,16},{16,14},{18,20},{2... | collective-permute-start | bytes 245768 | tf_op jit(solution)/shard_map/ppermute | solution.py:550
  21.6 11.5 %collective-permute-start.9 = (f32[256,128]{1,0:T(8,128)S(1)}, f32[256,128]{1,0:T(8,128)S(1)}, u32[]{:S(2)}, u32[]{:S(2)}) collective-permute-start(f32[256,128]{1,0:T(8,128)S(1)} %get-tuple-element.148), channel_id=1, source_target_pairs={{0,1},{1,0},{2,3},{3,2},{4,5},{5,4},{6,7},{7,6},{8,9},{9,8},{10,11... | collective-permute-start | bytes 393224 | tf_op jit(solution)/shard_map/ppermute | solution.py:549
  21.9 11.2 %collective-permute-start.5 = (f32[64,128]{1,0:T(8,128)S(1)}, f32[64,128]{1,0:T(8,128)S(1)}, u32[]{:S(2)}, u32[]{:S(2)}) collective-permute-start(f32[64,128]{1,0:T(8,128)S(1)} %get-tuple-element.144), channel_id=1, source_target_pairs={{0,32},{32,0},{64,96},{96,64},{1,33},{33,1},{65,97},{97,65},{2,34}... | collective-permute-start | bytes 98312 | tf_op jit(solution)/shard_map/ppermute | solution.py:552
  25.7 7.4 %collective-permute-start.6 = (f32[64,128]{1,0:T(8,128)S(1)}, f32[64,128]{1,0:T(8,128)S(1)}, u32[]{:S(2)}, u32[]{:S(2)}) collective-permute-start(f32[64,128]{1,0:T(8,128)S(1)} %get-tuple-element.145), channel_id=1, source_target_pairs={{32,64},{64,32},{33,65},{65,33},{34,66},{66,34},{35,67},{67,35},{3... | collective-permute-start | bytes 98312 | tf_op jit(solution)/shard_map/ppermute | solution.py:551
  26.4 6.7 %collective-permute-start.7 = (f32[64,128]{1,0:T(8,128)S(1)}, f32[64,128]{1,0:T(8,128)S(1)}, u32[]{:S(2)}, u32[]{:S(2)}) collective-permute-start(f32[64,128]{1,0:T(8,128)S(1)} %get-tuple-element.146), channel_id=1, source_target_pairs={{0,2},{2,0},{4,6},{6,4},{8,10},{10,8},{12,14},{14,12},{16,18},{18,... | collective-permute-start | bytes 98312 | tf_op jit(solution)/shard_map/ppermute | solution.py:553
  26.5 6.6 %collective-permute-start.8 = (f32[64,128]{1,0:T(8,128)S(1)}, f32[64,128]{1,0:T(8,128)S(1)}, u32[]{:S(2)}, u32[]{:S(2)}) collective-permute-start(f32[64,128]{1,0:T(8,128)S(1)} %get-tuple-element.147), channel_id=1, source_target_pairs={{2,4},{4,2},{6,8},{8,6},{10,12},{12,10},{14,16},{16,14},{18,20},{2... | collective-permute-start | bytes 98312 | tf_op jit(solution)/shard_map/ppermute | solution.py:550
  60.7 9.3 %collective-permute-start.14 = (f32[128,128]{1,0:T(8,128)S(1)}, f32[128,128]{1,0:T(8,128)S(1)}, u32[]{:S(2)}, u32[]{:S(2)}) collective-permute-start(f32[128,128]{1,0:T(8,128)S(1)} %get-tuple-element.183), channel_id=1, source_target_pairs={{0,1},{1,0},{2,3},{3,2},{4,5},{5,4},{6,7},{7,6},{8,9},{9,8},{10,11... | collective-permute-start | bytes 196616 | tf_op jit(solution)/shard_map/ppermute | solution.py:549
  61.9 8.1 %collective-permute-start.10 = (f32[32,128]{1,0:T(8,128)S(1)}, f32[32,128]{1,0:T(8,128)S(1)}, u32[]{:S(2)}, u32[]{:S(2)}) collective-permute-start(f32[32,128]{1,0:T(8,128)S(1)} %get-tuple-element.179), channel_id=1, source_target_pairs={{0,32},{32,0},{64,96},{96,64},{1,33},{33,1},{65,97},{97,65},{2,34}... | collective-permute-start | bytes 49160 | tf_op jit(solution)/shard_map/ppermute | solution.py:552
  62.2 7.8 %collective-permute-start.11 = (f32[32,128]{1,0:T(8,128)S(1)}, f32[32,128]{1,0:T(8,128)S(1)}, u32[]{:S(2)}, u32[]{:S(2)}) collective-permute-start(f32[32,128]{1,0:T(8,128)S(1)} %get-tuple-element.180), channel_id=1, source_target_pairs={{32,64},{64,32},{33,65},{65,33},{34,66},{66,34},{35,67},{67,35},{3... | collective-permute-start | bytes 49160 | tf_op jit(solution)/shard_map/ppermute | solution.py:551
  62.9 7.1 %collective-permute-start.12 = (f32[32,128]{1,0:T(8,128)S(1)}, f32[32,128]{1,0:T(8,128)S(1)}, u32[]{:S(2)}, u32[]{:S(2)}) collective-permute-start(f32[32,128]{1,0:T(8,128)S(1)} %get-tuple-element.181), channel_id=1, source_target_pairs={{0,2},{2,0},{4,6},{6,4},{8,10},{10,8},{12,14},{14,12},{16,18},{18,... | collective-permute-start | bytes 49160 | tf_op jit(solution)/shard_map/ppermute | solution.py:553
  64.0 6.0 %collective-permute-start.13 = (f32[32,128]{1,0:T(8,128)S(1)}, f32[32,128]{1,0:T(8,128)S(1)}, u32[]{:S(2)}, u32[]{:S(2)}) collective-permute-start(f32[32,128]{1,0:T(8,128)S(1)} %get-tuple-element.182), channel_id=1, source_target_pairs={{2,4},{4,2},{6,8},{8,6},{10,12},{12,10},{14,16},{16,14},{18,20},{2... | collective-permute-start | bytes 49160 | tf_op jit(solution)/shard_map/ppermute | solution.py:550
  71.2 12.1 %collective-permute-start.19 = (f32[256,128]{1,0:T(8,128)S(1)}, f32[256,128]{1,0:T(8,128)S(1)}, u32[]{:S(2)}, u32[]{:S(2)}) collective-permute-start(f32[256,128]{1,0:T(8,128)S(1)} %get-tuple-element.202), channel_id=1, source_target_pairs={{0,1},{1,0},{2,3},{3,2},{4,5},{5,4},{6,7},{7,6},{8,9},{9,8},{10,11... | collective-permute-start | bytes 393224 | tf_op jit(solution)/shard_map/ppermute | solution.py:549
  73.0 10.2 %collective-permute-start.15 = (f32[64,128]{1,0:T(8,128)S(1)}, f32[64,128]{1,0:T(8,128)S(1)}, u32[]{:S(2)}, u32[]{:S(2)}) collective-permute-start(f32[64,128]{1,0:T(8,128)S(1)} %get-tuple-element.198), channel_id=1, source_target_pairs={{0,32},{32,0},{64,96},{96,64},{1,33},{33,1},{65,97},{97,65},{2,34}... | collective-permute-start | bytes 98312 | tf_op jit(solution)/shard_map/ppermute | solution.py:552
  75.9 7.4 %collective-permute-start.16 = (f32[64,128]{1,0:T(8,128)S(1)}, f32[64,128]{1,0:T(8,128)S(1)}, u32[]{:S(2)}, u32[]{:S(2)}) collective-permute-start(f32[64,128]{1,0:T(8,128)S(1)} %get-tuple-element.199), channel_id=1, source_target_pairs={{32,64},{64,32},{33,65},{65,33},{34,66},{66,34},{35,67},{67,35},{3... | collective-permute-start | bytes 98312 | tf_op jit(solution)/shard_map/ppermute | solution.py:551
  76.5 6.7 %collective-permute-start.17 = (f32[64,128]{1,0:T(8,128)S(1)}, f32[64,128]{1,0:T(8,128)S(1)}, u32[]{:S(2)}, u32[]{:S(2)}) collective-permute-start(f32[64,128]{1,0:T(8,128)S(1)} %get-tuple-element.200), channel_id=1, source_target_pairs={{0,2},{2,0},{4,6},{6,4},{8,10},{10,8},{12,14},{14,12},{16,18},{18,... | collective-permute-start | bytes 98312 | tf_op jit(solution)/shard_map/ppermute | solution.py:553
  76.6 6.7 %collective-permute-start.18 = (f32[64,128]{1,0:T(8,128)S(1)}, f32[64,128]{1,0:T(8,128)S(1)}, u32[]{:S(2)}, u32[]{:S(2)}) collective-permute-start(f32[64,128]{1,0:T(8,128)S(1)} %get-tuple-element.201), channel_id=1, source_target_pairs={{2,4},{4,2},{6,8},{8,6},{10,12},{12,10},{14,16},{16,14},{18,20},{2... | collective-permute-start | bytes 98312 | tf_op jit(solution)/shard_map/ppermute | solution.py:550

commit v4 on v3

--- a/solution.py
+++ b/solution.py
@@ -223,7 +223,8 @@
 def places():
     x, y, z = (lax.axis_index(a) for a in AXES)
     more = [i < lax.axis_size(a) - 1 for a, i in zip(AXES, (x, y, z))]
-    return x % 2 == 0, y % 2 == 0, z == 0, more
+    less = [i > 0 for i in (x, y, z)]
+    return (x % 2 == 0, y % 2 == 0, z == 0), more, less
 
 
 def pick(flag, a, b):
@@ -231,7 +232,7 @@
 
 
 def pack_sends(sends, faces, index):
-    xeven, yeven, zlow, _ = places()
+    (xeven, yeven, zlow), _, _ = places()
     xa, xb, ya, yb, zz = sends
     for even, a, b, lo, hi in ((xeven, xa, xb, faces[0], faces[1]), (yeven, ya, yb, faces[2], faces[3])):
         s = slice(index * CZ, (index + 1) * CZ)
@@ -315,7 +316,7 @@
 
 
 def jumps(own, got, bases, prev_bases, back_bases, n, lifted):
-    xeven, yeven, zlow, more = places()
+    (xeven, yeven, zlow), more, less = places()
     xa, xb, ya, yb, zz = got
     for d, (even, a, b, rows) in enumerate(((xeven, xa, xb, n * CZ), (yeven, ya, yb, n * CZ), (zlow, zz, zz, n * C))):
         a = a[0:rows, :]
@@ -323,9 +324,7 @@
         up = own[2 * d + 1][...] - dot(pick(even, a, b), bases, d)
         up = jnp.where(more[d], up, 0.0)
         down = pick(even, b, a) - dot(own[2 * d][...], prev_bases, d)
-        back = -dot(down, back_bases, d)
-        if d == 2:
-            back = jnp.where(zlow, 0.0, back)
+        back = jnp.where(less[d], -dot(down, back_bases, d), 0.0)
         size = rows // n
         for i in range(n):
             lifted[i][2 * d][...] = back[i * size : (i + 1) * size, :]
@@ -359,7 +358,7 @@
     if first:
         prev, back = take(2)
     (turn,) = take(1)
-    xeven, yeven, zlow, _ = places()
+    (xeven, yeven, _), _, _ = places()
     if first:
         xa, xb, ya, yb, zz = got
         for d, base in enumerate((pick(xeven, xb[CZ:, :], xa[CZ:, :]), pick(yeven, yb[CZ:, :], ya[CZ:, :]), zz[C:, :])):
@@ -539,8 +538,9 @@
 def swap_pairs(axis, start):
     n = lax.axis_size(axis)
     pairs = []
-    for i in range(start, n - 1, 2):
-        pairs += [(i, i + 1), (i + 1, i)]
+    for i in range(start, n, 2):
+        j = (i + 1) % n
+        pairs += [(i, j), (j, i)]
     return pairs
 
 

time: 105 us -> 91.9 us (0.88)
  starting transfers between devices: 34.1 us -> 26.5 us
  blocking collectives: 39 us -> 32.2 us
  waiting for transfers between devices: 0.05 us -> 1.52 us
    ppermute x4, starting transfers between devices: 13.7 us -> 2.08 us  [exchange(): yb = lax.ppermute(yb, 'gy', swap_pairs('gy', 1))]
    ppermute x4, starting transfers between devices: 2.66 us -> 10 us  [exchange(): ya = lax.ppermute(ya, 'gy', swap_pairs('gy', 0))]
    all_to_all x2, blocking collectives: 39 us -> 32.2 us  [gather_rows(): rows = lax.all_to_all(rows.reshape(C, 1, C), AXES, 0, 0)]
    ppermute x4, starting transfers between devices: 8.33 us -> 2.43 us  [exchange(): xa = lax.ppermute(xa, 'gx', swap_pairs('gx', 0))]
    ppermute x4, starting transfers between devices: 2.61 us -> 4.61 us  [exchange(): xb = lax.ppermute(xb, 'gx', swap_pairs('gx', 1))]
    ppermute x4, waiting for transfers between devices: 0.01 us -> 1.48 us  [exchange(): yb = lax.ppermute(yb, 'gy', swap_pairs('gy', 1))]
  transfers between devices with their start and end apart: 20 -> 20, of which waited for: 0 -> 2; matrix products, arithmetic and copies ran while one was open for 0% -> 0% of each run, Pallas kernels for 13% -> 14%
where the time goes in v4:
time: 91.9 us; the launch traced here: 91.7 us
  blocking collectives  32.2 us (35%)
  Pallas kernels  30.5 us (33%)
  starting transfers between devices  26.5 us (29%)
  waiting for transfers between devices  1.52 us (2%)
  between operations  0.99 us (1%)
    all_to_all x2, blocking collectives, gather_rows(): rows = lax.all_to_all(rows.reshape(C, 1, C), AXES, 0, 0)  32.2 us
    pallas_call x11, Pallas kernels, call(): pl.pallas_call(kernel, out_shape=tuple(outs), in_specs=in_specs or [VM] *...  30.5 us
    ppermute x4, starting transfers between devices, exchange(): ya = lax.ppermute(ya, 'gy', swap_pairs('gy', 0))  10 us
    ppermute x4, starting transfers between devices, exchange(): zz = lax.ppermute(zz, 'gz', swap_pairs('gz', 0))  7.41 us
    ppermute x4, starting transfers between devices, exchange(): xb = lax.ppermute(xb, 'gx', swap_pairs('gx', 1))  4.61 us
    ppermute x4, starting transfers between devices, exchange(): xa = lax.ppermute(xa, 'gx', swap_pairs('gx', 0))  2.43 us
    ppermute x4, starting transfers between devices, exchange(): yb = lax.ppermute(yb, 'gy', swap_pairs('gy', 1))  2.08 us
  transfers between devices with their start and end apart: 20, of which 2 were waited for; matrix products, arithmetic and copies ran while one was open for 0% of the time, Pallas kernels for 14%

profile of v4, /device:TPU:1, one launch (start us, length us, event | category | flops | bytes accessed | tf_op | source)
XLA Modules:
  0.0 91.7 jit_solution(7911548366179588393)
XLA Ops:
  0.6 4.9 %first.1 = (f32[32,128,128]{2,1,0:T(8,128)S(1)}, f32[34,144,128]{2,1,0:T(8,128)S(1)}, bf16[9,128,128]{2,1,0:T(8,128)(2,1)S(1)}, f32[32,128,128]{2,1,0:T(8,128)S(...) custom-call(f32[32,128,128]{2,1,0:T(8,128)} %heat_in.1, ...), custom_call_target="tpu_custom_call" | custom-call | flops 40000000 | bytes 1048576 | tf_op jit(solution)/shard_map/first/pallas_call | solution.py:525
  5.6 3.6 %collective-permute-start.4 = (f32[256,128]{1,0:T(8,128)S(1)}, f32[256,128]{1,0:T(8,128)S(1)}, u32[]{:S(2)}, u32[]{:S(2)}) collective-permute-start(f32[256,128]{1,0:T(8,128)S(1)} %get-tuple-element.125), channel_id=1, source_target_pairs={{0,1},{1,0},{2,3},{3,2},{4,5},{5,4},{6,7},{7,6},{8,9},{9,8},{10,11... | collective-permute-start | bytes 393224 | tf_op jit(solution)/shard_map/ppermute | solution.py:549
  9.2 1.3 %collective-permute-start = (f32[160,128]{1,0:T(8,128)S(1)}, f32[160,128]{1,0:T(8,128)S(1)}, u32[]{:S(2)}, u32[]{:S(2)}) collective-permute-start(f32[160,128]{1,0:T(8,128)S(1)} %get-tuple-element.121), channel_id=1, source_target_pairs={{0,32},{32,0},{64,96},{96,64},{1,33},{33,1},{65,97},{97,65},{2,34}... | collective-permute-start | bytes 245768 | tf_op jit(solution)/shard_map/ppermute | solution.py:552
  10.5 1.9 %collective-permute-start.1 = (f32[160,128]{1,0:T(8,128)S(1)}, f32[160,128]{1,0:T(8,128)S(1)}, u32[]{:S(2)}, u32[]{:S(2)}) collective-permute-start(f32[160,128]{1,0:T(8,128)S(1)} %get-tuple-element.122), channel_id=1, source_target_pairs={{32,64},{64,32},{96,0},{0,96},{33,65},{65,33},{97,1},{1,97},{34,66... | collective-permute-start | bytes 245768 | tf_op jit(solution)/shard_map/ppermute | solution.py:551
  12.4 1.5 %collective-permute-start.2 = (f32[160,128]{1,0:T(8,128)S(1)}, f32[160,128]{1,0:T(8,128)S(1)}, u32[]{:S(2)}, u32[]{:S(2)}) collective-permute-start(f32[160,128]{1,0:T(8,128)S(1)} %get-tuple-element.123), channel_id=1, source_target_pairs={{0,2},{2,0},{4,6},{6,4},{8,10},{10,8},{12,14},{14,12},{16,18},{18,... | collective-permute-start | bytes 245768 | tf_op jit(solution)/shard_map/ppermute | solution.py:553
  13.9 1.5 %collective-permute-start.3 = (f32[160,128]{1,0:T(8,128)S(1)}, f32[160,128]{1,0:T(8,128)S(1)}, u32[]{:S(2)}, u32[]{:S(2)}) collective-permute-start(f32[160,128]{1,0:T(8,128)S(1)} %get-tuple-element.124), channel_id=1, source_target_pairs={{2,4},{4,2},{6,8},{8,6},{10,12},{12,10},{14,16},{16,14},{18,20},{2... | collective-permute-start | bytes 245768 | tf_op jit(solution)/shard_map/ppermute | solution.py:550
  15.4 4.3 %free.2 = (f32[34,144,128]{2,1,0:T(8,128)S(1)}, f32[32,128]{1,0:T(8,128)S(1)}, f32[32,128]{1,0:T(8,128)S(1)}, f32[32,128]{1,0:T(8,128)S(1)}, f32[32,128]{1,0:T(8...) custom-call(f32[34,144,128]{2,1,0:T(8,128)S(1)} %get-tuple-element.1, ...), custom_call_target="tpu_custom_call" | custom-call | flops 30000000 | bytes 1048576 | tf_op jit(solution)/shard_map/free/pallas_call | solution.py:525
  19.8 1.3 %second.2 = (f32[32,128]{1,0:T(8,128)S(1)}, f32[32,128]{1,0:T(8,128)S(1)}, f32[32,128]{1,0:T(8,128)S(1)}, f32[32,128]{1,0:T(8,128)S(1)}, f32[128,128]{1,0:T(8,12...) custom-call(f32[32,128]{1,0:T(8,128)S(1)} %get-tuple-element.115.ref, ...), custom_call_target="tpu_custom_call" | custom-call | flops 20000000 | bytes 1048576 | tf_op jit(solution)/shard_map/second/pallas_call | solution.py:525
  21.4 0.4 collective-permute-start.5
  21.8 0.4 collective-permute-start.6
  22.2 4.9 %collective-permute-start.7 = (f32[64,128]{1,0:T(8,128)S(1)}, f32[64,128]{1,0:T(8,128)S(1)}, u32[]{:S(2)}, u32[]{:S(2)}) collective-permute-start(f32[64,128]{1,0:T(8,128)S(1)} %get-tuple-element.146), channel_id=1, source_target_pairs={{0,2},{2,0},{4,6},{6,4},{8,10},{10,8},{12,14},{14,12},{16,18},{18,... | collective-permute-start | bytes 98312 | tf_op jit(solution)/shard_map/ppermute | solution.py:553
  27.1 2.7 %response.2 = (f32[34,144,128]{2,1,0:T(8,128)S(1)}, f32[1,128]{1,0:T(1,128)S(1)}) custom-call(f32[32,128]{1,0:T(8,128)S(1)} %get-tuple-element.151.refs_0_.refs_5_, f32[32,128]{1,0:T(8,128)S(1)} %get-tuple-element.152.refs_1_.refs_6_, f32[32,128]{1,0:T(8,128)S(1)} %get-tuple-element.153.refs_2_.refs_7_, f32[32,128]{1,0:T(8,128)S(1)} %get-tuple-element.154.refs_3_.refs_8_, ...), custom_call_target="tpu_custom_call" | custom-call | flops 30000000 | bytes 1048576 | tf_op jit(solution)/shard_map/response/pallas_call | solution.py:525
  29.8 0.9 %collective-permute-done.8.refs_9_ = f32[64,128]{1,0:T(8,128)S(1)} collective-permute-done((f32[64,128]{1,0:T(8,128)S(1)}, f32[64,128]{1,0:T(8,128)S(1)}, u32[]{:S(2)}, u32[]{:S(2)}) %collective-permute-start.8) | collective-permute-done | bytes 32800 | tf_op jit(solution)/shard_map/ppermute | solution.py:550
  30.8 1.5 %third.2 = (f32[32,128]{1,0:T(8,128)S(1)}, f32[32,128]{1,0:T(8,128)S(1)}, f32[128,128]{1,0:T(8,128)S(1)}, f32[32,128]{1,0:T(8,128)S(1)}, f32[32,128]{1,0:T(8,128...) custom-call(f32[64,128]{1,0:T(8,128)S(1)} %get-tuple-element.138.ref, ...), custom_call_target="tpu_custom_call" | custom-call | flops 20000000 | bytes 1048576 | tf_op jit(solution)/shard_map/third/pallas_call | solution.py:525
  32.3 17.2 %all_to_all.10 = f32[128,1,128]{2,1,0:T(1,128)S(1)} all-to-all(f32[128,1,128]{2,1,0:T(1,128)S(1)} %bitcast.15), channel_id=1, replica_groups=mesh['gx'=4,'gy'=16,'gz'=2] {'gx','gy','gz'}, dimensions={0} | all-to-all | bytes 131072 | tf_op jit(solution)/shard_map/all_to_all | solution.py:558
  49.4 4.8 %fourth.1 = (f32[32,128,128]{2,1,0:T(8,128)S(1)}, f32[34,144,128]{2,1,0:T(8,128)S(1)}, f32[32,128]{1,0:T(8,128)S(1)}, f32[32,128]{1,0:T(8,128)S(1)}, f32[128,128...) custom-call(f32[128,128]{1,0:T(8,128)S(1)} %bitcast.13, ...), custom_call_target="tpu_custom_call" | custom-call | flops 50000000 | bytes 1048576 | tf_op jit(solution)/shard_map/fourth/pallas_call | solution.py:525
  54.3 1.1 %collective-permute-start.14 = (f32[128,128]{1,0:T(8,128)S(1)}, f32[128,128]{1,0:T(8,128)S(1)}, u32[]{:S(2)}, u32[]{:S(2)}) collective-permute-start(f32[128,128]{1,0:T(8,128)S(1)} %get-tuple-element.183), channel_id=1, source_target_pairs={{0,1},{1,0},{2,3},{3,2},{4,5},{5,4},{6,7},{7,6},{8,9},{9,8},{10,11... | collective-permute-start | bytes 196616 | tf_op jit(solution)/shard_map/ppermute | solution.py:549
  55.4 0.4 collective-permute-start.10
  55.7 0.5 collective-permute-start.11
  56.2 1.3 %collective-permute-start.12 = (f32[32,128]{1,0:T(8,128)S(1)}, f32[32,128]{1,0:T(8,128)S(1)}, u32[]{:S(2)}, u32[]{:S(2)}) collective-permute-start(f32[32,128]{1,0:T(8,128)S(1)} %get-tuple-element.181), channel_id=1, source_target_pairs={{0,2},{2,0},{4,6},{6,4},{8,10},{10,8},{12,14},{14,12},{16,18},{18,... | collective-permute-start | bytes 49160 | tf_op jit(solution)/shard_map/ppermute | solution.py:553
  57.5 0.4 collective-permute-start.13
  58.0 3.6 %free.3 = (f32[34,144,128]{2,1,0:T(8,128)S(1)}, f32[32,128]{1,0:T(8,128)S(1)}, f32[32,128]{1,0:T(8,128)S(1)}, f32[32,128]{1,0:T(8,128)S(1)}, f32[32,128]{1,0:T(8...) custom-call(f32[34,144,128]{2,1,0:T(8,128)S(1)} %get-tuple-element.184.state, ...), custom_call_target="tpu_custom_call" | custom-call | flops 30000000 | bytes 1048576 | tf_op jit(solution)/shard_map/free/pallas_call | solution.py:525
  61.6 1.2 %second.3 = (f32[32,128]{1,0:T(8,128)S(1)}, f32[32,128]{1,0:T(8,128)S(1)}, f32[32,128]{1,0:T(8,128)S(1)}, f32[32,128]{1,0:T(8,128)S(1)}, f32[128,128]{1,0:T(8,12...) custom-call(f32[32,128]{1,0:T(8,128)S(1)} %get-tuple-element.173.ref, ...), custom_call_target="tpu_custom_call" | custom-call | flops 20000000 | bytes 1048576 | tf_op jit(solution)/shard_map/second/pallas_call | solution.py:525
  62.8 2.3 %collective-permute-start.19 = (f32[256,128]{1,0:T(8,128)S(1)}, f32[256,128]{1,0:T(8,128)S(1)}, u32[]{:S(2)}, u32[]{:S(2)}) collective-permute-start(f32[256,128]{1,0:T(8,128)S(1)} %get-tuple-element.202), channel_id=1, source_target_pairs={{0,1},{1,0},{2,3},{3,2},{4,5},{5,4},{6,7},{7,6},{8,9},{9,8},{10,11... | collective-permute-start | bytes 393224 | tf_op jit(solution)/shard_map/ppermute | solution.py:549
  65.1 0.4 collective-permute-start.15
  65.5 1.9 %collective-permute-start.16 = (f32[64,128]{1,0:T(8,128)S(1)}, f32[64,128]{1,0:T(8,128)S(1)}, u32[]{:S(2)}, u32[]{:S(2)}) collective-permute-start(f32[64,128]{1,0:T(8,128)S(1)} %get-tuple-element.199), channel_id=1, source_target_pairs={{32,64},{64,32},{96,0},{0,96},{33,65},{65,33},{97,1},{1,97},{34,66... | collective-permute-start | bytes 98312 | tf_op jit(solution)/shard_map/ppermute | solution.py:551
  67.3 2.2 %collective-permute-start.17 = (f32[64,128]{1,0:T(8,128)S(1)}, f32[64,128]{1,0:T(8,128)S(1)}, u32[]{:S(2)}, u32[]{:S(2)}) collective-permute-start(f32[64,128]{1,0:T(8,128)S(1)} %get-tuple-element.200), channel_id=1, source_target_pairs={{0,2},{2,0},{4,6},{6,4},{8,10},{10,8},{12,14},{14,12},{16,18},{18,... | collective-permute-start | bytes 98312 | tf_op jit(solution)/shard_map/ppermute | solution.py:553
  69.7 2.7 %response.3 = (f32[34,144,128]{2,1,0:T(8,128)S(1)}, f32[1,128]{1,0:T(1,128)S(1)}) custom-call(f32[32,128]{1,0:T(8,128)S(1)} %get-tuple-element.203.refs_0_, f32[32,128]{1,0:T(8,128)S(1)} %get-tuple-element.204.refs_1_.refs_6_, f32[32,128]{1,0:T(8,128)S(1)} %get-tuple-element.205.refs_2_, f32[32,128]{1,0:T(8,128)S(1)} %get-tuple-element.206.refs_3_.refs_7_, ...), custom_call_target="tpu_custom_call" | custom-call | flops 30000000 | bytes 1048576 | tf_op jit(solution)/shard_map/response/pallas_call | solution.py:525
  72.4 0.5 collective-permute-done.18.refs_9_
  72.9 1.5 %third.3 = (f32[32,128]{1,0:T(8,128)S(1)}, f32[32,128]{1,0:T(8,128)S(1)}, f32[128,128]{1,0:T(8,128)S(1)}, f32[32,128]{1,0:T(8,128)S(1)}, f32[32,128]{1,0:T(8,128...) custom-call(f32[64,128]{1,0:T(8,128)S(1)} %get-tuple-element.192.refs_0_, ...), custom_call_target="tpu_custom_call" | custom-call | flops 20000000 | bytes 1048576 | tf_op jit(solution)/shard_map/third/pallas_call | solution.py:525
  74.4 15.0 %all_to_all.11 = f32[128,1,128]{2,1,0:T(1,128)S(1)} all-to-all(f32[128,1,128]{2,1,0:T(1,128)S(1)} %bitcast.16), channel_id=1, replica_groups=mesh['gx'=4,'gy'=16,'gz'=2] {'gx','gy','gz'}, dimensions={0} | all-to-all | bytes 131072 | tf_op jit(solution)/shard_map/all_to_all | solution.py:558
  89.4 2.2 %last.1 = (f32[32,128,128]{2,1,0:T(8,128)}, f32[32,128]{1,0:T(8,128)}, f32[32,128]{1,0:T(8,128)}, f32[128,128]{1,0:T(8,128)}) custom-call(f32[128,128]{1,0:T(8,128)S(1)} %bitcast.14, f32[34,144,128]{2,1,0:T(8,128)S(1)} %get-tuple-element.211.refs_1_, f32[34,144,128]{2,1,0:T(8,128)S(1)} %get-tuple-element.212.refs_2_, ...), custom_call_target="tpu_custom_call" | custom-call | flops 20000000 | bytes 1048576 | tf_op jit(solution)/shard_map/last/pallas_call | solution.py:525
  (21 shorter events, 0.5 us)
Async XLA Ops:
  5.6 14.3 %collective-permute-start.4 = (f32[256,128]{1,0:T(8,128)S(1)}, f32[256,128]{1,0:T(8,128)S(1)}, u32[]{:S(2)}, u32[]{:S(2)}) collective-permute-start(f32[256,128]{1,0:T(8,128)S(1)} %get-tuple-element.125), channel_id=1, source_target_pairs={{0,1},{1,0},{2,3},{3,2},{4,5},{5,4},{6,7},{7,6},{8,9},{9,8},{10,11... | collective-permute-start | bytes 393224 | tf_op jit(solution)/shard_map/ppermute | solution.py:549
  9.2 10.6 %collective-permute-start = (f32[160,128]{1,0:T(8,128)S(1)}, f32[160,128]{1,0:T(8,128)S(1)}, u32[]{:S(2)}, u32[]{:S(2)}) collective-permute-start(f32[160,128]{1,0:T(8,128)S(1)} %get-tuple-element.121), channel_id=1, source_target_pairs={{0,32},{32,0},{64,96},{96,64},{1,33},{33,1},{65,97},{97,65},{2,34}... | collective-permute-start | bytes 245768 | tf_op jit(solution)/shard_map/ppermute | solution.py:552
  10.5 9.3 %collective-permute-start.1 = (f32[160,128]{1,0:T(8,128)S(1)}, f32[160,128]{1,0:T(8,128)S(1)}, u32[]{:S(2)}, u32[]{:S(2)}) collective-permute-start(f32[160,128]{1,0:T(8,128)S(1)} %get-tuple-element.122), channel_id=1, source_target_pairs={{32,64},{64,32},{96,0},{0,96},{33,65},{65,33},{97,1},{1,97},{34,66... | collective-permute-start | bytes 245768 | tf_op jit(solution)/shard_map/ppermute | solution.py:551
  12.4 7.4 %collective-permute-start.2 = (f32[160,128]{1,0:T(8,128)S(1)}, f32[160,128]{1,0:T(8,128)S(1)}, u32[]{:S(2)}, u32[]{:S(2)}) collective-permute-start(f32[160,128]{1,0:T(8,128)S(1)} %get-tuple-element.123), channel_id=1, source_target_pairs={{0,2},{2,0},{4,6},{6,4},{8,10},{10,8},{12,14},{14,12},{16,18},{18,... | collective-permute-start | bytes 245768 | tf_op jit(solution)/shard_map/ppermute | solution.py:553
  13.9 5.9 %collective-permute-start.3 = (f32[160,128]{1,0:T(8,128)S(1)}, f32[160,128]{1,0:T(8,128)S(1)}, u32[]{:S(2)}, u32[]{:S(2)}) collective-permute-start(f32[160,128]{1,0:T(8,128)S(1)} %get-tuple-element.124), channel_id=1, source_target_pairs={{2,4},{4,2},{6,8},{8,6},{10,12},{12,10},{14,16},{16,14},{18,20},{2... | collective-permute-start | bytes 245768 | tf_op jit(solution)/shard_map/ppermute | solution.py:550
  21.1 9.7 %collective-permute-start.9 = (f32[256,128]{1,0:T(8,128)S(1)}, f32[256,128]{1,0:T(8,128)S(1)}, u32[]{:S(2)}, u32[]{:S(2)}) collective-permute-start(f32[256,128]{1,0:T(8,128)S(1)} %get-tuple-element.148), channel_id=1, source_target_pairs={{0,1},{1,0},{2,3},{3,2},{4,5},{5,4},{6,7},{7,6},{8,9},{9,8},{10,11... | collective-permute-start | bytes 393224 | tf_op jit(solution)/shard_map/ppermute | solution.py:549
  21.4 8.4 %collective-permute-start.5 = (f32[64,128]{1,0:T(8,128)S(1)}, f32[64,128]{1,0:T(8,128)S(1)}, u32[]{:S(2)}, u32[]{:S(2)}) collective-permute-start(f32[64,128]{1,0:T(8,128)S(1)} %get-tuple-element.144), channel_id=1, source_target_pairs={{0,32},{32,0},{64,96},{96,64},{1,33},{33,1},{65,97},{97,65},{2,34}... | collective-permute-start | bytes 98312 | tf_op jit(solution)/shard_map/ppermute | solution.py:552
  21.8 8.0 %collective-permute-start.6 = (f32[64,128]{1,0:T(8,128)S(1)}, f32[64,128]{1,0:T(8,128)S(1)}, u32[]{:S(2)}, u32[]{:S(2)}) collective-permute-start(f32[64,128]{1,0:T(8,128)S(1)} %get-tuple-element.145), channel_id=1, source_target_pairs={{32,64},{64,32},{96,0},{0,96},{33,65},{65,33},{97,1},{1,97},{34,66... | collective-permute-start | bytes 98312 | tf_op jit(solution)/shard_map/ppermute | solution.py:551
  22.2 7.6 %collective-permute-start.7 = (f32[64,128]{1,0:T(8,128)S(1)}, f32[64,128]{1,0:T(8,128)S(1)}, u32[]{:S(2)}, u32[]{:S(2)}) collective-permute-start(f32[64,128]{1,0:T(8,128)S(1)} %get-tuple-element.146), channel_id=1, source_target_pairs={{0,2},{2,0},{4,6},{6,4},{8,10},{10,8},{12,14},{14,12},{16,18},{18,... | collective-permute-start | bytes 98312 | tf_op jit(solution)/shard_map/ppermute | solution.py:553
  27.1 3.6 %collective-permute-start.8 = (f32[64,128]{1,0:T(8,128)S(1)}, f32[64,128]{1,0:T(8,128)S(1)}, u32[]{:S(2)}, u32[]{:S(2)}) collective-permute-start(f32[64,128]{1,0:T(8,128)S(1)} %get-tuple-element.147), channel_id=1, source_target_pairs={{2,4},{4,2},{6,8},{8,6},{10,12},{12,10},{14,16},{16,14},{18,20},{2... | collective-permute-start | bytes 98312 | tf_op jit(solution)/shard_map/ppermute | solution.py:550
  54.3 7.3 %collective-permute-start.14 = (f32[128,128]{1,0:T(8,128)S(1)}, f32[128,128]{1,0:T(8,128)S(1)}, u32[]{:S(2)}, u32[]{:S(2)}) collective-permute-start(f32[128,128]{1,0:T(8,128)S(1)} %get-tuple-element.183), channel_id=1, source_target_pairs={{0,1},{1,0},{2,3},{3,2},{4,5},{5,4},{6,7},{7,6},{8,9},{9,8},{10,11... | collective-permute-start | bytes 196616 | tf_op jit(solution)/shard_map/ppermute | solution.py:549
  55.4 6.1 %collective-permute-start.10 = (f32[32,128]{1,0:T(8,128)S(1)}, f32[32,128]{1,0:T(8,128)S(1)}, u32[]{:S(2)}, u32[]{:S(2)}) collective-permute-start(f32[32,128]{1,0:T(8,128)S(1)} %get-tuple-element.179), channel_id=1, source_target_pairs={{0,32},{32,0},{64,96},{96,64},{1,33},{33,1},{65,97},{97,65},{2,34}... | collective-permute-start | bytes 49160 | tf_op jit(solution)/shard_map/ppermute | solution.py:552
  55.7 5.8 %collective-permute-start.11 = (f32[32,128]{1,0:T(8,128)S(1)}, f32[32,128]{1,0:T(8,128)S(1)}, u32[]{:S(2)}, u32[]{:S(2)}) collective-permute-start(f32[32,128]{1,0:T(8,128)S(1)} %get-tuple-element.180), channel_id=1, source_target_pairs={{32,64},{64,32},{96,0},{0,96},{33,65},{65,33},{97,1},{1,97},{34,66... | collective-permute-start | bytes 49160 | tf_op jit(solution)/shard_map/ppermute | solution.py:551
  56.2 5.3 %collective-permute-start.12 = (f32[32,128]{1,0:T(8,128)S(1)}, f32[32,128]{1,0:T(8,128)S(1)}, u32[]{:S(2)}, u32[]{:S(2)}) collective-permute-start(f32[32,128]{1,0:T(8,128)S(1)} %get-tuple-element.181), channel_id=1, source_target_pairs={{0,2},{2,0},{4,6},{6,4},{8,10},{10,8},{12,14},{14,12},{16,18},{18,... | collective-permute-start | bytes 49160 | tf_op jit(solution)/shard_map/ppermute | solution.py:553
  57.5 4.0 %collective-permute-start.13 = (f32[32,128]{1,0:T(8,128)S(1)}, f32[32,128]{1,0:T(8,128)S(1)}, u32[]{:S(2)}, u32[]{:S(2)}) collective-permute-start(f32[32,128]{1,0:T(8,128)S(1)} %get-tuple-element.182), channel_id=1, source_target_pairs={{2,4},{4,2},{6,8},{8,6},{10,12},{12,10},{14,16},{16,14},{18,20},{2... | collective-permute-start | bytes 49160 | tf_op jit(solution)/shard_map/ppermute | solution.py:550
  62.8 10.1 %collective-permute-start.19 = (f32[256,128]{1,0:T(8,128)S(1)}, f32[256,128]{1,0:T(8,128)S(1)}, u32[]{:S(2)}, u32[]{:S(2)}) collective-permute-start(f32[256,128]{1,0:T(8,128)S(1)} %get-tuple-element.202), channel_id=1, source_target_pairs={{0,1},{1,0},{2,3},{3,2},{4,5},{5,4},{6,7},{7,6},{8,9},{9,8},{10,11... | collective-permute-start | bytes 393224 | tf_op jit(solution)/shard_map/ppermute | solution.py:549
  65.1 7.3 %collective-permute-start.15 = (f32[64,128]{1,0:T(8,128)S(1)}, f32[64,128]{1,0:T(8,128)S(1)}, u32[]{:S(2)}, u32[]{:S(2)}) collective-permute-start(f32[64,128]{1,0:T(8,128)S(1)} %get-tuple-element.198), channel_id=1, source_target_pairs={{0,32},{32,0},{64,96},{96,64},{1,33},{33,1},{65,97},{97,65},{2,34}... | collective-permute-start | bytes 98312 | tf_op jit(solution)/shard_map/ppermute | solution.py:552
  65.5 6.9 %collective-permute-start.16 = (f32[64,128]{1,0:T(8,128)S(1)}, f32[64,128]{1,0:T(8,128)S(1)}, u32[]{:S(2)}, u32[]{:S(2)}) collective-permute-start(f32[64,128]{1,0:T(8,128)S(1)} %get-tuple-element.199), channel_id=1, source_target_pairs={{32,64},{64,32},{96,0},{0,96},{33,65},{65,33},{97,1},{1,97},{34,66... | collective-permute-start | bytes 98312 | tf_op jit(solution)/shard_map/ppermute | solution.py:551
  67.3 5.0 %collective-permute-start.17 = (f32[64,128]{1,0:T(8,128)S(1)}, f32[64,128]{1,0:T(8,128)S(1)}, u32[]{:S(2)}, u32[]{:S(2)}) collective-permute-start(f32[64,128]{1,0:T(8,128)S(1)} %get-tuple-element.200), channel_id=1, source_target_pairs={{0,2},{2,0},{4,6},{6,4},{8,10},{10,8},{12,14},{14,12},{16,18},{18,... | collective-permute-start | bytes 98312 | tf_op jit(solution)/shard_map/ppermute | solution.py:553
  69.6 3.3 %collective-permute-start.18 = (f32[64,128]{1,0:T(8,128)S(1)}, f32[64,128]{1,0:T(8,128)S(1)}, u32[]{:S(2)}, u32[]{:S(2)}) collective-permute-start(f32[64,128]{1,0:T(8,128)S(1)} %get-tuple-element.201), channel_id=1, source_target_pairs={{2,4},{4,2},{6,8},{8,6},{10,12},{12,10},{14,16},{16,14},{18,20},{2... | collective-permute-start | bytes 98312 | tf_op jit(solution)/shard_map/ppermute | solution.py:550

commit v5 on v4

--- a/solution.py
+++ b/solution.py
@@ -16,9 +16,9 @@
 F32 = jnp.float32
 UNROLL = 4
 WIDE = 16
-PARTS = 4
 BLOCK = 16
 DEPTH = 8
+PARTS = CZ // DEPTH
 KEPT = 1.0 - DAMPING_WEIGHT
 
 VM = pl.BlockSpec(memory_space=pltpu.MemorySpace.VMEM)
@@ -83,22 +83,25 @@
     return near + jnp.where(lanes == C - 1, 0.0, pltpu.roll(centre, C - 1, 1))
 
 
-def sweep(src, dst, weight, supply):
+def sweep_planes(src, dst, weight, supply, i):
     lanes = lane_of((BLOCK, C))
     low = lanes == 0
     high = lanes == C - 1
-
+    z = i * DEPTH
+    for x in range(0, C, BLOCK):
+        r = PAD + x
+        column = [src[z + j, r : r + BLOCK, :] for j in range(DEPTH + 2)]
+        for j in range(DEPTH):
+            centre = column[j + 1]
+            near = column[j] + column[j + 2]
+            near = near + src[z + j + 1, r - 1 : r - 1 + BLOCK, :] + src[z + j + 1, r + 1 : r + 1 + BLOCK, :]
+            near = near + jnp.where(low, 0.0, pltpu.roll(centre, 1, 1)) + jnp.where(high, 0.0, pltpu.roll(centre, C - 1, 1))
+            dst[z + j + 1, r : r + BLOCK, :] = KEPT * centre + weight[z + j, x : x + BLOCK, :] * (supply[z + j, x : x + BLOCK, :] + near)
+
+
+def sweep(src, dst, weight, supply):
     def planes(i, carry):
-        z = i * DEPTH
-        for x in range(0, C, BLOCK):
-            r = PAD + x
-            column = [src[z + j, r : r + BLOCK, :] for j in range(DEPTH + 2)]
-            for j in range(DEPTH):
-                centre = column[j + 1]
-                near = column[j] + column[j + 2]
-                near = near + src[z + j + 1, r - 1 : r - 1 + BLOCK, :] + src[z + j + 1, r + 1 : r + 1 + BLOCK, :]
-                near = near + jnp.where(low, 0.0, pltpu.roll(centre, 1, 1)) + jnp.where(high, 0.0, pltpu.roll(centre, C - 1, 1))
-                dst[z + j + 1, r : r + BLOCK, :] = KEPT * centre + weight[z + j, x : x + BLOCK, :] * (supply[z + j, x : x + BLOCK, :] + near)
+        sweep_planes(src, dst, weight, supply, i)
         return carry
 
     lax.fori_loop(0, CZ // DEPTH, planes, 0)
@@ -251,26 +254,25 @@
     own[5][...] = src[CZ, INNER, :]
 
 
-def first_kernel(heat_in, cond_in, proj_in, segs_in, weight, state, parts, heat, *refs):
+def first_kernel(heat_in, cond_in, proj_in, segs_in, weight, state, parts, heat, wx, wy, *refs):
     own = refs[:6]
     sends = refs[6:11]
-    cond, proj, segs, start, turn, sems, small = refs[11:]
+    cond, proj, segs, start, turn, pack, sems, small = refs[11:]
     tables = (pltpu.make_async_copy(proj_in, proj, small.at[0]), pltpu.make_async_copy(segs_in, segs, small.at[1]))
-    for c in tables:
-        c.start()
-    part = CZ // PARTS
-    copies = []
-    for i in range(PARTS):
-        s = pl.ds(i * part, part)
-        pair = (
+
+    def copies(i):
+        s = pl.ds(i * DEPTH, DEPTH)
+        return (
             pltpu.make_async_copy(cond_in.at[s], cond.at[s], sems.at[0, i]),
             pltpu.make_async_copy(heat_in.at[s], heat.at[s], sems.at[1, i]),
         )
-        for c in pair:
+
+    for i in range(PARTS):
+        for c in copies(i) + (tables if i == 0 else ()):
             c.start()
-        copies.append(pair)
     zero_ends(start)
     zero_ends(state)
+    pack[...] = jnp.zeros((C, C), F32)
     for c in tables:
         c.wait()
     for d in range(3):
@@ -281,38 +283,45 @@
             a[CZ : CZ + C, :] = base
         if d == 2:
             sends[4][C : 2 * C, :] = base
-
-    def plane(z, carry):
-        w = DAMPING_WEIGHT / (6.0 + cond[z])
-        weight[z] = w
-        start[z + 1, INNER, :] = w * heat[z]
+    group = lane_of((C, C)) // 4
+
+    def part(i, carry):
+        for c in copies(i):
+            c.wait()
+        packed = pack[...]
+        for j in range(DEPTH):
+            z = i * DEPTH + j
+            w = DAMPING_WEIGHT / (6.0 + cond[z])
+            weight[z] = w
+            start[z + 1, INNER, :] = w * heat[z]
+            packed = jnp.where(group == z, pltpu.roll(w, 4 * z + 2, 1), packed)
+        pack[...] = packed
+
+        @pl.when(i > 0)
+        def _():
+            sweep_planes(start, state, weight, heat, i - 1)
+
         return carry
 
-    for i, pair in enumerate(copies):
-        for c in pair:
-            c.wait()
-        lax.fori_loop(i * part, (i + 1) * part, plane, 0, unroll=UNROLL)
-    sweep(start, state, weight, heat)
+    lax.fori_loop(0, PARTS, part, 0)
+    sweep_planes(start, state, weight, heat, PARTS - 1)
     own_faces(state, own, turn)
     pack_sends(sends, [f[...] for f in own], 0)
-
-
-def free_kernel(first, state, weight, supply, *refs):
-    out = refs[0]
-    own = refs[1:7]
-    mid, turn = refs[-2:]
+    for i, e in enumerate(EDGES):
+        row_layer(weight, 0, e, wx.at[i])
+    turn[...] = pack[...].T
+    for i, e in enumerate((2, 3, 0, 1)):
+        wy[i] = turn[layer_rows(e), :]
+
+
+def free_kernel(state, weight, supply, out, *refs):
+    own = refs[:6]
+    mid, turn = refs[6:]
     zero_ends(mid)
     zero_ends(out)
     sweep(state, mid, weight, supply)
     sweep(mid, out, weight, supply)
     own_faces(out, own, turn)
-    if first:
-        wx, wy = refs[7:9]
-        for i, e in enumerate(EDGES):
-            row_layer(weight, 0, e, wx.at[i])
-        column_layers(weight, 0, turn)
-        for i, e in enumerate((2, 3, 0, 1)):
-            wy[i] = turn[layer_rows(e), :]
 
 
 def jumps(own, got, bases, prev_bases, back_bases, n, lifted):
@@ -487,11 +496,10 @@
         state[z] = free[z + 1, INNER, :] - one * resp[z + 1, INNER, :]
         return carry
 
-    part = CZ // PARTS
     copies = []
     for i in range(PARTS):
-        lax.fori_loop(i * part, (i + 1) * part, plane, 0, unroll=UNROLL)
-        s = pl.ds(i * part, part)
+        lax.fori_loop(i * DEPTH, (i + 1) * DEPTH, plane, 0, unroll=UNROLL)
+        s = pl.ds(i * DEPTH, DEPTH)
         copies.append(pltpu.make_async_copy(state.at[s], out.at[s], sems.at[i]))
         copies[-1].start()
     for i in range(3):
@@ -537,11 +545,10 @@
 
 def swap_pairs(axis, start):
     n = lax.axis_size(axis)
-    pairs = []
-    for i in range(start, n, 2):
-        j = (i + 1) % n
-        pairs += [(i, j), (j, i)]
-    return pairs
+    pairs = [(i, i) for i in range(start)]
+    for i in range(start, n - 1, 2):
+        pairs += [(i, i + 1), (i + 1, i)]
+    return pairs + [(i, i) for i in range(n - start, n)]
 
 
 def exchange(sends):
@@ -563,22 +570,19 @@
     proj = projection[0, 0, 0]
     segs = segment_map.reshape(3, 1, C)
     dma = pltpu.SemaphoreType.DMA
-    scratch = [S_FIELD, pltpu.VMEM(proj.shape, F32), pltpu.VMEM(segs.shape, jnp.int32), S_PADDED, S_SQUARE, dma((2, PARTS)), dma((2,))]
-    outs = [FIELD, PADDED, PIECES, FIELD] + FACES + sends_of(1, C)
+    scratch = [S_FIELD, pltpu.VMEM(proj.shape, F32), pltpu.VMEM(segs.shape, jnp.int32), S_PADDED, S_SQUARE, S_SQUARE, dma((2, PARTS)), dma((2,))]
+    outs = [FIELD, PADDED, PIECES, FIELD, LAYERS, LAYERS] + FACES + sends_of(1, C)
     out = call(first_kernel, "first", outs, scratch, [pltpu.with_memory_space_constraint(a, pltpu.MemorySpace.HBM) for a in (heat, cond, proj, segs)], 4, [AWAY] * 4)
-    weight, state, bases, heat = out[:4]
-    own, sends = out[4:10], out[10:]
+    weight, state, bases, heat, wx, wy = out[:6]
+    own, sends = out[6:12], out[12:]
     supply = heat
     prev = []
     held = None
     for pair in range(2):
         first = pair == 0
         got = exchange(sends)
-        outs = [PADDED] + FACES + ([LAYERS, LAYERS] if first else [])
-        out = call(functools.partial(free_kernel, first), "free", outs, [S_PADDED, S_SQUARE], (state, weight, supply), 3)
-        free, own_u = out[0], out[1:7]
-        if first:
-            wx, wy = out[7:]
+        out = call(free_kernel, "free", [PADDED] + FACES, [S_PADDED, S_SQUARE], (state, weight, supply), 3)
+        free, own_u = out[0], out[1:]
         args = own + got + [bases] + prev + [weight, wx, wy] + own_u
         stacked = [jax.ShapeDtypeStruct((2 * f.shape[0], C), F32) for f in FACES]
         outs = FACES + stacked + sends_of(2, 0) + ([PIECES, PIECES] if first else [])

time: 91.9 us -> 105 us (1.14)
  starting transfers between devices: 26.5 us -> 34.1 us
  blocking collectives: 32.2 us -> 39 us
  waiting for transfers between devices: 1.52 us -> 0.05 us
    ppermute x4, starting transfers between devices: 2.08 us -> 13.7 us  [exchange(): yb = lax.ppermute(yb, 'gy', swap_pairs('gy', 1))]
    ppermute x4, starting transfers between devices: 10 us -> 2.66 us  [exchange(): ya = lax.ppermute(ya, 'gy', swap_pairs('gy', 0))]
    all_to_all x2, blocking collectives: 32.2 us -> 39 us  [gather_rows(): rows = lax.all_to_all(rows.reshape(C, 1, C), AXES, 0, 0)]
    ppermute x4, starting transfers between devices: 2.43 us -> 8.33 us  [exchange(): xa = lax.ppermute(xa, 'gx', swap_pairs('gx', 0))]
    ppermute x4, starting transfers between devices: 4.61 us -> 2.61 us  [exchange(): xb = lax.ppermute(xb, 'gx', swap_pairs('gx', 1))]
    ppermute x4, waiting for transfers between devices: 1.48 us -> 0.01 us  [exchange(): yb = lax.ppermute(yb, 'gy', swap_pairs('gy', 1))]
  transfers between devices with their start and end apart: 20 -> 20, of which waited for: 2 -> 0; matrix products, arithmetic and copies ran while one was open for 0% -> 0% of each run, Pallas kernels for 14% -> 12%
where the time goes in v5:
time: 105 us
  blocking collectives  39 us (37%)
  starting transfers between devices  34.1 us (32%)
  Pallas kernels  30.3 us (29%)
  between operations  1.1 us (1%)
    all_to_all x2, blocking collectives, gather_rows(): rows = lax.all_to_all(rows.reshape(C, 1, C), AXES, 0, 0)  39 us
    pallas_call x11, Pallas kernels, call(): pl.pallas_call(kernel, out_shape=tuple(outs), in_specs=in_specs or [VM] *...  30.3 us
    ppermute x4, starting transfers between devices, exchange(): yb = lax.ppermute(yb, 'gy', swap_pairs('gy', 1))  13.7 us
    ppermute x4, starting transfers between devices, exchange(): xa = lax.ppermute(xa, 'gx', swap_pairs('gx', 0))  8.33 us
    ppermute x4, starting transfers between devices, exchange(): zz = lax.ppermute(zz, 'gz', swap_pairs('gz', 0))  6.87 us
    ppermute x4, starting transfers between devices, exchange(): ya = lax.ppermute(ya, 'gy', swap_pairs('gy', 0))  2.66 us
    ppermute x4, starting transfers between devices, exchange(): xb = lax.ppermute(xb, 'gx', swap_pairs('gx', 1))  2.61 us
  transfers between devices with their start and end apart: 20, of which 0 were waited for; matrix products, arithmetic and copies ran while one was open for 0% of the time, Pallas kernels for 12%

profile of v5, /device:TPU:1, one launch (start us, length us, event | category | flops | bytes accessed | tf_op | source)
XLA Modules:
  0.0 104.6 jit_solution(1547616541555241936)
XLA Ops:
  0.6 5.4 %first.1 = (f32[32,128,128]{2,1,0:T(8,128)S(1)}, f32[34,144,128]{2,1,0:T(8,128)S(1)}, bf16[9,128,128]{2,1,0:T(8,128)(2,1)S(1)}, f32[32,128,128]{2,1,0:T(8,128)S(...) custom-call(f32[32,128,128]{2,1,0:T(8,128)} %heat_in.1, ...), custom_call_target="tpu_custom_call" | custom-call | flops 40000000 | bytes 1048576 | tf_op jit(solution)/shard_map/first/pallas_call | solution.py:533
  6.1 3.6 %collective-permute-start.4 = (f32[256,128]{1,0:T(8,128)S(1)}, f32[256,128]{1,0:T(8,128)S(1)}, u32[]{:S(2)}, u32[]{:S(2)}) collective-permute-start(f32[256,128]{1,0:T(8,128)S(1)} %get-tuple-element.125), channel_id=1, source_target_pairs={{0,1},{1,0},{2,3},{3,2},{4,5},{5,4},{6,7},{7,6},{8,9},{9,8},{10,11... | collective-permute-start | bytes 393224 | tf_op jit(solution)/shard_map/ppermute | solution.py:556
  9.7 1.3 %collective-permute-start = (f32[160,128]{1,0:T(8,128)S(1)}, f32[160,128]{1,0:T(8,128)S(1)}, u32[]{:S(2)}, u32[]{:S(2)}) collective-permute-start(f32[160,128]{1,0:T(8,128)S(1)} %get-tuple-element.121), channel_id=1, source_target_pairs={{0,32},{32,0},{64,96},{96,64},{1,33},{33,1},{65,97},{97,65},{2,34}... | collective-permute-start | bytes 245768 | tf_op jit(solution)/shard_map/ppermute | solution.py:559
  11.0 0.7 collective-permute-start.1
  11.7 1.3 %collective-permute-start.2 = (f32[160,128]{1,0:T(8,128)S(1)}, f32[160,128]{1,0:T(8,128)S(1)}, u32[]{:S(2)}, u32[]{:S(2)}) collective-permute-start(f32[160,128]{1,0:T(8,128)S(1)} %get-tuple-element.123), channel_id=1, source_target_pairs={{0,2},{2,0},{4,6},{6,4},{8,10},{10,8},{12,14},{14,12},{16,18},{18,... | collective-permute-start | bytes 245768 | tf_op jit(solution)/shard_map/ppermute | solution.py:560
  13.0 3.4 %collective-permute-start.3 = (f32[160,128]{1,0:T(8,128)S(1)}, f32[160,128]{1,0:T(8,128)S(1)}, u32[]{:S(2)}, u32[]{:S(2)}) collective-permute-start(f32[160,128]{1,0:T(8,128)S(1)} %get-tuple-element.124), channel_id=1, source_target_pairs={{0,0},{2,4},{4,2},{6,8},{8,6},{10,12},{12,10},{14,16},{16,14},{18,... | collective-permute-start | bytes 245768 | tf_op jit(solution)/shard_map/ppermute | solution.py:557
  16.4 3.6 %free.2 = (f32[34,144,128]{2,1,0:T(8,128)S(1)}, f32[32,128]{1,0:T(8,128)S(1)}, f32[32,128]{1,0:T(8,128)S(1)}, f32[32,128]{1,0:T(8,128)S(1)}, f32[32,128]{1,0:T(8...) custom-call(f32[34,144,128]{2,1,0:T(8,128)S(1)} %get-tuple-element.130.state, ...), custom_call_target="tpu_custom_call" | custom-call | flops 30000000 | bytes 1048576 | tf_op jit(solution)/shard_map/free/pallas_call | solution.py:533
  20.1 1.3 %second.2 = (f32[32,128]{1,0:T(8,128)S(1)}, f32[32,128]{1,0:T(8,128)S(1)}, f32[32,128]{1,0:T(8,128)S(1)}, f32[32,128]{1,0:T(8,128)S(1)}, f32[128,128]{1,0:T(8,12...) custom-call(f32[32,128]{1,0:T(8,128)S(1)} %get-tuple-element.115.ref, ...), custom_call_target="tpu_custom_call" | custom-call | flops 20000000 | bytes 1048576 | tf_op jit(solution)/shard_map/second/pallas_call | solution.py:533
  21.3 0.3 collective-permute-start.9
  21.6 3.8 %collective-permute-start.5 = (f32[64,128]{1,0:T(8,128)S(1)}, f32[64,128]{1,0:T(8,128)S(1)}, u32[]{:S(2)}, u32[]{:S(2)}) collective-permute-start(f32[64,128]{1,0:T(8,128)S(1)} %get-tuple-element.144), channel_id=1, source_target_pairs={{0,32},{32,0},{64,96},{96,64},{1,33},{33,1},{65,97},{97,65},{2,34}... | collective-permute-start | bytes 98312 | tf_op jit(solution)/shard_map/ppermute | solution.py:559
  25.5 0.7 collective-permute-start.6
  26.1 0.1 collective-permute-start.7
  26.2 3.9 %collective-permute-start.8 = (f32[64,128]{1,0:T(8,128)S(1)}, f32[64,128]{1,0:T(8,128)S(1)}, u32[]{:S(2)}, u32[]{:S(2)}) collective-permute-start(f32[64,128]{1,0:T(8,128)S(1)} %get-tuple-element.147), channel_id=1, source_target_pairs={{0,0},{2,4},{4,2},{6,8},{8,6},{10,12},{12,10},{14,16},{16,14},{18,... | collective-permute-start | bytes 98312 | tf_op jit(solution)/shard_map/ppermute | solution.py:557
  30.1 2.7 %response.2 = (f32[34,144,128]{2,1,0:T(8,128)S(1)}, f32[1,128]{1,0:T(1,128)S(1)}) custom-call(f32[32,128]{1,0:T(8,128)S(1)} %get-tuple-element.151.refs_0_.refs_5_, f32[32,128]{1,0:T(8,128)S(1)} %get-tuple-element.152.refs_1_.refs_6_, f32[32,128]{1,0:T(8,128)S(1)} %get-tuple-element.153.refs_2_.refs_7_, f32[32,128]{1,0:T(8,128)S(1)} %get-tuple-element.154.refs_3_.refs_8_, ...), custom_call_target="tpu_custom_call" | custom-call | flops 30000000 | bytes 1048576 | tf_op jit(solution)/shard_map/response/pallas_call | solution.py:533
  32.9 1.5 %third.2 = (f32[32,128]{1,0:T(8,128)S(1)}, f32[32,128]{1,0:T(8,128)S(1)}, f32[128,128]{1,0:T(8,128)S(1)}, f32[32,128]{1,0:T(8,128)S(1)}, f32[32,128]{1,0:T(8,128...) custom-call(f32[64,128]{1,0:T(8,128)S(1)} %get-tuple-element.138.ref, ...), custom_call_target="tpu_custom_call" | custom-call | flops 20000000 | bytes 1048576 | tf_op jit(solution)/shard_map/third/pallas_call | solution.py:533
  34.4 21.3 %all_to_all.10 = f32[128,1,128]{2,1,0:T(1,128)S(1)} all-to-all(f32[128,1,128]{2,1,0:T(1,128)S(1)} %bitcast.15), channel_id=1, replica_groups=mesh['gx'=4,'gy'=16,'gz'=2] {'gx','gy','gz'}, dimensions={0} | all-to-all | bytes 131072 | tf_op jit(solution)/shard_map/all_to_all | solution.py:565
  55.7 4.8 %fourth.1 = (f32[32,128,128]{2,1,0:T(8,128)S(1)}, f32[34,144,128]{2,1,0:T(8,128)S(1)}, f32[32,128]{1,0:T(8,128)S(1)}, f32[32,128]{1,0:T(8,128)S(1)}, f32[128,128...) custom-call(f32[128,128]{1,0:T(8,128)S(1)} %bitcast.13, ...), custom_call_target="tpu_custom_call" | custom-call | flops 50000000 | bytes 1048576 | tf_op jit(solution)/shard_map/fourth/pallas_call | solution.py:533
  60.5 1.1 %collective-permute-start.14 = (f32[128,128]{1,0:T(8,128)S(1)}, f32[128,128]{1,0:T(8,128)S(1)}, u32[]{:S(2)}, u32[]{:S(2)}) collective-permute-start(f32[128,128]{1,0:T(8,128)S(1)} %get-tuple-element.183), channel_id=1, source_target_pairs={{0,1},{1,0},{2,3},{3,2},{4,5},{5,4},{6,7},{7,6},{8,9},{9,8},{10,11... | collective-permute-start | bytes 196616 | tf_op jit(solution)/shard_map/ppermute | solution.py:556
  61.6 0.4 collective-permute-start.10
  62.0 0.7 collective-permute-start.11
  62.6 1.2 %collective-permute-start.12 = (f32[32,128]{1,0:T(8,128)S(1)}, f32[32,128]{1,0:T(8,128)S(1)}, u32[]{:S(2)}, u32[]{:S(2)}) collective-permute-start(f32[32,128]{1,0:T(8,128)S(1)} %get-tuple-element.181), channel_id=1, source_target_pairs={{0,2},{2,0},{4,6},{6,4},{8,10},{10,8},{12,14},{14,12},{16,18},{18,... | collective-permute-start | bytes 49160 | tf_op jit(solution)/shard_map/ppermute | solution.py:560
  63.8 2.4 %collective-permute-start.13 = (f32[32,128]{1,0:T(8,128)S(1)}, f32[32,128]{1,0:T(8,128)S(1)}, u32[]{:S(2)}, u32[]{:S(2)}) collective-permute-start(f32[32,128]{1,0:T(8,128)S(1)} %get-tuple-element.182), channel_id=1, source_target_pairs={{0,0},{2,4},{4,2},{6,8},{8,6},{10,12},{12,10},{14,16},{16,14},{18,... | collective-permute-start | bytes 49160 | tf_op jit(solution)/shard_map/ppermute | solution.py:557
  66.2 3.6 %free.3 = (f32[34,144,128]{2,1,0:T(8,128)S(1)}, f32[32,128]{1,0:T(8,128)S(1)}, f32[32,128]{1,0:T(8,128)S(1)}, f32[32,128]{1,0:T(8,128)S(1)}, f32[32,128]{1,0:T(8...) custom-call(f32[34,144,128]{2,1,0:T(8,128)S(1)} %get-tuple-element.184.state, ...), custom_call_target="tpu_custom_call" | custom-call | flops 30000000 | bytes 1048576 | tf_op jit(solution)/shard_map/free/pallas_call | solution.py:533
  69.8 1.2 %second.3 = (f32[32,128]{1,0:T(8,128)S(1)}, f32[32,128]{1,0:T(8,128)S(1)}, f32[32,128]{1,0:T(8,128)S(1)}, f32[32,128]{1,0:T(8,128)S(1)}, f32[128,128]{1,0:T(8,12...) custom-call(f32[32,128]{1,0:T(8,128)S(1)} %get-tuple-element.173.ref, ...), custom_call_target="tpu_custom_call" | custom-call | flops 20000000 | bytes 1048576 | tf_op jit(solution)/shard_map/second/pallas_call | solution.py:533
  71.0 1.8 %collective-permute-start.19 = (f32[256,128]{1,0:T(8,128)S(1)}, f32[256,128]{1,0:T(8,128)S(1)}, u32[]{:S(2)}, u32[]{:S(2)}) collective-permute-start(f32[256,128]{1,0:T(8,128)S(1)} %get-tuple-element.202), channel_id=1, source_target_pairs={{0,1},{1,0},{2,3},{3,2},{4,5},{5,4},{6,7},{7,6},{8,9},{9,8},{10,11... | collective-permute-start | bytes 393224 | tf_op jit(solution)/shard_map/ppermute | solution.py:556
  72.8 2.9 %collective-permute-start.15 = (f32[64,128]{1,0:T(8,128)S(1)}, f32[64,128]{1,0:T(8,128)S(1)}, u32[]{:S(2)}, u32[]{:S(2)}) collective-permute-start(f32[64,128]{1,0:T(8,128)S(1)} %get-tuple-element.198), channel_id=1, source_target_pairs={{0,32},{32,0},{64,96},{96,64},{1,33},{33,1},{65,97},{97,65},{2,34}... | collective-permute-start | bytes 98312 | tf_op jit(solution)/shard_map/ppermute | solution.py:559
  75.6 0.7 collective-permute-start.16
  76.4 4.0 %collective-permute-start.18 = (f32[64,128]{1,0:T(8,128)S(1)}, f32[64,128]{1,0:T(8,128)S(1)}, u32[]{:S(2)}, u32[]{:S(2)}) collective-permute-start(f32[64,128]{1,0:T(8,128)S(1)} %get-tuple-element.201), channel_id=1, source_target_pairs={{0,0},{2,4},{4,2},{6,8},{8,6},{10,12},{12,10},{14,16},{16,14},{18,... | collective-permute-start | bytes 98312 | tf_op jit(solution)/shard_map/ppermute | solution.py:557
  80.3 2.7 %response.3 = (f32[34,144,128]{2,1,0:T(8,128)S(1)}, f32[1,128]{1,0:T(1,128)S(1)}) custom-call(f32[32,128]{1,0:T(8,128)S(1)} %get-tuple-element.203.refs_0_, f32[32,128]{1,0:T(8,128)S(1)} %get-tuple-element.204.refs_1_.refs_6_, f32[32,128]{1,0:T(8,128)S(1)} %get-tuple-element.205.refs_2_, f32[32,128]{1,0:T(8,128)S(1)} %get-tuple-element.206.refs_3_.refs_7_, ...), custom_call_target="tpu_custom_call" | custom-call | flops 30000000 | bytes 1048576 | tf_op jit(solution)/shard_map/response/pallas_call | solution.py:533
  83.1 1.5 %third.3 = (f32[32,128]{1,0:T(8,128)S(1)}, f32[32,128]{1,0:T(8,128)S(1)}, f32[128,128]{1,0:T(8,128)S(1)}, f32[32,128]{1,0:T(8,128)S(1)}, f32[32,128]{1,0:T(8,128...) custom-call(f32[64,128]{1,0:T(8,128)S(1)} %get-tuple-element.192.refs_0_, ...), custom_call_target="tpu_custom_call" | custom-call | flops 20000000 | bytes 1048576 | tf_op jit(solution)/shard_map/third/pallas_call | solution.py:533
  84.6 17.7 %all_to_all.11 = f32[128,1,128]{2,1,0:T(1,128)S(1)} all-to-all(f32[128,1,128]{2,1,0:T(1,128)S(1)} %bitcast.16), channel_id=1, replica_groups=mesh['gx'=4,'gy'=16,'gz'=2] {'gx','gy','gz'}, dimensions={0} | all-to-all | bytes 131072 | tf_op jit(solution)/shard_map/all_to_all | solution.py:565
  102.3 2.2 %last.1 = (f32[32,128,128]{2,1,0:T(8,128)}, f32[32,128]{1,0:T(8,128)}, f32[32,128]{1,0:T(8,128)}, f32[128,128]{1,0:T(8,128)}) custom-call(f32[128,128]{1,0:T(8,128)S(1)} %bitcast.14, f32[34,144,128]{2,1,0:T(8,128)S(1)} %get-tuple-element.211.refs_1_, f32[34,144,128]{2,1,0:T(8,128)S(1)} %get-tuple-element.212.refs_2_, ...), custom_call_target="tpu_custom_call" | custom-call | flops 20000000 | bytes 1048576 | tf_op jit(solution)/shard_map/last/pallas_call | solution.py:533
  (21 shorter events, 0.1 us)
Async XLA Ops:
  6.1 14.0 %collective-permute-start.4 = (f32[256,128]{1,0:T(8,128)S(1)}, f32[256,128]{1,0:T(8,128)S(1)}, u32[]{:S(2)}, u32[]{:S(2)}) collective-permute-start(f32[256,128]{1,0:T(8,128)S(1)} %get-tuple-element.125), channel_id=1, source_target_pairs={{0,1},{1,0},{2,3},{3,2},{4,5},{5,4},{6,7},{7,6},{8,9},{9,8},{10,11... | collective-permute-start | bytes 393224 | tf_op jit(solution)/shard_map/ppermute | solution.py:556
  9.7 10.3 %collective-permute-start = (f32[160,128]{1,0:T(8,128)S(1)}, f32[160,128]{1,0:T(8,128)S(1)}, u32[]{:S(2)}, u32[]{:S(2)}) collective-permute-start(f32[160,128]{1,0:T(8,128)S(1)} %get-tuple-element.121), channel_id=1, source_target_pairs={{0,32},{32,0},{64,96},{96,64},{1,33},{33,1},{65,97},{97,65},{2,34}... | collective-permute-start | bytes 245768 | tf_op jit(solution)/shard_map/ppermute | solution.py:559
  11.0 9.0 %collective-permute-start.1 = (f32[160,128]{1,0:T(8,128)S(1)}, f32[160,128]{1,0:T(8,128)S(1)}, u32[]{:S(2)}, u32[]{:S(2)}) collective-permute-start(f32[160,128]{1,0:T(8,128)S(1)} %get-tuple-element.122), channel_id=1, source_target_pairs={{0,0},{32,64},{64,32},{96,96},{1,1},{33,65},{65,33},{97,97},{2,2},... | collective-permute-start | bytes 245768 | tf_op jit(solution)/shard_map/ppermute | solution.py:558
  11.7 8.4 %collective-permute-start.2 = (f32[160,128]{1,0:T(8,128)S(1)}, f32[160,128]{1,0:T(8,128)S(1)}, u32[]{:S(2)}, u32[]{:S(2)}) collective-permute-start(f32[160,128]{1,0:T(8,128)S(1)} %get-tuple-element.123), channel_id=1, source_target_pairs={{0,2},{2,0},{4,6},{6,4},{8,10},{10,8},{12,14},{14,12},{16,18},{18,... | collective-permute-start | bytes 245768 | tf_op jit(solution)/shard_map/ppermute | solution.py:560
  13.0 7.1 %collective-permute-start.3 = (f32[160,128]{1,0:T(8,128)S(1)}, f32[160,128]{1,0:T(8,128)S(1)}, u32[]{:S(2)}, u32[]{:S(2)}) collective-permute-start(f32[160,128]{1,0:T(8,128)S(1)} %get-tuple-element.124), channel_id=1, source_target_pairs={{0,0},{2,4},{4,2},{6,8},{8,6},{10,12},{12,10},{14,16},{16,14},{18,... | collective-permute-start | bytes 245768 | tf_op jit(solution)/shard_map/ppermute | solution.py:557
  21.3 11.5 %collective-permute-start.9 = (f32[256,128]{1,0:T(8,128)S(1)}, f32[256,128]{1,0:T(8,128)S(1)}, u32[]{:S(2)}, u32[]{:S(2)}) collective-permute-start(f32[256,128]{1,0:T(8,128)S(1)} %get-tuple-element.148), channel_id=1, source_target_pairs={{0,1},{1,0},{2,3},{3,2},{4,5},{5,4},{6,7},{7,6},{8,9},{9,8},{10,11... | collective-permute-start | bytes 393224 | tf_op jit(solution)/shard_map/ppermute | solution.py:556
  21.6 11.2 %collective-permute-start.5 = (f32[64,128]{1,0:T(8,128)S(1)}, f32[64,128]{1,0:T(8,128)S(1)}, u32[]{:S(2)}, u32[]{:S(2)}) collective-permute-start(f32[64,128]{1,0:T(8,128)S(1)} %get-tuple-element.144), channel_id=1, source_target_pairs={{0,32},{32,0},{64,96},{96,64},{1,33},{33,1},{65,97},{97,65},{2,34}... | collective-permute-start | bytes 98312 | tf_op jit(solution)/shard_map/ppermute | solution.py:559
  25.5 7.4 %collective-permute-start.6 = (f32[64,128]{1,0:T(8,128)S(1)}, f32[64,128]{1,0:T(8,128)S(1)}, u32[]{:S(2)}, u32[]{:S(2)}) collective-permute-start(f32[64,128]{1,0:T(8,128)S(1)} %get-tuple-element.145), channel_id=1, source_target_pairs={{0,0},{32,64},{64,32},{96,96},{1,1},{33,65},{65,33},{97,97},{2,2},... | collective-permute-start | bytes 98312 | tf_op jit(solution)/shard_map/ppermute | solution.py:558
  26.1 6.7 %collective-permute-start.7 = (f32[64,128]{1,0:T(8,128)S(1)}, f32[64,128]{1,0:T(8,128)S(1)}, u32[]{:S(2)}, u32[]{:S(2)}) collective-permute-start(f32[64,128]{1,0:T(8,128)S(1)} %get-tuple-element.146), channel_id=1, source_target_pairs={{0,2},{2,0},{4,6},{6,4},{8,10},{10,8},{12,14},{14,12},{16,18},{18,... | collective-permute-start | bytes 98312 | tf_op jit(solution)/shard_map/ppermute | solution.py:560
  26.2 6.6 %collective-permute-start.8 = (f32[64,128]{1,0:T(8,128)S(1)}, f32[64,128]{1,0:T(8,128)S(1)}, u32[]{:S(2)}, u32[]{:S(2)}) collective-permute-start(f32[64,128]{1,0:T(8,128)S(1)} %get-tuple-element.147), channel_id=1, source_target_pairs={{0,0},{2,4},{4,2},{6,8},{8,6},{10,12},{12,10},{14,16},{16,14},{18,... | collective-permute-start | bytes 98312 | tf_op jit(solution)/shard_map/ppermute | solution.py:557
  60.5 9.3 %collective-permute-start.14 = (f32[128,128]{1,0:T(8,128)S(1)}, f32[128,128]{1,0:T(8,128)S(1)}, u32[]{:S(2)}, u32[]{:S(2)}) collective-permute-start(f32[128,128]{1,0:T(8,128)S(1)} %get-tuple-element.183), channel_id=1, source_target_pairs={{0,1},{1,0},{2,3},{3,2},{4,5},{5,4},{6,7},{7,6},{8,9},{9,8},{10,11... | collective-permute-start | bytes 196616 | tf_op jit(solution)/shard_map/ppermute | solution.py:556
  61.6 8.1 %collective-permute-start.10 = (f32[32,128]{1,0:T(8,128)S(1)}, f32[32,128]{1,0:T(8,128)S(1)}, u32[]{:S(2)}, u32[]{:S(2)}) collective-permute-start(f32[32,128]{1,0:T(8,128)S(1)} %get-tuple-element.179), channel_id=1, source_target_pairs={{0,32},{32,0},{64,96},{96,64},{1,33},{33,1},{65,97},{97,65},{2,34}... | collective-permute-start | bytes 49160 | tf_op jit(solution)/shard_map/ppermute | solution.py:559
  62.0 7.8 %collective-permute-start.11 = (f32[32,128]{1,0:T(8,128)S(1)}, f32[32,128]{1,0:T(8,128)S(1)}, u32[]{:S(2)}, u32[]{:S(2)}) collective-permute-start(f32[32,128]{1,0:T(8,128)S(1)} %get-tuple-element.180), channel_id=1, source_target_pairs={{0,0},{32,64},{64,32},{96,96},{1,1},{33,65},{65,33},{97,97},{2,2},... | collective-permute-start | bytes 49160 | tf_op jit(solution)/shard_map/ppermute | solution.py:558
  62.6 7.1 %collective-permute-start.12 = (f32[32,128]{1,0:T(8,128)S(1)}, f32[32,128]{1,0:T(8,128)S(1)}, u32[]{:S(2)}, u32[]{:S(2)}) collective-permute-start(f32[32,128]{1,0:T(8,128)S(1)} %get-tuple-element.181), channel_id=1, source_target_pairs={{0,2},{2,0},{4,6},{6,4},{8,10},{10,8},{12,14},{14,12},{16,18},{18,... | collective-permute-start | bytes 49160 | tf_op jit(solution)/shard_map/ppermute | solution.py:560
  63.8 6.0 %collective-permute-start.13 = (f32[32,128]{1,0:T(8,128)S(1)}, f32[32,128]{1,0:T(8,128)S(1)}, u32[]{:S(2)}, u32[]{:S(2)}) collective-permute-start(f32[32,128]{1,0:T(8,128)S(1)} %get-tuple-element.182), channel_id=1, source_target_pairs={{0,0},{2,4},{4,2},{6,8},{8,6},{10,12},{12,10},{14,16},{16,14},{18,... | collective-permute-start | bytes 49160 | tf_op jit(solution)/shard_map/ppermute | solution.py:557
  71.0 12.1 %collective-permute-start.19 = (f32[256,128]{1,0:T(8,128)S(1)}, f32[256,128]{1,0:T(8,128)S(1)}, u32[]{:S(2)}, u32[]{:S(2)}) collective-permute-start(f32[256,128]{1,0:T(8,128)S(1)} %get-tuple-element.202), channel_id=1, source_target_pairs={{0,1},{1,0},{2,3},{3,2},{4,5},{5,4},{6,7},{7,6},{8,9},{9,8},{10,11... | collective-permute-start | bytes 393224 | tf_op jit(solution)/shard_map/ppermute | solution.py:556
  72.8 10.2 %collective-permute-start.15 = (f32[64,128]{1,0:T(8,128)S(1)}, f32[64,128]{1,0:T(8,128)S(1)}, u32[]{:S(2)}, u32[]{:S(2)}) collective-permute-start(f32[64,128]{1,0:T(8,128)S(1)} %get-tuple-element.198), channel_id=1, source_target_pairs={{0,32},{32,0},{64,96},{96,64},{1,33},{33,1},{65,97},{97,65},{2,34}... | collective-permute-start | bytes 98312 | tf_op jit(solution)/shard_map/ppermute | solution.py:559
  75.6 7.4 %collective-permute-start.16 = (f32[64,128]{1,0:T(8,128)S(1)}, f32[64,128]{1,0:T(8,128)S(1)}, u32[]{:S(2)}, u32[]{:S(2)}) collective-permute-start(f32[64,128]{1,0:T(8,128)S(1)} %get-tuple-element.199), channel_id=1, source_target_pairs={{0,0},{32,64},{64,32},{96,96},{1,1},{33,65},{65,33},{97,97},{2,2},... | collective-permute-start | bytes 98312 | tf_op jit(solution)/shard_map/ppermute | solution.py:558
  76.3 6.7 %collective-permute-start.17 = (f32[64,128]{1,0:T(8,128)S(1)}, f32[64,128]{1,0:T(8,128)S(1)}, u32[]{:S(2)}, u32[]{:S(2)}) collective-permute-start(f32[64,128]{1,0:T(8,128)S(1)} %get-tuple-element.200), channel_id=1, source_target_pairs={{0,2},{2,0},{4,6},{6,4},{8,10},{10,8},{12,14},{14,12},{16,18},{18,... | collective-permute-start | bytes 98312 | tf_op jit(solution)/shard_map/ppermute | solution.py:560
  76.4 6.7 %collective-permute-start.18 = (f32[64,128]{1,0:T(8,128)S(1)}, f32[64,128]{1,0:T(8,128)S(1)}, u32[]{:S(2)}, u32[]{:S(2)}) collective-permute-start(f32[64,128]{1,0:T(8,128)S(1)} %get-tuple-element.201), channel_id=1, source_target_pairs={{0,0},{2,4},{4,2},{6,8},{8,6},{10,12},{12,10},{14,16},{16,14},{18,... | collective-permute-start | bytes 98312 | tf_op jit(solution)/shard_map/ppermute | solution.py:557

commit v6 on v5

--- a/solution.py
+++ b/solution.py
@@ -16,7 +16,6 @@
 F32 = jnp.float32
 UNROLL = 4
 WIDE = 16
-BLOCK = 16
 DEPTH = 8
 PARTS = CZ // DEPTH
 KEPT = 1.0 - DAMPING_WEIGHT
@@ -83,28 +82,27 @@
     return near + jnp.where(lanes == C - 1, 0.0, pltpu.roll(centre, C - 1, 1))
 
 
-def sweep_planes(src, dst, weight, supply, i):
-    lanes = lane_of((BLOCK, C))
+def sweep_planes(src, dst, weight, supply, z, depth, block):
+    lanes = lane_of((block, C))
     low = lanes == 0
     high = lanes == C - 1
-    z = i * DEPTH
-    for x in range(0, C, BLOCK):
+    for x in range(0, C, block):
         r = PAD + x
-        column = [src[z + j, r : r + BLOCK, :] for j in range(DEPTH + 2)]
-        for j in range(DEPTH):
+        column = [src[z + j, r : r + block, :] for j in range(depth + 2)]
+        for j in range(depth):
             centre = column[j + 1]
             near = column[j] + column[j + 2]
-            near = near + src[z + j + 1, r - 1 : r - 1 + BLOCK, :] + src[z + j + 1, r + 1 : r + 1 + BLOCK, :]
+            near = near + src[z + j + 1, r - 1 : r - 1 + block, :] + src[z + j + 1, r + 1 : r + 1 + block, :]
             near = near + jnp.where(low, 0.0, pltpu.roll(centre, 1, 1)) + jnp.where(high, 0.0, pltpu.roll(centre, C - 1, 1))
-            dst[z + j + 1, r : r + BLOCK, :] = KEPT * centre + weight[z + j, x : x + BLOCK, :] * (supply[z + j, x : x + BLOCK, :] + near)
+            dst[z + j + 1, r : r + block, :] = KEPT * centre + weight[z + j, x : x + block, :] * (supply[z + j, x : x + block, :] + near)
 
 
 def sweep(src, dst, weight, supply):
     def planes(i, carry):
-        sweep_planes(src, dst, weight, supply, i)
+        sweep_planes(src, dst, weight, supply, i * WIDE, WIDE, 8)
         return carry
 
-    lax.fori_loop(0, CZ // DEPTH, planes, 0)
+    lax.fori_loop(0, CZ // WIDE, planes, 0)
 
 
 def row_layer(src, base, at, out):
@@ -118,7 +116,7 @@
     def plane(z, packed):
         return jnp.where(group == z, pltpu.roll(src[z + base, PAD * base : PAD * base + C, :], 4 * z + 2, 1), packed)
 
-    packed = lax.fori_loop(0, CZ, plane, jnp.zeros((C, C), F32), unroll=WIDE)
+    packed = lax.fori_loop(0, CZ, plane, jnp.zeros((C, C), F32), unroll=CZ)
     turn[...] = packed.T
 
 
@@ -267,8 +265,10 @@
             pltpu.make_async_copy(heat_in.at[s], heat.at[s], sems.at[1, i]),
         )
 
+    for c in tables:
+        c.start()
     for i in range(PARTS):
-        for c in copies(i) + (tables if i == 0 else ()):
+        for c in copies(i):
             c.start()
     zero_ends(start)
     zero_ends(state)
@@ -299,12 +299,12 @@
 
         @pl.when(i > 0)
         def _():
-            sweep_planes(start, state, weight, heat, i - 1)
+            sweep_planes(start, state, weight, heat, (i - 1) * DEPTH, DEPTH, 16)
 
         return carry
 
     lax.fori_loop(0, PARTS, part, 0)
-    sweep_planes(start, state, weight, heat, PARTS - 1)
+    sweep_planes(start, state, weight, heat, CZ - DEPTH, DEPTH, 16)
     own_faces(state, own, turn)
     pack_sends(sends, [f[...] for f in own], 0)
     for i, e in enumerate(EDGES):
@@ -471,7 +471,7 @@
         state[z + 1, INNER, :] = free[z + 1, INNER, :] - one * resp[z + 1, INNER, :]
         return carry
 
-    lax.fori_loop(0, CZ, plane, 0, unroll=2 * UNROLL)
+    lax.fori_loop(0, CZ, plane, 0, unroll=WIDE)
     add_rows(supply, held, -1.0)
     sweep(state, mid, weight, supply)
     sweep(mid, state, weight, supply)
@@ -545,10 +545,11 @@
 
 def swap_pairs(axis, start):
     n = lax.axis_size(axis)
-    pairs = [(i, i) for i in range(start)]
-    for i in range(start, n - 1, 2):
-        pairs += [(i, i + 1), (i + 1, i)]
-    return pairs + [(i, i) for i in range(n - start, n)]
+    pairs = []
+    for i in range(start, n, 2):
+        j = (i + 1) % n
+        pairs += [(i, j), (j, i)]
+    return pairs
 
 
 def exchange(sends):

time: 105 us -> 90.9 us (0.87)
  starting transfers between devices: 34.1 us -> 27 us
  blocking collectives: 39 us -> 32.2 us
  waiting for transfers between devices: 0.05 us -> 1.91 us
  Pallas kernels: 30.3 us -> 28.7 us
    ppermute x4, starting transfers between devices: 13.7 us -> 1.97 us  [exchange(): yb = lax.ppermute(yb, 'gy', swap_pairs('gy', 1))]
    ppermute x4, starting transfers between devices: 2.66 us -> 10.4 us  [exchange(): ya = lax.ppermute(ya, 'gy', swap_pairs('gy', 0))]
    all_to_all x2, blocking collectives: 39 us -> 32.2 us  [gather_rows(): rows = lax.all_to_all(rows.reshape(C, 1, C), AXES, 0, 0)]
    ppermute x4, starting transfers between devices: 8.33 us -> 2.43 us  [exchange(): xa = lax.ppermute(xa, 'gx', swap_pairs('gx', 0))]
    ppermute x4, starting transfers between devices: 2.61 us -> 4.61 us  [exchange(): xb = lax.ppermute(xb, 'gx', swap_pairs('gx', 1))]
    ppermute x4, waiting for transfers between devices: 0.01 us -> 1.87 us  [exchange(): yb = lax.ppermute(yb, 'gy', swap_pairs('gy', 1))]
    pallas_call x11, Pallas kernels: 30.3 us -> 28.7 us  [call(): pl.pallas_call(kernel, out_shape=tuple(outs), in_specs=in_specs or [VM] *...]
  transfers between devices with their start and end apart: 20 -> 20, of which waited for: 0 -> 2; matrix products, arithmetic and copies ran while one was open for 0% -> 0% of each run, Pallas kernels for 12% -> 13%
where the time goes in v6:
time: 90.9 us; the launch traced here: 90.7 us
  blocking collectives  32.2 us (35%)
  Pallas kernels  28.7 us (32%)
  starting transfers between devices  27 us (30%)
  waiting for transfers between devices  1.91 us (2%)
  between operations  0.97 us (1%)
    all_to_all x2, blocking collectives, gather_rows(): rows = lax.all_to_all(rows.reshape(C, 1, C), AXES, 0, 0)  32.2 us
    pallas_call x11, Pallas kernels, call(): pl.pallas_call(kernel, out_shape=tuple(outs), in_specs=in_specs or [VM] *...  28.7 us
    ppermute x4, starting transfers between devices, exchange(): ya = lax.ppermute(ya, 'gy', swap_pairs('gy', 0))  10.4 us
    ppermute x4, starting transfers between devices, exchange(): zz = lax.ppermute(zz, 'gz', swap_pairs('gz', 0))  7.6 us
    ppermute x4, starting transfers between devices, exchange(): xb = lax.ppermute(xb, 'gx', swap_pairs('gx', 1))  4.61 us
    ppermute x4, starting transfers between devices, exchange(): xa = lax.ppermute(xa, 'gx', swap_pairs('gx', 0))  2.43 us
    ppermute x4, starting transfers between devices, exchange(): yb = lax.ppermute(yb, 'gy', swap_pairs('gy', 1))  1.97 us
    ppermute x4, waiting for transfers between devices, exchange(): yb = lax.ppermute(yb, 'gy', swap_pairs('gy', 1))  1.87 us
  transfers between devices with their start and end apart: 20, of which 2 were waited for; matrix products, arithmetic and copies ran while one was open for 0% of the time, Pallas kernels for 13%

profile of v6, /device:TPU:1, one launch (start us, length us, event | category | flops | bytes accessed | tf_op | source)
XLA Modules:
  0.0 90.7 jit_solution(7033863398349072699)
XLA Ops:
  0.6 5.4 %first.1 = (f32[32,128,128]{2,1,0:T(8,128)S(1)}, f32[34,144,128]{2,1,0:T(8,128)S(1)}, bf16[9,128,128]{2,1,0:T(8,128)(2,1)S(1)}, f32[32,128,128]{2,1,0:T(8,128)S(...) custom-call(f32[32,128,128]{2,1,0:T(8,128)} %heat_in.1, ...), custom_call_target="tpu_custom_call" | custom-call | flops 40000000 | bytes 1048576 | tf_op jit(solution)/shard_map/first/pallas_call | solution.py:533
  6.0 3.6 %collective-permute-start.4 = (f32[256,128]{1,0:T(8,128)S(1)}, f32[256,128]{1,0:T(8,128)S(1)}, u32[]{:S(2)}, u32[]{:S(2)}) collective-permute-start(f32[256,128]{1,0:T(8,128)S(1)} %get-tuple-element.125), channel_id=1, source_target_pairs={{0,1},{1,0},{2,3},{3,2},{4,5},{5,4},{6,7},{7,6},{8,9},{9,8},{10,11... | collective-permute-start | bytes 393224 | tf_op jit(solution)/shard_map/ppermute | solution.py:557
  9.6 1.3 %collective-permute-start = (f32[160,128]{1,0:T(8,128)S(1)}, f32[160,128]{1,0:T(8,128)S(1)}, u32[]{:S(2)}, u32[]{:S(2)}) collective-permute-start(f32[160,128]{1,0:T(8,128)S(1)} %get-tuple-element.121), channel_id=1, source_target_pairs={{0,32},{32,0},{64,96},{96,64},{1,33},{33,1},{65,97},{97,65},{2,34}... | collective-permute-start | bytes 245768 | tf_op jit(solution)/shard_map/ppermute | solution.py:560
  10.9 1.9 %collective-permute-start.1 = (f32[160,128]{1,0:T(8,128)S(1)}, f32[160,128]{1,0:T(8,128)S(1)}, u32[]{:S(2)}, u32[]{:S(2)}) collective-permute-start(f32[160,128]{1,0:T(8,128)S(1)} %get-tuple-element.122), channel_id=1, source_target_pairs={{32,64},{64,32},{96,0},{0,96},{33,65},{65,33},{97,1},{1,97},{34,66... | collective-permute-start | bytes 245768 | tf_op jit(solution)/shard_map/ppermute | solution.py:559
  12.8 1.5 %collective-permute-start.2 = (f32[160,128]{1,0:T(8,128)S(1)}, f32[160,128]{1,0:T(8,128)S(1)}, u32[]{:S(2)}, u32[]{:S(2)}) collective-permute-start(f32[160,128]{1,0:T(8,128)S(1)} %get-tuple-element.123), channel_id=1, source_target_pairs={{0,2},{2,0},{4,6},{6,4},{8,10},{10,8},{12,14},{14,12},{16,18},{18,... | collective-permute-start | bytes 245768 | tf_op jit(solution)/shard_map/ppermute | solution.py:561
  14.4 1.5 %collective-permute-start.3 = (f32[160,128]{1,0:T(8,128)S(1)}, f32[160,128]{1,0:T(8,128)S(1)}, u32[]{:S(2)}, u32[]{:S(2)}) collective-permute-start(f32[160,128]{1,0:T(8,128)S(1)} %get-tuple-element.124), channel_id=1, source_target_pairs={{2,4},{4,2},{6,8},{8,6},{10,12},{12,10},{14,16},{16,14},{18,20},{2... | collective-permute-start | bytes 245768 | tf_op jit(solution)/shard_map/ppermute | solution.py:558
  15.9 3.2 %free.2 = (f32[34,144,128]{2,1,0:T(8,128)S(1)}, f32[32,128]{1,0:T(8,128)S(1)}, f32[32,128]{1,0:T(8,128)S(1)}, f32[32,128]{1,0:T(8,128)S(1)}, f32[32,128]{1,0:T(8...) custom-call(f32[34,144,128]{2,1,0:T(8,128)S(1)} %get-tuple-element.130.state, ...), custom_call_target="tpu_custom_call" | custom-call | flops 30000000 | bytes 1048576 | tf_op jit(solution)/shard_map/free/pallas_call | solution.py:533
  19.1 1.3 %second.2 = (f32[32,128]{1,0:T(8,128)S(1)}, f32[32,128]{1,0:T(8,128)S(1)}, f32[32,128]{1,0:T(8,128)S(1)}, f32[32,128]{1,0:T(8,128)S(1)}, f32[128,128]{1,0:T(8,12...) custom-call(f32[32,128]{1,0:T(8,128)S(1)} %get-tuple-element.115.ref, ...), custom_call_target="tpu_custom_call" | custom-call | flops 20000000 | bytes 1048576 | tf_op jit(solution)/shard_map/second/pallas_call | solution.py:533
  20.7 0.4 collective-permute-start.5
  21.1 0.4 collective-permute-start.6
  21.5 4.9 %collective-permute-start.7 = (f32[64,128]{1,0:T(8,128)S(1)}, f32[64,128]{1,0:T(8,128)S(1)}, u32[]{:S(2)}, u32[]{:S(2)}) collective-permute-start(f32[64,128]{1,0:T(8,128)S(1)} %get-tuple-element.146), channel_id=1, source_target_pairs={{0,2},{2,0},{4,6},{6,4},{8,10},{10,8},{12,14},{14,12},{16,18},{18,... | collective-permute-start | bytes 98312 | tf_op jit(solution)/shard_map/ppermute | solution.py:561
  26.4 2.5 %response.2 = (f32[34,144,128]{2,1,0:T(8,128)S(1)}, f32[1,128]{1,0:T(1,128)S(1)}) custom-call(f32[32,128]{1,0:T(8,128)S(1)} %get-tuple-element.151.refs_0_.refs_5_, f32[32,128]{1,0:T(8,128)S(1)} %get-tuple-element.152.refs_1_.refs_6_, f32[32,128]{1,0:T(8,128)S(1)} %get-tuple-element.153.refs_2_.refs_7_, f32[32,128]{1,0:T(8,128)S(1)} %get-tuple-element.154.refs_3_.refs_8_, ...), custom_call_target="tpu_custom_call" | custom-call | flops 30000000 | bytes 1048576 | tf_op jit(solution)/shard_map/response/pallas_call | solution.py:533
  29.0 1.1 %collective-permute-done.8.refs_9_ = f32[64,128]{1,0:T(8,128)S(1)} collective-permute-done((f32[64,128]{1,0:T(8,128)S(1)}, f32[64,128]{1,0:T(8,128)S(1)}, u32[]{:S(2)}, u32[]{:S(2)}) %collective-permute-start.8) | collective-permute-done | bytes 32800 | tf_op jit(solution)/shard_map/ppermute | solution.py:558
  30.0 1.5 %third.2 = (f32[32,128]{1,0:T(8,128)S(1)}, f32[32,128]{1,0:T(8,128)S(1)}, f32[128,128]{1,0:T(8,128)S(1)}, f32[32,128]{1,0:T(8,128)S(1)}, f32[32,128]{1,0:T(8,128...) custom-call(f32[64,128]{1,0:T(8,128)S(1)} %get-tuple-element.138.ref, ...), custom_call_target="tpu_custom_call" | custom-call | flops 20000000 | bytes 1048576 | tf_op jit(solution)/shard_map/third/pallas_call | solution.py:533
  31.6 17.3 %all_to_all.10 = f32[128,1,128]{2,1,0:T(1,128)S(1)} all-to-all(f32[128,1,128]{2,1,0:T(1,128)S(1)} %bitcast.15), channel_id=1, replica_groups=mesh['gx'=4,'gy'=16,'gz'=2] {'gx','gy','gz'}, dimensions={0} | all-to-all | bytes 131072 | tf_op jit(solution)/shard_map/all_to_all | solution.py:566
  48.9 4.3 %fourth.1 = (f32[32,128,128]{2,1,0:T(8,128)S(1)}, f32[34,144,128]{2,1,0:T(8,128)S(1)}, f32[32,128]{1,0:T(8,128)S(1)}, f32[32,128]{1,0:T(8,128)S(1)}, f32[128,128...) custom-call(f32[128,128]{1,0:T(8,128)S(1)} %bitcast.13, ...), custom_call_target="tpu_custom_call" | custom-call | flops 50000000 | bytes 1048576 | tf_op jit(solution)/shard_map/fourth/pallas_call | solution.py:533
  53.2 1.3 %collective-permute-start.14 = (f32[128,128]{1,0:T(8,128)S(1)}, f32[128,128]{1,0:T(8,128)S(1)}, u32[]{:S(2)}, u32[]{:S(2)}) collective-permute-start(f32[128,128]{1,0:T(8,128)S(1)} %get-tuple-element.183), channel_id=1, source_target_pairs={{0,1},{1,0},{2,3},{3,2},{4,5},{5,4},{6,7},{7,6},{8,9},{9,8},{10,11... | collective-permute-start | bytes 196616 | tf_op jit(solution)/shard_map/ppermute | solution.py:557
  54.5 0.4 collective-permute-start.10
  54.9 0.5 collective-permute-start.11
  55.3 1.3 %collective-permute-start.12 = (f32[32,128]{1,0:T(8,128)S(1)}, f32[32,128]{1,0:T(8,128)S(1)}, u32[]{:S(2)}, u32[]{:S(2)}) collective-permute-start(f32[32,128]{1,0:T(8,128)S(1)} %get-tuple-element.181), channel_id=1, source_target_pairs={{0,2},{2,0},{4,6},{6,4},{8,10},{10,8},{12,14},{14,12},{16,18},{18,... | collective-permute-start | bytes 49160 | tf_op jit(solution)/shard_map/ppermute | solution.py:561
  56.6 0.4 collective-permute-start.13
  57.1 3.2 %free.3 = (f32[34,144,128]{2,1,0:T(8,128)S(1)}, f32[32,128]{1,0:T(8,128)S(1)}, f32[32,128]{1,0:T(8,128)S(1)}, f32[32,128]{1,0:T(8,128)S(1)}, f32[32,128]{1,0:T(8...) custom-call(f32[34,144,128]{2,1,0:T(8,128)S(1)} %get-tuple-element.184.state, ...), custom_call_target="tpu_custom_call" | custom-call | flops 30000000 | bytes 1048576 | tf_op jit(solution)/shard_map/free/pallas_call | solution.py:533
  60.3 1.2 %second.3 = (f32[32,128]{1,0:T(8,128)S(1)}, f32[32,128]{1,0:T(8,128)S(1)}, f32[32,128]{1,0:T(8,128)S(1)}, f32[32,128]{1,0:T(8,128)S(1)}, f32[128,128]{1,0:T(8,12...) custom-call(f32[32,128]{1,0:T(8,128)S(1)} %get-tuple-element.173.ref, ...), custom_call_target="tpu_custom_call" | custom-call | flops 20000000 | bytes 1048576 | tf_op jit(solution)/shard_map/second/pallas_call | solution.py:533
  61.5 2.3 %collective-permute-start.19 = (f32[256,128]{1,0:T(8,128)S(1)}, f32[256,128]{1,0:T(8,128)S(1)}, u32[]{:S(2)}, u32[]{:S(2)}) collective-permute-start(f32[256,128]{1,0:T(8,128)S(1)} %get-tuple-element.202), channel_id=1, source_target_pairs={{0,1},{1,0},{2,3},{3,2},{4,5},{5,4},{6,7},{7,6},{8,9},{9,8},{10,11... | collective-permute-start | bytes 393224 | tf_op jit(solution)/shard_map/ppermute | solution.py:557
  63.8 0.4 collective-permute-start.15
  64.2 1.9 %collective-permute-start.16 = (f32[64,128]{1,0:T(8,128)S(1)}, f32[64,128]{1,0:T(8,128)S(1)}, u32[]{:S(2)}, u32[]{:S(2)}) collective-permute-start(f32[64,128]{1,0:T(8,128)S(1)} %get-tuple-element.199), channel_id=1, source_target_pairs={{32,64},{64,32},{96,0},{0,96},{33,65},{65,33},{97,1},{1,97},{34,66... | collective-permute-start | bytes 98312 | tf_op jit(solution)/shard_map/ppermute | solution.py:559
  66.1 2.6 %collective-permute-start.17 = (f32[64,128]{1,0:T(8,128)S(1)}, f32[64,128]{1,0:T(8,128)S(1)}, u32[]{:S(2)}, u32[]{:S(2)}) collective-permute-start(f32[64,128]{1,0:T(8,128)S(1)} %get-tuple-element.200), channel_id=1, source_target_pairs={{0,2},{2,0},{4,6},{6,4},{8,10},{10,8},{12,14},{14,12},{16,18},{18,... | collective-permute-start | bytes 98312 | tf_op jit(solution)/shard_map/ppermute | solution.py:561
  68.7 2.5 %response.3 = (f32[34,144,128]{2,1,0:T(8,128)S(1)}, f32[1,128]{1,0:T(1,128)S(1)}) custom-call(f32[32,128]{1,0:T(8,128)S(1)} %get-tuple-element.203.refs_0_, f32[32,128]{1,0:T(8,128)S(1)} %get-tuple-element.204.refs_1_.refs_6_, f32[32,128]{1,0:T(8,128)S(1)} %get-tuple-element.205.refs_2_, f32[32,128]{1,0:T(8,128)S(1)} %get-tuple-element.206.refs_3_.refs_7_, ...), custom_call_target="tpu_custom_call" | custom-call | flops 30000000 | bytes 1048576 | tf_op jit(solution)/shard_map/response/pallas_call | solution.py:533
  71.3 0.8 collective-permute-done.18.refs_9_
  72.0 1.5 %third.3 = (f32[32,128]{1,0:T(8,128)S(1)}, f32[32,128]{1,0:T(8,128)S(1)}, f32[128,128]{1,0:T(8,128)S(1)}, f32[32,128]{1,0:T(8,128)S(1)}, f32[32,128]{1,0:T(8,128...) custom-call(f32[64,128]{1,0:T(8,128)S(1)} %get-tuple-element.192.refs_0_, ...), custom_call_target="tpu_custom_call" | custom-call | flops 20000000 | bytes 1048576 | tf_op jit(solution)/shard_map/third/pallas_call | solution.py:533
  73.5 14.8 %all_to_all.11 = f32[128,1,128]{2,1,0:T(1,128)S(1)} all-to-all(f32[128,1,128]{2,1,0:T(1,128)S(1)} %bitcast.16), channel_id=1, replica_groups=mesh['gx'=4,'gy'=16,'gz'=2] {'gx','gy','gz'}, dimensions={0} | all-to-all | bytes 131072 | tf_op jit(solution)/shard_map/all_to_all | solution.py:566
  88.4 2.2 %last.1 = (f32[32,128,128]{2,1,0:T(8,128)}, f32[32,128]{1,0:T(8,128)}, f32[32,128]{1,0:T(8,128)}, f32[128,128]{1,0:T(8,128)}) custom-call(f32[128,128]{1,0:T(8,128)S(1)} %bitcast.14, f32[34,144,128]{2,1,0:T(8,128)S(1)} %get-tuple-element.211.refs_1_, f32[34,144,128]{2,1,0:T(8,128)S(1)} %get-tuple-element.212.refs_2_, ...), custom_call_target="tpu_custom_call" | custom-call | flops 20000000 | bytes 1048576 | tf_op jit(solution)/shard_map/last/pallas_call | solution.py:533
  (21 shorter events, 0.4 us)
Async XLA Ops:
  6.0 13.1 %collective-permute-start.4 = (f32[256,128]{1,0:T(8,128)S(1)}, f32[256,128]{1,0:T(8,128)S(1)}, u32[]{:S(2)}, u32[]{:S(2)}) collective-permute-start(f32[256,128]{1,0:T(8,128)S(1)} %get-tuple-element.125), channel_id=1, source_target_pairs={{0,1},{1,0},{2,3},{3,2},{4,5},{5,4},{6,7},{7,6},{8,9},{9,8},{10,11... | collective-permute-start | bytes 393224 | tf_op jit(solution)/shard_map/ppermute | solution.py:557
  9.6 9.4 %collective-permute-start = (f32[160,128]{1,0:T(8,128)S(1)}, f32[160,128]{1,0:T(8,128)S(1)}, u32[]{:S(2)}, u32[]{:S(2)}) collective-permute-start(f32[160,128]{1,0:T(8,128)S(1)} %get-tuple-element.121), channel_id=1, source_target_pairs={{0,32},{32,0},{64,96},{96,64},{1,33},{33,1},{65,97},{97,65},{2,34}... | collective-permute-start | bytes 245768 | tf_op jit(solution)/shard_map/ppermute | solution.py:560
  10.9 8.1 %collective-permute-start.1 = (f32[160,128]{1,0:T(8,128)S(1)}, f32[160,128]{1,0:T(8,128)S(1)}, u32[]{:S(2)}, u32[]{:S(2)}) collective-permute-start(f32[160,128]{1,0:T(8,128)S(1)} %get-tuple-element.122), channel_id=1, source_target_pairs={{32,64},{64,32},{96,0},{0,96},{33,65},{65,33},{97,1},{1,97},{34,66... | collective-permute-start | bytes 245768 | tf_op jit(solution)/shard_map/ppermute | solution.py:559
  12.8 6.2 %collective-permute-start.2 = (f32[160,128]{1,0:T(8,128)S(1)}, f32[160,128]{1,0:T(8,128)S(1)}, u32[]{:S(2)}, u32[]{:S(2)}) collective-permute-start(f32[160,128]{1,0:T(8,128)S(1)} %get-tuple-element.123), channel_id=1, source_target_pairs={{0,2},{2,0},{4,6},{6,4},{8,10},{10,8},{12,14},{14,12},{16,18},{18,... | collective-permute-start | bytes 245768 | tf_op jit(solution)/shard_map/ppermute | solution.py:561
  14.4 4.7 %collective-permute-start.3 = (f32[160,128]{1,0:T(8,128)S(1)}, f32[160,128]{1,0:T(8,128)S(1)}, u32[]{:S(2)}, u32[]{:S(2)}) collective-permute-start(f32[160,128]{1,0:T(8,128)S(1)} %get-tuple-element.124), channel_id=1, source_target_pairs={{2,4},{4,2},{6,8},{8,6},{10,12},{12,10},{14,16},{16,14},{18,20},{2... | collective-permute-start | bytes 245768 | tf_op jit(solution)/shard_map/ppermute | solution.py:558
  20.4 9.7 %collective-permute-start.9 = (f32[256,128]{1,0:T(8,128)S(1)}, f32[256,128]{1,0:T(8,128)S(1)}, u32[]{:S(2)}, u32[]{:S(2)}) collective-permute-start(f32[256,128]{1,0:T(8,128)S(1)} %get-tuple-element.148), channel_id=1, source_target_pairs={{0,1},{1,0},{2,3},{3,2},{4,5},{5,4},{6,7},{7,6},{8,9},{9,8},{10,11... | collective-permute-start | bytes 393224 | tf_op jit(solution)/shard_map/ppermute | solution.py:557
  20.7 8.3 %collective-permute-start.5 = (f32[64,128]{1,0:T(8,128)S(1)}, f32[64,128]{1,0:T(8,128)S(1)}, u32[]{:S(2)}, u32[]{:S(2)}) collective-permute-start(f32[64,128]{1,0:T(8,128)S(1)} %get-tuple-element.144), channel_id=1, source_target_pairs={{0,32},{32,0},{64,96},{96,64},{1,33},{33,1},{65,97},{97,65},{2,34}... | collective-permute-start | bytes 98312 | tf_op jit(solution)/shard_map/ppermute | solution.py:560
  21.1 7.9 %collective-permute-start.6 = (f32[64,128]{1,0:T(8,128)S(1)}, f32[64,128]{1,0:T(8,128)S(1)}, u32[]{:S(2)}, u32[]{:S(2)}) collective-permute-start(f32[64,128]{1,0:T(8,128)S(1)} %get-tuple-element.145), channel_id=1, source_target_pairs={{32,64},{64,32},{96,0},{0,96},{33,65},{65,33},{97,1},{1,97},{34,66... | collective-permute-start | bytes 98312 | tf_op jit(solution)/shard_map/ppermute | solution.py:559
  21.5 7.5 %collective-permute-start.7 = (f32[64,128]{1,0:T(8,128)S(1)}, f32[64,128]{1,0:T(8,128)S(1)}, u32[]{:S(2)}, u32[]{:S(2)}) collective-permute-start(f32[64,128]{1,0:T(8,128)S(1)} %get-tuple-element.146), channel_id=1, source_target_pairs={{0,2},{2,0},{4,6},{6,4},{8,10},{10,8},{12,14},{14,12},{16,18},{18,... | collective-permute-start | bytes 98312 | tf_op jit(solution)/shard_map/ppermute | solution.py:561
  26.4 3.6 %collective-permute-start.8 = (f32[64,128]{1,0:T(8,128)S(1)}, f32[64,128]{1,0:T(8,128)S(1)}, u32[]{:S(2)}, u32[]{:S(2)}) collective-permute-start(f32[64,128]{1,0:T(8,128)S(1)} %get-tuple-element.147), channel_id=1, source_target_pairs={{2,4},{4,2},{6,8},{8,6},{10,12},{12,10},{14,16},{16,14},{18,20},{2... | collective-permute-start | bytes 98312 | tf_op jit(solution)/shard_map/ppermute | solution.py:558
  53.2 7.1 %collective-permute-start.14 = (f32[128,128]{1,0:T(8,128)S(1)}, f32[128,128]{1,0:T(8,128)S(1)}, u32[]{:S(2)}, u32[]{:S(2)}) collective-permute-start(f32[128,128]{1,0:T(8,128)S(1)} %get-tuple-element.183), channel_id=1, source_target_pairs={{0,1},{1,0},{2,3},{3,2},{4,5},{5,4},{6,7},{7,6},{8,9},{9,8},{10,11... | collective-permute-start | bytes 196616 | tf_op jit(solution)/shard_map/ppermute | solution.py:557
  54.5 5.8 %collective-permute-start.10 = (f32[32,128]{1,0:T(8,128)S(1)}, f32[32,128]{1,0:T(8,128)S(1)}, u32[]{:S(2)}, u32[]{:S(2)}) collective-permute-start(f32[32,128]{1,0:T(8,128)S(1)} %get-tuple-element.179), channel_id=1, source_target_pairs={{0,32},{32,0},{64,96},{96,64},{1,33},{33,1},{65,97},{97,65},{2,34}... | collective-permute-start | bytes 49160 | tf_op jit(solution)/shard_map/ppermute | solution.py:560
  54.9 5.4 %collective-permute-start.11 = (f32[32,128]{1,0:T(8,128)S(1)}, f32[32,128]{1,0:T(8,128)S(1)}, u32[]{:S(2)}, u32[]{:S(2)}) collective-permute-start(f32[32,128]{1,0:T(8,128)S(1)} %get-tuple-element.180), channel_id=1, source_target_pairs={{32,64},{64,32},{96,0},{0,96},{33,65},{65,33},{97,1},{1,97},{34,66... | collective-permute-start | bytes 49160 | tf_op jit(solution)/shard_map/ppermute | solution.py:559
  55.3 5.0 %collective-permute-start.12 = (f32[32,128]{1,0:T(8,128)S(1)}, f32[32,128]{1,0:T(8,128)S(1)}, u32[]{:S(2)}, u32[]{:S(2)}) collective-permute-start(f32[32,128]{1,0:T(8,128)S(1)} %get-tuple-element.181), channel_id=1, source_target_pairs={{0,2},{2,0},{4,6},{6,4},{8,10},{10,8},{12,14},{14,12},{16,18},{18,... | collective-permute-start | bytes 49160 | tf_op jit(solution)/shard_map/ppermute | solution.py:561
  56.6 3.7 %collective-permute-start.13 = (f32[32,128]{1,0:T(8,128)S(1)}, f32[32,128]{1,0:T(8,128)S(1)}, u32[]{:S(2)}, u32[]{:S(2)}) collective-permute-start(f32[32,128]{1,0:T(8,128)S(1)} %get-tuple-element.182), channel_id=1, source_target_pairs={{2,4},{4,2},{6,8},{8,6},{10,12},{12,10},{14,16},{16,14},{18,20},{2... | collective-permute-start | bytes 49160 | tf_op jit(solution)/shard_map/ppermute | solution.py:558
  61.5 10.5 %collective-permute-start.19 = (f32[256,128]{1,0:T(8,128)S(1)}, f32[256,128]{1,0:T(8,128)S(1)}, u32[]{:S(2)}, u32[]{:S(2)}) collective-permute-start(f32[256,128]{1,0:T(8,128)S(1)} %get-tuple-element.202), channel_id=1, source_target_pairs={{0,1},{1,0},{2,3},{3,2},{4,5},{5,4},{6,7},{7,6},{8,9},{9,8},{10,11... | collective-permute-start | bytes 393224 | tf_op jit(solution)/shard_map/ppermute | solution.py:557
  63.8 7.4 %collective-permute-start.15 = (f32[64,128]{1,0:T(8,128)S(1)}, f32[64,128]{1,0:T(8,128)S(1)}, u32[]{:S(2)}, u32[]{:S(2)}) collective-permute-start(f32[64,128]{1,0:T(8,128)S(1)} %get-tuple-element.198), channel_id=1, source_target_pairs={{0,32},{32,0},{64,96},{96,64},{1,33},{33,1},{65,97},{97,65},{2,34}... | collective-permute-start | bytes 98312 | tf_op jit(solution)/shard_map/ppermute | solution.py:560
  64.2 7.0 %collective-permute-start.16 = (f32[64,128]{1,0:T(8,128)S(1)}, f32[64,128]{1,0:T(8,128)S(1)}, u32[]{:S(2)}, u32[]{:S(2)}) collective-permute-start(f32[64,128]{1,0:T(8,128)S(1)} %get-tuple-element.199), channel_id=1, source_target_pairs={{32,64},{64,32},{96,0},{0,96},{33,65},{65,33},{97,1},{1,97},{34,66... | collective-permute-start | bytes 98312 | tf_op jit(solution)/shard_map/ppermute | solution.py:559
  66.1 5.2 %collective-permute-start.17 = (f32[64,128]{1,0:T(8,128)S(1)}, f32[64,128]{1,0:T(8,128)S(1)}, u32[]{:S(2)}, u32[]{:S(2)}) collective-permute-start(f32[64,128]{1,0:T(8,128)S(1)} %get-tuple-element.200), channel_id=1, source_target_pairs={{0,2},{2,0},{4,6},{6,4},{8,10},{10,8},{12,14},{14,12},{16,18},{18,... | collective-permute-start | bytes 98312 | tf_op jit(solution)/shard_map/ppermute | solution.py:561
  68.7 3.3 %collective-permute-start.18 = (f32[64,128]{1,0:T(8,128)S(1)}, f32[64,128]{1,0:T(8,128)S(1)}, u32[]{:S(2)}, u32[]{:S(2)}) collective-permute-start(f32[64,128]{1,0:T(8,128)S(1)} %get-tuple-element.201), channel_id=1, source_target_pairs={{2,4},{4,2},{6,8},{8,6},{10,12},{12,10},{14,16},{16,14},{18,20},{2... | collective-permute-start | bytes 98312 | tf_op jit(solution)/shard_map/ppermute | solution.py:558
